TPU v7x, 32 devices: a whole 2x2x4 slice. The times are simulated.
32 devices in a mesh: dp: 8 (over z, x), tensor: 4 (over y, core).
Axes of the slice: x: 2, y: 2, z: 4, core: 2. Of those that a mesh axis runs over, the one named last changes fastest.
Arguments:
- tokens: float32 [160, 197, 768], P('dp'), may hold values from -6 to 6
- cotangent: float32 [160, 197, 768], P('dp'), may hold values from -6 to 6
- counts: int32 [8], P('dp'), may hold values from 1 to 20, 96 in all
- qkv_weight: float32 [768, 3, 768], P('dp', None, 'tensor'), may hold values from -1.6237976 to 1.6237976
- proj_weight: float32 [768, 768], P('tensor', 'dp'), may hold values from -0.75 to 0.75
- expand_weight: float32 [768, 3072], P('dp', 'tensor'), may hold values from -0.21875 to 0.21875
- reduce_weight: float32 [3072, 768], P('tensor', 'dp'), may hold values from -0.109375 to 0.109375
- qv_bias: float32 [2, 768], P(None, ('tensor', 'dp')), may hold values from -3 to 3
- expand_bias: float32 [3072], P(('tensor', 'dp')), may hold values from -3 to 3
- vectors: float32 [6, 768], P(None, 'dp'), may hold values from -1.25 to 2.5
- first_qkv_weight: float32 [768, 3, 768], P('dp', None, 'tensor'), may hold values from -24 to 24
- second_qkv_weight: float32 [768, 3, 768], P('dp', None, 'tensor'), may hold values from 3.7824 to 75.648
- first_proj_weight: float32 [768, 768], P('tensor', 'dp'), may hold values from -24 to 24
- second_proj_weight: float32 [768, 768], P('tensor', 'dp'), may hold values from 3.7824 to 75.648
- first_expand_weight: float32 [768, 3072], P('dp', 'tensor'), may hold values from -24 to 24
- second_expand_weight: float32 [768, 3072], P('dp', 'tensor'), may hold values from 3.7824 to 75.648
- first_reduce_weight: float32 [3072, 768], P('tensor', 'dp'), may hold values from -24 to 24
- second_reduce_weight: float32 [3072, 768], P('tensor', 'dp'), may hold values from 3.7824 to 75.648
- first_qv_bias: float32 [2, 768], P(None, ('tensor', 'dp')), may hold values from -24 to 24
- second_qv_bias: float32 [2, 768], P(None, ('tensor', 'dp')), may hold values from 3.7824 to 75.648
- first_expand_bias: float32 [3072], P(('tensor', 'dp')), may hold values from -24 to 24
- second_expand_bias: float32 [3072], P(('tensor', 'dp')), may hold values from 3.7824 to 75.648
- first_vectors: float32 [6, 768], P(None, 'dp'), may hold values from -24 to 24
- second_vectors: float32 [6, 768], P(None, 'dp'), may hold values from 3.7824 to 75.648
Outputs:
- output: float32 [160, 197, 768], P('dp', None, 'tensor')
- grad_tokens: float32 [160, 197, 768], P('dp', None, 'tensor')
- grad_qkv_weight: float32 [768, 3, 768], P('dp', None, 'tensor')
- new_qkv_weight: float32 [768, 3, 768], P('dp', None, 'tensor')
- new_first_qkv_weight: float32 [768, 3, 768], P('dp', None, 'tensor')
- new_second_qkv_weight: float32 [768, 3, 768], P('dp', None, 'tensor')
- grad_proj_weight: float32 [768, 768], P('tensor', 'dp')
- new_proj_weight: float32 [768, 768], P('tensor', 'dp')
- new_first_proj_weight: float32 [768, 768], P('tensor', 'dp')
- new_second_proj_weight: float32 [768, 768], P('tensor', 'dp')
- grad_expand_weight: float32 [768, 3072], P('dp', 'tensor')
- new_expand_weight: float32 [768, 3072], P('dp', 'tensor')
- new_first_expand_weight: float32 [768, 3072], P('dp', 'tensor')
- new_second_expand_weight: float32 [768, 3072], P('dp', 'tensor')
- grad_reduce_weight: float32 [3072, 768], P('tensor', 'dp')
- new_reduce_weight: float32 [3072, 768], P('tensor', 'dp')
- new_first_reduce_weight: float32 [3072, 768], P('tensor', 'dp')
- new_second_reduce_weight: float32 [3072, 768], P('tensor', 'dp')
- grad_qv_bias: float32 [2, 768], P(None, ('tensor', 'dp'))
- new_qv_bias: float32 [2, 768], P(None, ('tensor', 'dp'))
- new_first_qv_bias: float32 [2, 768], P(None, ('tensor', 'dp'))
- new_second_qv_bias: float32 [2, 768], P(None, ('tensor', 'dp'))
- grad_expand_bias: float32 [3072], P(('tensor', 'dp'))
- new_expand_bias: float32 [3072], P(('tensor', 'dp'))
- new_first_expand_bias: float32 [3072], P(('tensor', 'dp'))
- new_second_expand_bias: float32 [3072], P(('tensor', 'dp'))
- grad_vectors: float32 [6, 768], P(None, 'dp')
- new_vectors: float32 [6, 768], P(None, 'dp')
- new_first_vectors: float32 [6, 768], P(None, 'dp')
- new_second_vectors: float32 [6, 768], P(None, 'dp')
Inputs may be any that keep to these rules, and one draw needn't show every extreme that they name: counts[i] of the 20 slots of data group i hold live images, the first ones; the counts sum to 96 and the largest is 20.
All inputs are finite; a program needn't handle non-finite values.
Results may differ from a plain program's by a relative error of at most 0.025.
The roundings to bfloat16 on the way count: a program that leaves them out, or rounds other values in their place, can miss the bound.
Values may be sent and summed in bfloat16 or wider, within the bound.
A program may use at most 320 MiB of HBM per device.

v0:
```python
import jax
import jax.numpy as jnp
from jax import lax
from jax.sharding import PartitionSpec as P

HEAD_DIM = 64


lr_matrix = 0.006
lr_vector = 0.1
decay = 0.05
beta_one = 0.9
beta_two = 0.999
adam_eps = 1e-08
adam_step = 2.0
norm_eps = 1e-06


def layer_norm(rows, gain, shift):
    mean = jnp.mean(rows, axis=-1, keepdims=True)
    centred = rows - mean
    variance = jnp.mean(centred * centred, axis=-1, keepdims=True)
    scale = lax.rsqrt(variance + norm_eps)
    normed = centred * scale
    return (normed * gain + shift, normed, scale)


def norm_back(grad_in, normed, scale, gain):
    scaled = grad_in * gain
    return scale * (
        scaled
        - jnp.mean(scaled, axis=-1, keepdims=True)
        - normed * jnp.mean(scaled * normed, axis=-1, keepdims=True)
    )


def gelu_exact(value):
    return jax.nn.gelu(value, approximate=False)


def inner_rows(left, right):
    return lax.dot_general(
        left, right, (((0,), (0,)), ((), ())), preferred_element_type=jnp.float32
    )


def times_transposed(left, right):
    return lax.dot_general(
        left, right, (((1,), (1,)), ((), ())), preferred_element_type=jnp.float32
    )


def adamw(master, grad, first, second, rate, decay_rate):
    first_new = beta_one * first + (1.0 - beta_one) * grad
    second_new = beta_two * second + (1.0 - beta_two) * grad * grad
    first_hat = first_new / (1.0 - beta_one**adam_step)
    second_hat = second_new / (1.0 - beta_two**adam_step)
    new = master - rate * (first_hat / (jnp.sqrt(second_hat) + adam_eps) + decay_rate * master)
    return (new, first_new, second_new)


def on_device(
    tokens,
    cotangent,
    counts,
    qkv_weight,
    proj_weight,
    expand_weight,
    reduce_weight,
    qv_bias,
    expand_bias,
    vectors,
    first_qkv_weight,
    second_qkv_weight,
    first_proj_weight,
    second_proj_weight,
    first_expand_weight,
    second_expand_weight,
    first_reduce_weight,
    second_reduce_weight,
    first_qv_bias,
    second_qv_bias,
    first_expand_bias,
    second_expand_bias,
    first_vectors,
    second_vectors,
):
    f32 = jnp.float32
    bf16 = jnp.bfloat16
    w_qkv, w_proj, w_expand, w_reduce, b_qv, b_expand, vec_half = (
        lax.all_gather(qkv_weight.astype(bf16), "dp", axis=0, tiled=True),
        lax.all_gather(proj_weight.astype(bf16), "dp", axis=1, tiled=True),
        lax.all_gather(expand_weight.astype(bf16), "dp", axis=0, tiled=True),
        lax.all_gather(reduce_weight.astype(bf16), "dp", axis=1, tiled=True),
        lax.all_gather(qv_bias.astype(bf16), "dp", axis=1, tiled=True),
        lax.all_gather(expand_bias.astype(bf16), "dp", axis=0, tiled=True),
        lax.all_gather(vectors.astype(bf16), "dp", axis=1, tiled=True),
    )
    vec = vec_half.astype(f32)
    slots = tokens.shape[0]
    seq = tokens.shape[1]
    width = tokens.shape[2]
    rows = slots * seq
    local = w_qkv.shape[2]
    heads_local = local // HEAD_DIM
    scale_qk = HEAD_DIM ** (-0.5)
    col_count = width // lax.axis_size("tensor")
    col_start = lax.axis_index("tensor") * col_count
    live = (jnp.arange(slots) < counts[0]).astype(f32)
    live_rows = jnp.broadcast_to(live[:, None], (slots, seq)).reshape(rows, 1)
    flat = tokens.reshape(rows, width)
    a1, normed1, scale1 = layer_norm(flat, vec[0], vec[1])
    a1_half = a1.astype(bf16)
    qkv_flat = w_qkv.reshape(width, 3 * local)
    qkv = jnp.dot(a1_half, qkv_flat, preferred_element_type=f32).reshape(rows, 3, local)
    bias_f = b_qv.astype(f32)
    qkv = qkv + jnp.stack([bias_f[0], jnp.zeros((local,), f32), bias_f[1]])
    qkv_half = qkv.astype(bf16).reshape(slots, seq, 3, heads_local, HEAD_DIM)
    query = qkv_half[:, :, 0]
    key = qkv_half[:, :, 1]
    value = qkv_half[:, :, 2]
    scores = jnp.einsum("sqhc,skhc->shqk", query, key, preferred_element_type=f32) * scale_qk
    top = jnp.max(scores, axis=-1, keepdims=True)
    lse = top + jnp.log(jnp.sum(jnp.exp(scores - top), axis=-1, keepdims=True))
    probs_half = jnp.exp(scores - lse).astype(bf16)
    mixed = (
        jnp.einsum("shqk,skhc->sqhc", probs_half, value, preferred_element_type=f32)
        .astype(bf16)
        .reshape(rows, local)
    )
    attention = lax.psum(
        jnp.dot(mixed, w_proj, preferred_element_type=f32).astype(jnp.bfloat16), "tensor"
    ).astype(jnp.float32)
    resid = flat + attention + vec[2]
    a2, normed2, scale2 = layer_norm(resid, vec[3], vec[4])
    a2_half = a2.astype(bf16)
    pre = jnp.dot(a2_half, w_expand, preferred_element_type=f32) + b_expand.astype(f32)
    hidden = gelu_exact(pre).astype(bf16)
    mlp_part = jnp.dot(hidden, w_reduce, preferred_element_type=f32)
    mlp_whole_sum = lax.psum(mlp_part.astype(jnp.bfloat16), "tensor").astype(jnp.float32)
    mlp_own = lax.dynamic_slice_in_dim(mlp_whole_sum, col_start, col_count, 1)
    resid_own = lax.dynamic_slice_in_dim(resid, col_start, col_count, 1)
    bias_own = lax.dynamic_slice_in_dim(vec[5], col_start, col_count, 0)
    output = ((resid_own + mlp_own + bias_own) * live_rows).reshape(slots, seq, col_count)
    grad_out = cotangent.reshape(rows, width) * live_rows
    grad_half = grad_out.astype(bf16)
    d_reduce = inner_rows(hidden, grad_half)
    d_hidden = times_transposed(grad_half, w_reduce)
    unused, gelu_back = jax.vjp(gelu_exact, pre)
    d_pre = gelu_back(d_hidden)[0]
    d_expand_bias = jnp.sum(d_pre, axis=0)
    d_pre_half = d_pre.astype(bf16)
    d_expand = inner_rows(a2_half, d_pre_half)
    d_a2 = lax.psum(times_transposed(d_pre_half, w_expand).astype(jnp.bfloat16), "tensor").astype(
        jnp.float32
    )
    d_resid = grad_out + norm_back(d_a2, normed2, scale2, vec[3])
    d_resid_half = d_resid.astype(bf16)
    d_proj = inner_rows(mixed, d_resid_half)
    d_mixed = (
        times_transposed(d_resid_half, w_proj)
        .astype(bf16)
        .reshape(slots, seq, heads_local, HEAD_DIM)
    )
    again = jnp.einsum("sqhc,skhc->shqk", query, key, preferred_element_type=f32) * scale_qk
    probs_f = jnp.exp(again - lse)
    probs_again = probs_f.astype(bf16)
    d_value = jnp.einsum("shqk,sqhc->skhc", probs_again, d_mixed, preferred_element_type=f32)
    d_probs = jnp.einsum("sqhc,skhc->shqk", d_mixed, value, preferred_element_type=f32)
    delta = jnp.sum(probs_f * d_probs, axis=-1, keepdims=True)
    d_scores = (probs_f * (d_probs - delta) * scale_qk).astype(bf16)
    d_query = jnp.einsum("shqk,skhc->sqhc", d_scores, key, preferred_element_type=f32)
    d_key = jnp.einsum("shqk,sqhc->skhc", d_scores, query, preferred_element_type=f32)
    d_qv_bias = jnp.stack(
        [
            jnp.sum(d_query.reshape(rows, local), axis=0),
            jnp.sum(d_value.reshape(rows, local), axis=0),
        ]
    )
    d_qkv_half = jnp.stack([d_query, d_key, d_value], axis=2).astype(bf16).reshape(rows, 3 * local)
    d_qkv = inner_rows(a1_half, d_qkv_half).reshape(width, 3, local)
    d_a1 = lax.psum(times_transposed(d_qkv_half, qkv_flat).astype(jnp.bfloat16), "tensor").astype(
        jnp.float32
    )
    d_flat = d_resid + norm_back(d_a1, normed1, scale1, vec[0])
    grad_tokens = lax.dynamic_slice_in_dim(d_flat, col_start, col_count, 1).reshape(
        slots, seq, col_count
    )
    d_vectors = jnp.stack(
        [
            jnp.sum(d_a1 * normed1, axis=0),
            jnp.sum(d_a1, axis=0),
            jnp.sum(d_resid, axis=0),
            jnp.sum(d_a2 * normed2, axis=0),
            jnp.sum(d_a2, axis=0),
            jnp.sum(grad_out, axis=0),
        ]
    )
    g_qkv, g_proj, g_expand, g_reduce, g_qvb, g_expb, g_vec = (
        lax.psum_scatter(d_qkv.astype(jnp.bfloat16), "dp", scatter_dimension=0, tiled=True).astype(
            jnp.float32
        ),
        lax.psum_scatter(d_proj.astype(jnp.bfloat16), "dp", scatter_dimension=1, tiled=True).astype(
            jnp.float32
        ),
        lax.psum_scatter(
            d_expand.astype(jnp.bfloat16), "dp", scatter_dimension=0, tiled=True
        ).astype(jnp.float32),
        lax.psum_scatter(
            d_reduce.astype(jnp.bfloat16), "dp", scatter_dimension=1, tiled=True
        ).astype(jnp.float32),
        lax.psum_scatter(
            d_qv_bias.astype(jnp.bfloat16), "dp", scatter_dimension=1, tiled=True
        ).astype(jnp.float32),
        lax.psum_scatter(
            d_expand_bias.astype(jnp.bfloat16), "dp", scatter_dimension=0, tiled=True
        ).astype(jnp.float32),
        lax.psum_scatter(
            d_vectors.astype(jnp.bfloat16), "dp", scatter_dimension=1, tiled=True
        ).astype(jnp.float32),
    )
    n_qkv, f_qkv, s_qkv = adamw(
        qkv_weight, g_qkv, first_qkv_weight, second_qkv_weight, lr_matrix, decay
    )
    n_proj, f_proj, s_proj = adamw(
        proj_weight, g_proj, first_proj_weight, second_proj_weight, lr_matrix, decay
    )
    n_expand, f_expand, s_expand = adamw(
        expand_weight, g_expand, first_expand_weight, second_expand_weight, lr_matrix, decay
    )
    n_reduce, f_reduce, s_reduce = adamw(
        reduce_weight, g_reduce, first_reduce_weight, second_reduce_weight, lr_matrix, decay
    )
    n_qvb, f_qvb, s_qvb = adamw(qv_bias, g_qvb, first_qv_bias, second_qv_bias, lr_vector, 0.0)
    n_expb, f_expb, s_expb = adamw(
        expand_bias, g_expb, first_expand_bias, second_expand_bias, lr_vector, 0.0
    )
    n_vec, f_vec, s_vec = adamw(vectors, g_vec, first_vectors, second_vectors, lr_vector, 0.0)
    return (
        output,
        grad_tokens,
        g_qkv,
        n_qkv,
        f_qkv,
        s_qkv,
        g_proj,
        n_proj,
        f_proj,
        s_proj,
        g_expand,
        n_expand,
        f_expand,
        s_expand,
        g_reduce,
        n_reduce,
        f_reduce,
        s_reduce,
        g_qvb,
        n_qvb,
        f_qvb,
        s_qvb,
        g_expb,
        n_expb,
        f_expb,
        s_expb,
        g_vec,
        n_vec,
        f_vec,
        s_vec,
    )


def solution(mesh):
    return jax.shard_map(
        on_device,
        mesh=mesh,
        in_specs=(
            P("dp", None, None),
            P("dp", None, None),
            P("dp"),
            P("dp", None, "tensor"),
            P("tensor", "dp"),
            P("dp", "tensor"),
            P("tensor", "dp"),
            P(None, ("tensor", "dp")),
            P(("tensor", "dp")),
            P(None, "dp"),
            P("dp", None, "tensor"),
            P("dp", None, "tensor"),
            P("tensor", "dp"),
            P("tensor", "dp"),
            P("dp", "tensor"),
            P("dp", "tensor"),
            P("tensor", "dp"),
            P("tensor", "dp"),
            P(None, ("tensor", "dp")),
            P(None, ("tensor", "dp")),
            P(("tensor", "dp")),
            P(("tensor", "dp")),
            P(None, "dp"),
            P(None, "dp"),
        ),
        out_specs=(
            P("dp", None, "tensor"),
            P("dp", None, "tensor"),
            P("dp", None, "tensor"),
            P("dp", None, "tensor"),
            P("dp", None, "tensor"),
            P("dp", None, "tensor"),
            P("tensor", "dp"),
            P("tensor", "dp"),
            P("tensor", "dp"),
            P("tensor", "dp"),
            P("dp", "tensor"),
            P("dp", "tensor"),
            P("dp", "tensor"),
            P("dp", "tensor"),
            P("tensor", "dp"),
            P("tensor", "dp"),
            P("tensor", "dp"),
            P("tensor", "dp"),
            P(None, ("tensor", "dp")),
            P(None, ("tensor", "dp")),
            P(None, ("tensor", "dp")),
            P(None, ("tensor", "dp")),
            P(("tensor", "dp")),
            P(("tensor", "dp")),
            P(("tensor", "dp")),
            P(("tensor", "dp")),
            P(None, "dp"),
            P(None, "dp"),
            P(None, "dp"),
            P(None, "dp"),
        ),
        check_vma=False,
    )
```

profile of v0, /device:TPU:0, one launch (start us, length us, event | category | flops | bytes accessed | tf_op | source)
XLA Modules:
  0.0 1077.0 jit_solution(497541703004520291)
XLA Ops:
  9.5 22.3 %all-gather.1 = bf16[8,24,2]{1,2,0:T(2,128)(2,1)S(1)} all-gather(bf16[1,24,2]{1,2,0:T(2,128)(2,1)S(1)} %convert_bitcast_fusion.2), channel_id=1, replica_groups=mesh['dp'=8,'tensor'=4] {'dp'}, dimensions={0}, use_global_device_ids=true | all-gather | bytes 864 | tf_op jit(solution)/shard_map/all_gather | solution.py:95
  31.8 26.1 %all-gather = bf16[8,96,6]{1,2,0:T(8,128)(2,1)S(1)} all-gather(bf16[1,96,6]{1,2,0:T(8,128)(2,1)S(1)} %convert_bitcast_fusion.1), channel_id=1, replica_groups=mesh['dp'=8,'tensor'=4] {'dp'}, dimensions={0}, use_global_device_ids=true | all-gather | bytes 10368 | tf_op jit(solution)/shard_map/all_gather | solution.py:97
  70.2 31.7 %all_gather.24 = bf16[192,768]{0,1:T(8,128)(2,1)S(1)} all-gather(bf16[192,96]{0,1:T(8,128)(2,1)S(1)} %copy.114), channel_id=1, replica_groups=mesh['dp'=8,'tensor'=4] {'dp'}, dimensions={1}, use_global_device_ids=true | all-gather | bytes 331776 | tf_op jit(solution)/shard_map/all_gather | solution.py:92
  101.9 37.0 %all_gather.22 = bf16[768,3,192]{2,1,0:T(4,128)(2,1)S(1)} all-gather(bf16[96,3,192]{2,1,0:T(4,128)(2,1)S(1)} %copy.106), channel_id=1, replica_groups=mesh['dp'=8,'tensor'=4] {'dp'}, dimensions={0}, use_global_device_ids=true | all-gather | bytes 995328 | tf_op jit(solution)/shard_map/all_gather | solution.py:91
  162.5 13.3 %reshape.234 = bf16[20,197,3,3,64]{1,0,4,3,2:T(8,128)(2,1)} reshape(bf16[3940,3,192]{0,2,1:T(8,128)(2,1)} %add_convert_fusion.2) | data formatting | bytes 9077760 | tf_op jit(solution)/shard_map/reshape | solution.py:118
  200.7 14.3 %reshape.232 = f32[3940,768]{1,0:T(8,128)} reshape(f32[20,197,768]{2,1,0:T(8,128)} %param.24) | data formatting | bytes 24207360 | tf_op jit(solution)/shard_map/reshape | solution.py:111
  217.3 18.3 %all-reduce = bf16[768]{0:T(1024)(128)(2,1)S(1)} all-reduce(bf16[768]{0:T(1024)(128)(2,1)S(1)} %dynamic-update-slice), channel_id=1, replica_groups=mesh['dp'=8,'tensor'=4] {'dp'}, use_global_device_ids=true, to_apply=%add | all-reduce | flops 768 | bytes 3072
  235.8 14.0 %reshape.237 = f32[3940,768]{1,0:T(8,128)} reshape(f32[20,197,768]{2,1,0:T(8,128)} %param.25) | data formatting | bytes 24207360 | tf_op jit(solution)/shard_map/reshape | solution.py:145
  249.7 63.4 %all-reduce.9.cloned.1.call-done = bf16[3940,768]{1,0:T(8,128)(2,1)} async-done(((bf16[3940,768]{1,0:T(8,128)(2,1)}), bf16[3940,768]{1,0:T(8,128)(2,1)}) %all-reduce.9.cloned.1.call-update) | async-done | bytes 6051856 | tf_op jit(solution)/shard_map/psum | solution.py:131
  313.1 12.2 %fusion.86 = (f32[3940]{0:T(1024)S(1)}, f32[3940,768]{1,0:T(8,128)}) fusion(f32[768]{0:T(1024)S(1)} %get-tuple-element.158, f32[3940,768]{1,0:T(8,128)} %reshape.232, bf16[3940,768]{1,0:T(8,128)(2,1)} %all-reduce.9.cloned.1.call-done), kind=kLoop, calls=%fused_computation.151 | loop fusion | flops 12099740 | bytes 30278032 | tf_op jit(solution)/shard_map/reduce_sum | solution.py:20
  331.2 33.8 %multiply_convert_fusion.1 = (bf16[3940,768]{1,0:T(8,128)(2,1)S(1)}, f32[3940,768]{1,0:T(8,128)}, f32[3940,768]{1,0:T(8,128)}) fusion(f32[768]{0:T(1024)S(1)} %convert_element_type.171, bf16[768,768]{1,0:T(8,128)(2,1)} %all-gather.5.cloned.1.call-done, f32[3940,768]{1,0:T(8,128)} %get-tuple-element.199, f32[768]{0:T(1024)S(1)} %get-tuple-element.157, ...), kind=kOutput, calls=%fused_computation.27 | convolution fusion | flops 4862653440 | bytes 43583264 | tf_op jit(solution)/shard_map/dot_general | solution.py:137
  367.7 10.7 convolution_convert_fusion.5
  378.4 65.0 %reduce-scatter.15.cloned.1.call-done = bf16[768,96]{0,1:T(8,128)(2,1)} async-done(((bf16[768,768]{0,1:T(8,128)(2,1)}), bf16[768,96]{0,1:T(8,128)(2,1)}) %reduce-scatter.15.cloned.1.call-update) | async-done | bytes 147472 | tf_op jit(solution)/shard_map/reduce_scatter | solution.py:209
  445.5 41.0 %all-gather.7.cloned.1.call-done = bf16[768,768]{0,1:T(8,128)(2,1)} async-done(((bf16[768,96]{0,1:T(8,128)(2,1)}), bf16[768,768]{0,1:T(8,128)(2,1)}) %all-gather.7.cloned.1.call-update) | async-done | bytes 1179664 | tf_op jit(solution)/shard_map/all_gather | solution.py:94
  486.5 18.5 %fusion.92 = (bf16[768]{0:T(1024)(128)(2,1)S(1)}, bf16[3940,768]{1,0:T(8,128)(2,1)}) fusion(f32[3940,768]{1,0:T(8,128)} %get-tuple-element.197, bf16[768,768]{0,1:T(8,128)(2,1)} %all-gather.7.cloned.1.call-done, f32[3940,768]{1,0:T(8,128)} %reshape.237, f32[3940]{0:T(1024)S(1)} %mul.448, f32[3940,768]{1,0:T(8,128)} %get-tuple-element.212, ...), kind=kOutput, calls=%fused_computation.155 | convolution fusion | flops 4702278656 | bytes 43562896 | tf_op jit(solution)/shard_map/dot_general | solution.py:48
  505.0 9.6 convolution_convert_fusion.2
  515.1 14.6 %fusion.46 = bf16[768,768]{1,0:T(8,128)(2,1)} fusion(bf16[3940,768]{1,0:T(8,128)(2,1)} %get-tuple-element.218, f32[3940,768]{1,0:T(8,128)} %get-tuple-element.199, f32[768]{0:T(1024)S(1)} %get-tuple-element.157, f32[768]{0:T(1024)S(1)} %get-tuple-element.156, f32[3940]{0:T(1024)S(1)} %add_rsqrt_fusion.1, f32[3940]{0:T(1024)S(1)} %broadcast_multiply_fusion.5), kind=kOutput, calls=%fused_computation.81 | convolution fusion | flops 4663532544 | bytes 19372832 | tf_op jit(solution)/shard_map/dot_general | solution.py:42
  529.7 99.2 %all-reduce.11.cloned.1.call-done = bf16[3940,768]{1,0:T(8,128)(2,1)} async-done(((bf16[3940,768]{1,0:T(8,128)(2,1)}), bf16[3940,768]{1,0:T(8,128)(2,1)}) %all-reduce.11.cloned.1.call-update) | async-done | bytes 6051856 | tf_op jit(solution)/shard_map/psum | solution.py:154
  628.9 11.1 %fusion.9 = (bf16[768]{0:T(1024)(128)(2,1)S(1)}, f32[3940]{0:T(1024)S(1)}, f32[3940]{0:T(1024)S(1)}) fusion(bf16[3940,768]{1,0:T(8,128)(2,1)} %all-reduce.11.cloned.1.call-done, f32[3940,768]{1,0:T(8,128)} %get-tuple-element.199, f32[3940]{0:T(1024)S(1)} %add_rsqrt_fusion.1, f32[3940]{0:T(1024)S(1)} %broadcast_multiply_fusion.5, f32[768]{0:T(1024)S(1)} %get-tuple-element.156), kind=kLoop, calls=%fused_computation.21 | loop fusion | flops 27224632 | bytes 18223168 | tf_op jit(solution)/shard_map/reduce_sum | solution.py:194
  640.0 12.2 %fusion.77 = (bf16[768]{0:T(1024)(128)(2,1)S(1)}, f32[3940,768]{1,0:T(8,128)S(1)}) fusion(f32[3940]{0:T(1024)S(1)} %get-tuple-element.219, f32[3940,768]{1,0:T(8,128)} %get-tuple-element.199, f32[3940]{0:T(1024)S(1)} %broadcast_multiply_fusion.5, f32[3940]{0:T(1024)S(1)} %get-tuple-element.220, f32[768]{0:T(1024)S(1)} %get-tuple-element.156, ...), kind=kLoop, calls=%fused_computation.150 | loop fusion | flops 33284352 | bytes 42446288 | tf_op jit(solution)/shard_map/reduce_sum | solution.py:193
  674.2 19.3 %fusion.43 = bf16[20,197,1,3,64]{1,4,3,0,2:T(8,128)(2,1)} fusion(f32[20,3,197,197]{2,3,1,0:T(8,128)} %fusion.49, f32[20,3,197,197]{2,3,1,0:T(8,128)} %copy-done.1, f32[20,3,197]{2,1,0:T(4,128)S(1)} %copy-done.20, bf16[20,197,1,3,64]{1,0,4,3,2:T(8,128)(2,1)} %copy-done.8), kind=kOutput, calls=%fused_computation.76 | convolution fusion | flops 319021984 | bytes 21701520 | tf_op jit(solution)/shard_map/shqk,sqhc->skhc/dot_general | solution.py:173
  693.5 20.9 %bitcast_reduce_fusion.1 = (bf16[3,64]{1,0:T(4,128)(2,1)S(1)}, bf16[20,3,64,197]{3,2,1,0:T(8,128)(2,1)}) fusion(f32[20,3,197,197]{2,3,1,0:T(8,128)} %fusion.49, f32[20,3,197,197]{2,3,1,0:T(8,128)} %copy-done.1, f32[20,3,197]{2,1,0:T(4,128)S(1)} %copy-done.20, bf16[20,197,1,3,64]{1,0,4,3,2:T(8,128)(2,1)} %copy-done.7), kind=kOutput, calls=%fused_computation.69 | convolution fusion | flops 320534752 | bytes 21701904 | tf_op jit(solution)/shard_map/shqk,skhc->sqhc/dot_general | solution.py:172
  730.1 11.1 %convert_element_type.185 = bf16[3940,576]{0,1:T(8,128)(2,1)} reshape(bf16[20,197,3,3,64]{1,0,4,3,2:T(8,128)(2,1)} %copy.122) | data formatting | bytes 9077760 | tf_op jit(solution)/shard_map/convert_element_type | solution.py:180
  741.7 10.3 convolution_convert_fusion.6
  752.1 9.7 convolution_convert_fusion.3
  761.7 9.2 convolution_convert_fusion
  786.7 21.2 %all-reduce.3 = (bf16[2,192]{1,0:T(2,128)(2,1)S(1)}, bf16[768]{0:T(1024)(128)(2,1)S(1)}) all-reduce(bf16[2,192]{1,0:T(2,128)(2,1)S(1)} %pad_maximum_fusion.1, bf16[768]{0:T(1024)(128)(2,1)S(1)} %get-tuple-element.217), channel_id=6, replica_groups=mesh['dp'=8,'tensor'=4] {'dp'}, use_global_device_ids=true, to_apply=%region_21.0.clone | all-reduce | flops 1152 | bytes 4608
  810.9 60.5 %reduce-scatter.11.cloned.1.call-done = bf16[96,3,192]{2,0,1:T(8,128)(2,1)} async-done(((bf16[768,3,192]{2,0,1:T(8,128)(2,1)}), bf16[96,3,192]{2,0,1:T(8,128)(2,1)}) %reduce-scatter.11.cloned.1.call-update) | async-done | bytes 110608 | tf_op jit(solution)/shard_map/reduce_scatter | solution.py:200
  873.5 111.1 %all-reduce.13.cloned.1.call-done = (bf16[3940,768]{1,0:T(8,128)(2,1)}, bf16[3940,768]{1,0:T(8,128)(2,1)}) async-done(((bf16[3940,768]{1,0:T(8,128)(2,1)}, bf16[3940,768]{1,0:T(8,128)(2,1)}), (bf16[3940,768]{1,0:T(8,128)(2,1)}, bf16[3940,768]{1,0:T(8,128)(2,1)})) %all-reduce.13.cloned.1.call-update) | async-done | bytes 12103696 | tf_op jit(solution)/shard_map/psum | solution.py:140
  988.2 16.8 %fusion.10 = (bf16[768]{0:T(1024)(128)(2,1)S(1)}, f32[3940]{0:T(1024)S(1)}, f32[3940]{0:T(1024)S(1)}, f32[3940,768]{1,0:T(8,128)}, f32[3940,768]{1,0:T(8,128)}) fusion(bf16[3940,768]{1,0:T(8,128)(2,1)} %get-tuple-element.164, f32[768]{0:T(1024)S(1)} %copy-done.37, f32[3940]{0:T(1024)S(1)} %rsqrt.22, f32[3940,768]{1,0:T(8,128)} %reshape.232, f32[3940]{0:T(1024)S(1)} %div.138), kind=kLoop, calls=%fused_computation.22 | loop fusion | flops 27224632 | bytes 42430528 | tf_op jit(solution)/shard_map/reduce_sum | solution.py:191
  1006.0 10.9 %dynamic-slice_add_fusion = f32[3940,192]{1,0:T(8,128)} fusion(f32[3940,768]{1,0:T(8,128)} %copy-done, s32[]{:T(128)S(6)} %select_n.2, f32[3940,768]{1,0:T(8,128)} %get-tuple-element.195, f32[3940,768]{1,0:T(8,128)} %get-tuple-element.203, f32[3940]{0:T(1024)S(1)} %rsqrt.22, f32[3940]{0:T(1024)S(1)} %broadcast_multiply_fusion.1, ...), kind=kLoop, calls=%fused_computation.62 | loop fusion | flops 3782400 | bytes 12150964 | tf_op jit(solution)/shard_map/add | solution.py:185
  1043.4 24.8 %reduce-scatter.19.cloned.1.call-done = bf16[96,6]{1,0:T(8,128)(2,1)} async-done(((bf16[768,6]{1,0:T(8,128)(2,1)}), bf16[96,6]{1,0:T(8,128)(2,1)}) %reduce-scatter.19.cloned.1.call-update) | async-done | bytes 1168
  (214 shorter events, 164.3 us)
Async XLA Ops:
  8.0 305.1 %all-reduce.9.cloned.1.call-start = ((), (), s32[]{:S(2)}) async-start(), calls=%async_computation.5 | async-start | bytes 12115968 | tf_op jit(solution)/shard_map/psum | solution.py:131
  58.6 81.1 %copy-start.36 = (f32[768]{0:T(1024)}, f32[768]{0:T(1024)S(1)}, u32[]{:S(2)}) copy-start(f32[768]{0:T(1024)S(1)} %get-tuple-element.160) | copy-start | bytes 9220
  63.9 84.2 %copy-start.21 = (f32[20,197]{1,0:T(8,128)}, f32[20,197]{1,0:T(8,128)S(1)}, u32[]{:S(2)}) copy-start(f32[20,197]{1,0:T(8,128)S(1)} %broadcast_multiply_fusion) | copy-start | bytes 47284
  69.9 84.2 %copy-start.32 = (f32[20,197]{1,0:T(8,128)}, f32[20,197]{1,0:T(8,128)S(1)}, u32[]{:S(2)}) copy-start(f32[20,197]{1,0:T(8,128)S(1)} %add_rsqrt_fusion) | copy-start | bytes 47284
  101.9 93.5 %copy-start.9 = (bf16[192,768]{0,1:T(8,128)(2,1)}, bf16[192,768]{0,1:T(8,128)(2,1)S(1)}, u32[]{:S(2)}) copy-start(bf16[192,768]{0,1:T(8,128)(2,1)S(1)} %all_gather.24) | copy-start | bytes 884740
  199.9 131.3 %all-gather.5.cloned.1.call-start = ((), (), s32[]{:S(2)}) async-start(), calls=%async_computation.6 | async-start | bytes 1327104 | tf_op jit(solution)/shard_map/all_gather | solution.py:93
  200.6 242.8 %reduce-scatter.15.cloned.1.call-start = ((), (), s32[]{:S(2)}) async-start(), calls=%async_computation.11 | async-start | bytes 1327104 | tf_op jit(solution)/shard_map/reduce_scatter | solution.py:209
  367.7 75.7 %copy-start.25 = (f32[768,96]{0,1:T(8,128)S(1)}, f32[768,96]{0,1:T(8,128)}, u32[]{:S(2)}) copy-start(f32[768,96]{0,1:T(8,128)} %param.30) | copy-start | bytes 884740
  367.7 75.7 %copy-start.26 = (f32[768,96]{0,1:T(8,128)S(1)}, f32[768,96]{0,1:T(8,128)}, u32[]{:S(2)}) copy-start(f32[768,96]{0,1:T(8,128)} %param.40) | copy-start | bytes 884740
  367.7 75.7 %copy-start.27 = (f32[768,96]{0,1:T(8,128)S(1)}, f32[768,96]{0,1:T(8,128)}, u32[]{:S(2)}) copy-start(f32[768,96]{0,1:T(8,128)} %param.41) | copy-start | bytes 884740
  378.4 108.1 %all-gather.7.cloned.1.call-start = ((), (), s32[]{:S(2)}) async-start(), calls=%async_computation.7 | async-start | bytes 1327104 | tf_op jit(solution)/shard_map/all_gather | solution.py:94
  445.5 183.5 %all-reduce.11.cloned.1.call-start = ((), (), s32[]{:S(2)}) async-start(), calls=%async_computation.8 | async-start | bytes 12115968 | tf_op jit(solution)/shard_map/psum | solution.py:154
  514.6 266.2 %reduce-scatter.13.cloned.1.call-start = ((), (), s32[]{:S(2)}) async-start(), calls=%async_computation.10 | async-start | bytes 1327104 | tf_op jit(solution)/shard_map/reduce_scatter | solution.py:206
  529.7 279.6 %reduce-scatter.17.cloned.1.call-start = ((), (), s32[]{:S(2)}) async-start(), calls=%async_computation.12 | async-start | bytes 442368
  741.2 130.3 %reduce-scatter.11.cloned.1.call-start = ((), (), s32[]{:S(2)}) async-start(), calls=%async_computation.9 | async-start | bytes 1327104 | tf_op jit(solution)/shard_map/reduce_scatter | solution.py:200
  752.0 232.5 %all-reduce.13.cloned.1.call-start = ((), (), s32[]{:S(2)}) async-start(), calls=%async_computation.14 | async-start | bytes 24231936 | tf_op jit(solution)/shard_map/psum | solution.py:140
  771.0 36.9 %copy-start.48 = (f32[96]{0:T(128)S(1)}, f32[96]{0:T(128)}, u32[]{:S(2)}) copy-start(f32[96]{0:T(128)} %param.32) | copy-start | bytes 1156
  771.0 36.9 %copy-start.49 = (f32[96]{0:T(128)S(1)}, f32[96]{0:T(128)}, u32[]{:S(2)}) copy-start(f32[96]{0:T(128)} %param.44) | copy-start | bytes 1156
  771.0 37.5 %copy-start.44 = (f32[2,24]{1,0:T(2,128)S(1)}, f32[2,24]{1,0:T(2,128)}, u32[]{:S(2)}) copy-start(f32[2,24]{1,0:T(2,128)} %param.31) | copy-start | bytes 580
  771.0 37.5 %copy-start.45 = (f32[2,24]{1,0:T(2,128)S(1)}, f32[2,24]{1,0:T(2,128)}, u32[]{:S(2)}) copy-start(f32[2,24]{1,0:T(2,128)} %param.42) | copy-start | bytes 580
  771.1 37.5 %copy-start.46 = (f32[2,24]{1,0:T(2,128)S(1)}, f32[2,24]{1,0:T(2,128)}, u32[]{:S(2)}) copy-start(f32[2,24]{1,0:T(2,128)} %param.43) | copy-start | bytes 580
  771.1 39.1 %copy-start.24 = (f32[192,96]{1,0:T(8,128)S(1)}, f32[192,96]{1,0:T(8,128)}, u32[]{:S(2)}) copy-start(f32[192,96]{1,0:T(8,128)} %param.28) | copy-start | bytes 221188
  771.1 39.1 %copy-start.34 = (f32[192,96]{1,0:T(8,128)S(1)}, f32[192,96]{1,0:T(8,128)}, u32[]{:S(2)}) copy-start(f32[192,96]{1,0:T(8,128)} %param.36) | copy-start | bytes 221188
  771.1 39.1 %copy-start.35 = (f32[192,96]{1,0:T(8,128)S(1)}, f32[192,96]{1,0:T(8,128)}, u32[]{:S(2)}) copy-start(f32[192,96]{1,0:T(8,128)} %param.37) | copy-start | bytes 221188
  771.1 100.4 %copy-start.16 = (f32[96,3,192]{2,0,1:T(8,128)S(1)}, f32[96,3,192]{2,0,1:T(8,128)}, u32[]{:S(2)}) copy-start(f32[96,3,192]{2,0,1:T(8,128)} %param.27) | copy-start | bytes 663556
  771.1 100.4 %copy-start.30 = (f32[96,3,192]{2,0,1:T(8,128)S(1)}, f32[96,3,192]{2,0,1:T(8,128)}, u32[]{:S(2)}) copy-start(f32[96,3,192]{2,0,1:T(8,128)} %param.34) | copy-start | bytes 663556
  771.1 100.3 %copy-start.31 = (f32[96,3,192]{2,0,1:T(8,128)S(1)}, f32[96,3,192]{2,0,1:T(8,128)}, u32[]{:S(2)}) copy-start(f32[96,3,192]{2,0,1:T(8,128)} %param.35) | copy-start | bytes 663556
  771.1 297.1 %reduce-scatter.19.cloned.1.call-start = ((), (), s32[]{:S(2)}) async-start(), calls=%async_computation.13 | async-start | bytes 221184
  773.2 215.0 %copy-start.37 = (f32[768]{0:T(1024)S(1)}, f32[768]{0:T(1024)}, u32[]{:S(2)}) copy-start(f32[768]{0:T(1024)} %copy-done.36) | copy-start | bytes 9220
  1027.6 41.4 %copy-start.38 = (f32[6,96]{1,0:T(8,128)S(1)}, f32[6,96]{1,0:T(8,128)}, u32[]{:S(2)}) copy-start(f32[6,96]{1,0:T(8,128)} %param.33) | copy-start | bytes 6916
  1027.6 41.4 %copy-start.39 = (f32[6,96]{1,0:T(8,128)S(1)}, f32[6,96]{1,0:T(8,128)}, u32[]{:S(2)}) copy-start(f32[6,96]{1,0:T(8,128)} %param.46) | copy-start | bytes 6916
  1027.6 41.4 %copy-start.40 = (f32[6,96]{1,0:T(8,128)S(1)}, f32[6,96]{1,0:T(8,128)}, u32[]{:S(2)}) copy-start(f32[6,96]{1,0:T(8,128)} %param.47) | copy-start | bytes 6916
  (32 other events, 345.3 us)
Sparse Core Ops, SparseCore 0:
  200.0 113.1 all-reduce.8
  514.7 114.1 all-reduce.10
  771.1 213.3 all-reduce.12
Sparse Core Ops, SparseCore 1:
  203.1 38.7 all-gather.4
  378.5 64.9 reduce-scatter.14
  446.0 40.4 all-gather.6
  529.7 63.0 reduce-scatter.12
  741.3 62.4 reduce-scatter.16
  807.7 63.7 reduce-scatter.10
  1006.1 62.1 reduce-scatter.18
where the time goes:
time: 1080 us
  waiting for transfers between devices  465 us (43%)
  matrix products  195 us (18%)
  blocking collectives  156 us (14%)
  other arithmetic  124 us (11%)
  local copies, waits for them, and re-layouts  116 us (11%)
  between operations  18.9 us (2%)
    psum x1, waiting for transfers between devices, on_device(): lax.psum(mlp_part.astype(jnp.bfloat16), 'tensor').astype(jnp.float32)  111 us
    psum x1, waiting for transfers between devices, on_device(): lax.psum(times_transposed(d_pre_half, w_expand).astype(jnp.bfloat16), 'te...  99.2 us
    reduce_scatter x1, waiting for transfers between devices, on_device(): lax.psum_scatter(d_reduce.astype(jnp.bfloat16), 'dp', scatter_dimension=1...  65 us
    psum x1, waiting for transfers between devices, on_device(): lax.psum(jnp.dot(mixed, w_proj, preferred_element_type=f32).astype(jnp.bf...  63.4 us
    reduce_scatter x1, waiting for transfers between devices, on_device(): lax.psum_scatter(d_qkv.astype(jnp.bfloat16), 'dp', scatter_dimension=0, t...  60.5 us
    all_gather x1, waiting for transfers between devices, on_device(): lax.all_gather(reduce_weight.astype(bf16), 'dp', axis=1, tiled=True)  41 us
    dot_general x4, matrix products, times_transposed(): lax.dot_general(left, right, (((1,), (1,)), ((), ())), preferred_element_...  40.4 us
    unnamed x2, blocking collectives  39.5 us
  transfers between devices with their start and end apart: 10, of which 7 were waited for; matrix products, arithmetic and copies ran while one was open for 24% of the time, Pallas kernels for 0%

commit v1 on v0

v1 whole, which is shorter than its diff:
```python
import functools

import jax
import jax.numpy as jnp
from jax import lax
from jax.experimental import pallas as pl
from jax.experimental.pallas import tpu as pltpu
from jax.sharding import PartitionSpec as P

HEAD_DIM = 64
f32 = jnp.float32
bf16 = jnp.bfloat16

lr_matrix = 0.006
lr_vector = 0.1
decay = 0.05
beta_one = 0.9
beta_two = 0.999
adam_eps = 1e-08
adam_step = 2.0
norm_eps = 1e-06
SMALL_ROWS = 16
VMEM_MAX = 63 * 1024 * 1024


def dot_nn(a, b):
    return lax.dot_general(a, b, (((1,), (0,)), ((), ())), preferred_element_type=f32)


def dot_nt(a, b):
    return lax.dot_general(a, b, (((1,), (1,)), ((), ())), preferred_element_type=f32)


def dot_tn(a, b):
    return lax.dot_general(a, b, (((0,), (0,)), ((), ())), preferred_element_type=f32)


def half_round(v):
    return v.astype(bf16).astype(f32)


def norm_stats(rows):
    mean = jnp.mean(rows, axis=-1, keepdims=True)
    centred = rows - mean
    variance = jnp.mean(centred * centred, axis=-1, keepdims=True)
    scale = lax.rsqrt(variance + norm_eps)
    return centred * scale, scale


def norm_back(grad_in, normed, scale, gain):
    scaled = grad_in * gain
    return scale * (
        scaled
        - jnp.mean(scaled, axis=-1, keepdims=True)
        - normed * jnp.mean(scaled * normed, axis=-1, keepdims=True)
    )


def places(n_z):
    dp = lax.axis_index("dp")
    t = lax.axis_index("tensor")
    z, x = dp // 2, dp % 2
    y, c = t // 2, t % 2
    fy, fx = 1 - 2 * y, 1 - 2 * x
    first = (dp + c * fx, t + (1 - c) * 2 * fy)
    second = (dp + (1 - c) * fx, t + c * 2 * fy)
    sibling = (dp, t + 1 - 2 * c)
    sets = (
        (y, x),
        (y + (1 - c) * fy, x + c * fx),
        (y + c * fy, x + (1 - c) * fx),
        (1 - y, 1 - x),
    )
    along_z = [(lax.rem(z + k, n_z) * 2 + x, t) for k in range(1, n_z)]
    return z, x, y, c, first, second, sibling, sets, along_z


def greet(peers):
    barrier = pltpu.get_barrier_semaphore()
    for peer in peers:
        pl.semaphore_signal(barrier, inc=1, device_id=peer, device_id_type=pl.DeviceIdType.MESH)
    pl.semaphore_wait(barrier, len(peers))


def push(src, dst, send, recv, peer):
    return pltpu.make_async_remote_copy(
        src_ref=src,
        dst_ref=dst,
        send_sem=send,
        recv_sem=recv,
        device_id=peer,
        device_id_type=pl.DeviceIdType.MESH,
    )


def gather_body(n_w, n_z, *refs):
    shards, outs = refs[:n_w], refs[n_w : 2 * n_w]
    local_sem, z_send, z_recv, s_send, s_recv = refs[2 * n_w :]
    z, x, y, c, first, second, sibling, sets, along_z = places(n_z)
    greet([first, second, sibling] + along_z)

    def own(w):
        return pltpu.make_async_copy(shards[w], outs[w].at[y, c, z, x], local_sem.at[w])

    def to_z(w, k):
        return push(shards[w], outs[w].at[y, c, z, x], z_send.at[w, k], z_recv.at[w, k], along_z[k])

    def move(w, which, peer, slot):
        sy, sx = sets[which]
        part = outs[w].at[sy, c, :, sx]
        return push(part, part, s_send.at[w, slot], s_recv.at[w, slot], peer)

    plan = {
        0: (0, first),
        1: (0, second),
        2: (1, second),
        3: (0, sibling),
        4: (1, sibling),
        5: (2, sibling),
        6: (3, sibling),
    }

    def go(w, slot):
        which, peer = plan[slot]
        move(w, which, peer, slot).start()

    def arrived(w, slot):
        which, peer = plan[slot]
        move(w, which, peer, slot).wait_recv()

    for w in range(n_w):
        own(w).start()
        for k in range(n_z - 1):
            to_z(w, k).start()
    for step in range(n_w + 3):
        w = step
        if 0 <= w < n_w:
            own(w).wait()
            for k in range(n_z - 1):
                to_z(w, k).wait_recv()
            for slot in (0, 1, 3):
                go(w, slot)
        w = step - 1
        if 0 <= w < n_w:
            arrived(w, 0)
            go(w, 2)
            go(w, 4)
        w = step - 2
        if 0 <= w < n_w:
            arrived(w, 1)
            go(w, 5)
            arrived(w, 2)
            go(w, 6)
        w = step - 3
        if 0 <= w < n_w:
            for slot in (3, 4, 5, 6):
                arrived(w, slot)
    for w in range(n_w):
        for k in range(n_z - 1):
            to_z(w, k).wait_send()
        for slot, (which, peer) in plan.items():
            move(w, which, peer, slot).wait_send()


def gather_all(shards, n_dp):
    n_w, n_z = len(shards), n_dp // 2
    shapes = [(2, 2, n_z, 2) + s.shape for s in shards]
    return pl.pallas_call(
        functools.partial(gather_body, n_w, n_z),
        out_shape=[jax.ShapeDtypeStruct(s, bf16) for s in shapes],
        in_specs=[pl.BlockSpec(memory_space=pltpu.VMEM)] * n_w,
        out_specs=[pl.BlockSpec(memory_space=pl.ANY)] * n_w,
        scratch_shapes=[
            pltpu.SemaphoreType.DMA((n_w,)),
            pltpu.SemaphoreType.DMA((n_w, n_z - 1)),
            pltpu.SemaphoreType.DMA((n_w, n_z - 1)),
            pltpu.SemaphoreType.DMA((n_w, 7)),
            pltpu.SemaphoreType.DMA((n_w, 7)),
        ],
        compiler_params=pltpu.CompilerParams(collective_id=0, has_side_effects=True),
        name="gather_weights",
    )(*shards)


def reduce_body(n_w, n_z, widths, *refs):
    grads, outs = refs[:n_w], refs[n_w : 2 * n_w]
    acc, got = refs[2 * n_w : 3 * n_w], refs[3 * n_w : 4 * n_w]
    got2, got1, gotz = refs[4 * n_w : 5 * n_w], refs[5 * n_w : 6 * n_w], refs[6 * n_w : 7 * n_w]
    local_sem, c_send, c_recv, s_send, s_recv, z_send, z_recv = refs[7 * n_w :]
    z, x, y, c, first, second, sibling, sets, along_z = places(n_z)
    greet([first, second, sibling] + along_z)
    swap = (0, 2, 1, 3)

    def part(w, which, core):
        sy, sx = sets[which]
        lanes = pl.ds(pl.multiple_of((sy * 2 + core) * widths[w], 128), widths[w])
        return grads[w].at[:, sx, :, lanes]

    def mine(w, k):
        return pltpu.make_async_copy(part(w, k, c), acc[w].at[k], local_sem.at[w, k])

    def to_sibling(w, k):
        s = swap[k]
        return push(part(w, k, 1 - c), got[w].at[s], c_send.at[w, s], c_recv.at[w, s], sibling)

    def to_second(w, k):
        return push(acc[w].at[k], got2[w].at[k - 2], s_send.at[w, k - 2], s_recv.at[w, k - 2], second)

    def to_first(w):
        return push(acc[w].at[1], got1[w], s_send.at[w, 2], s_recv.at[w, 2], first)

    def to_z(w, k):
        return push(
            acc[w].at[0, along_z[k][0] // 2], gotz[w].at[k], z_send.at[w, k], z_recv.at[w, k], along_z[k]
        )

    def add(w, k, other):
        def one(i, carry):
            acc[w][k, i] = (acc[w][k, i].astype(f32) + other(i).astype(f32)).astype(bf16)
            return carry

        lax.fori_loop(0, n_z, one, 0)

    for w in range(n_w):
        for k in (3, 1, 2, 0):
            to_sibling(w, k).start()
        for k in (3, 2, 1, 0):
            mine(w, k).start()
    for step in range(n_w + 3):
        w = step
        if 0 <= w < n_w:
            for k in (3, 2, 1, 0):
                mine(w, k).wait()
                to_sibling(w, swap[k]).wait_recv()
                add(w, k, lambda i, k=k: got[w][k, i])
                if k >= 2:
                    to_second(w, k).start()
        w = step - 1
        if 0 <= w < n_w:
            to_second(w, 3).wait_recv()
            add(w, 1, lambda i: got2[w][1, i])
            to_first(w).start()
            to_second(w, 2).wait_recv()
            add(w, 0, lambda i: got2[w][0, i])
        w = step - 2
        if 0 <= w < n_w:
            to_first(w).wait_recv()
            add(w, 0, lambda i: got1[w][i])
            for k in range(n_z - 1):
                to_z(w, k).start()
        w = step - 3
        if 0 <= w < n_w:
            total = acc[w][0, z].astype(f32)
            for k in range(n_z - 1):
                to_z(w, k).wait_recv()
                total = total + gotz[w][k].astype(f32)
            outs[w][...] = total
    for w in range(n_w):
        for k in range(4):
            to_sibling(w, k).wait_send()
        to_second(w, 2).wait_send()
        to_second(w, 3).wait_send()
        to_first(w).wait_send()
        for k in range(n_z - 1):
            to_z(w, k).wait_send()


def reduce_all(grads, widths, n_dp):
    n_w, n_z = len(grads), n_dp // 2
    rows = [g.shape[0] // n_dp for g in grads]
    shaped = [g.reshape(n_z, 2, r, g.shape[1]) for g, r in zip(grads, rows)]
    blocks = list(zip(rows, widths))
    scratch = [pltpu.VMEM((4, n_z) + b, bf16) for b in blocks]
    scratch += [pltpu.VMEM((4, n_z) + b, bf16) for b in blocks]
    scratch += [pltpu.VMEM((2, n_z) + b, bf16) for b in blocks]
    scratch += [pltpu.VMEM((n_z,) + b, bf16) for b in blocks]
    scratch += [pltpu.VMEM((n_z - 1,) + b, bf16) for b in blocks]
    scratch += [pltpu.SemaphoreType.DMA((n_w, 4))] * 3
    scratch += [pltpu.SemaphoreType.DMA((n_w, 3))] * 2
    scratch += [pltpu.SemaphoreType.DMA((n_w, n_z - 1))] * 2
    return pl.pallas_call(
        functools.partial(reduce_body, n_w, n_z, tuple(widths)),
        out_shape=[jax.ShapeDtypeStruct(b, f32) for b in blocks],
        in_specs=[pl.BlockSpec(memory_space=pl.ANY)] * n_w,
        out_specs=[pl.BlockSpec(memory_space=pltpu.VMEM)] * n_w,
        scratch_shapes=scratch,
        compiler_params=pltpu.CompilerParams(
            collective_id=1, has_side_effects=True, vmem_limit_bytes=VMEM_MAX
        ),
        name="reduce_grads",
    )(*shaped)


def key_mask(rows, seq):
    return lax.broadcasted_iota(jnp.int32, (rows, rows), 1) < seq


def load_rows(src, dst, seq):
    dst[pl.ds(0, seq), :] = src[0]


def front_body(seq, n_heads, where, x_ref, vec_ref, bias_ref, wq_ref, a1_ref, qkv_ref, mix_ref, lse_ref, xs):
    rows = xs.shape[0]

    @pl.when(pl.program_id(0) == 0)
    def _():
        xs[...] = jnp.zeros_like(xs)

    load_rows(x_ref, xs, seq)
    normed, unused = norm_stats(xs[...])
    a1 = (normed * vec_ref[0:1, :] + vec_ref[1:2, :]).astype(bf16)
    a1_ref[...] = a1
    mask = key_mask(rows, seq)
    lane = lax.broadcasted_iota(jnp.int32, (rows, 128), 1)
    lse_ref[...] = jnp.zeros_like(lse_ref)
    q_width = n_heads * HEAD_DIM
    wide = bias_ref.shape[2]
    pad = mix_ref.shape[1] // 4 - q_width
    for t in range(4):
        qkv = (dot_nn(a1_ref[...], wq_ref[t, :, :wide]) + bias_ref[t, 0:1, :]).astype(bf16)
        qkv_ref[:, t * wide : (t + 1) * wide] = qkv
        outs = [jnp.zeros((rows, pad), bf16)]
        for h in range(n_heads):
            q = qkv[:, h * HEAD_DIM : (h + 1) * HEAD_DIM]
            k = qkv[:, q_width + h * HEAD_DIM : q_width + (h + 1) * HEAD_DIM]
            v = qkv[:, 2 * q_width + h * HEAD_DIM : 2 * q_width + (h + 1) * HEAD_DIM]
            s = jnp.where(mask, dot_nt(q, k) * (HEAD_DIM**-0.5), -1e30)
            top = jnp.max(s, axis=-1, keepdims=True)
            e = jnp.exp(s - top)
            total = jnp.sum(e, axis=-1, keepdims=True)
            p = (e * (1.0 / total)).astype(bf16)
            outs.append(dot_nn(p, v).astype(bf16))
            lse = top + jnp.log(total)
            lse_ref[...] = jnp.where(lane == t * n_heads + h, lse, lse_ref[...])
        mix_ref[:, t * (pad + q_width) : (t + 1) * (pad + q_width)] = jnp.concatenate(outs, axis=1)


def front(where, tokens, vec, bias, wq, n_img, rows, n_heads):
    slots, seq, width = tokens.shape
    wide = bias.shape[2]
    mix = width - (3 * n_heads * HEAD_DIM // 128) * 128
    total = n_img * rows
    return pl.pallas_call(
        functools.partial(front_body, seq, n_heads),
        out_shape=[
            jax.ShapeDtypeStruct((total, width), bf16),
            jax.ShapeDtypeStruct((total, 4 * wide), bf16),
            jax.ShapeDtypeStruct((total, 4 * mix), bf16),
            jax.ShapeDtypeStruct((total, 128), f32),
        ],
        grid_spec=pltpu.PrefetchScalarGridSpec(
            num_scalar_prefetch=1,
            grid=(n_img,),
            in_specs=[
                pl.BlockSpec((1, seq, width), lambda i, s: (s[0] + i, 0, 0)),
                pl.BlockSpec(vec.shape, lambda i, s: (0, 0)),
                pl.BlockSpec(bias.shape, lambda i, s: (0, 0, 0)),
                pl.BlockSpec(wq.shape, lambda i, s: (0, 0, 0), pipeline_mode=pl.Buffered(1)),
            ],
            out_specs=[
                pl.BlockSpec((rows, width), lambda i, s: (i, 0)),
                pl.BlockSpec((rows, 4 * wide), lambda i, s: (i, 0)),
                pl.BlockSpec((rows, 4 * mix), lambda i, s: (i, 0)),
                pl.BlockSpec((rows, 128), lambda i, s: (i, 0)),
            ],
            scratch_shapes=[pltpu.VMEM((rows, width), f32)],
        ),
        compiler_params=pltpu.CompilerParams(vmem_limit_bytes=VMEM_MAX),
        name="front",
    )(where, tokens, vec, bias, wq)


def middle_body(
    seq,
    where,
    x_ref,
    cot_ref,
    mix_ref,
    vec_ref,
    bexp_ref,
    wq_ref,
    we_ref,
    wr_ref,
    a2_ref,
    hid_ref,
    dpre_ref,
    gh_ref,
    dres_ref,
    drh_ref,
    dmix_ref,
    out_ref,
    dvec_ref,
    dbexp_ref,
    xs,
    gs,
):
    i = pl.program_id(0)

    @pl.when(i == 0)
    def _():
        xs[...] = jnp.zeros_like(xs)
        gs[...] = jnp.zeros_like(gs)
        dvec_ref[...] = jnp.zeros_like(dvec_ref)
        dbexp_ref[...] = jnp.zeros_like(dbexp_ref)

    live = jnp.where(where[0] + i < where[1], 1.0, 0.0).astype(f32)
    load_rows(x_ref, xs, seq)
    gs[pl.ds(0, seq), :] = cot_ref[0] * live
    rows, width = xs.shape
    mix = mix_ref.shape[1] // 4
    ff = we_ref.shape[2]
    att = jnp.zeros((rows, width), f32)
    for t in range(4):
        att += half_round(dot_nt(mix_ref[:, t * mix : (t + 1) * mix], wq_ref[t, :, width - mix :]))
    resid = xs[...] + att + vec_ref[2:3, :]
    normed2, scale2 = norm_stats(resid)
    a2_ref[...] = (normed2 * vec_ref[3:4, :] + vec_ref[4:5, :]).astype(bf16)
    gh_ref[...] = gs[...].astype(bf16)
    feed = jnp.zeros((rows, width), f32)
    d_a2 = jnp.zeros((rows, width), f32)
    for t in range(4):
        pre = dot_nn(a2_ref[...], we_ref[t]) + bexp_ref[t, 0:1, :]
        cdf = 0.5 + 0.5 * lax.erf(pre * (0.5**0.5))
        hid = (pre * cdf).astype(bf16)
        slope = cdf + pre * jnp.exp(-0.5 * pre * pre) * ((2.0 * jnp.pi) ** -0.5)
        hid_ref[:, t * ff : (t + 1) * ff] = hid
        d_pre = dot_nn(gh_ref[...], wr_ref[t]) * slope
        dbexp_ref[t, 0:1, :] += jnp.sum(d_pre, axis=0, keepdims=True)
        dph = d_pre.astype(bf16)
        dpre_ref[:, t * ff : (t + 1) * ff] = dph
        feed += half_round(dot_nt(hid, wr_ref[t]))
        d_a2 += half_round(dot_nt(dph, we_ref[t]))
    out = (resid + feed + vec_ref[5:6, :]) * live
    col = width // 4
    for t in range(4):
        out_ref[t, 0] = out[:seq, t * col : (t + 1) * col].astype(bf16)
    d_resid = gs[...] + norm_back(d_a2, normed2, scale2, vec_ref[3:4, :])
    dres_ref[...] = d_resid
    drh = d_resid.astype(bf16)
    drh_ref[...] = drh
    for t in range(4):
        dmix_ref[:, t * mix : (t + 1) * mix] = dot_nn(drh, wq_ref[t, :, width - mix :]).astype(bf16)
    dvec_ref[2:3, :] += jnp.sum(d_resid, axis=0, keepdims=True)
    dvec_ref[3:4, :] += jnp.sum(d_a2 * normed2, axis=0, keepdims=True)
    dvec_ref[4:5, :] += jnp.sum(d_a2, axis=0, keepdims=True)
    dvec_ref[5:6, :] += jnp.sum(gs[...], axis=0, keepdims=True)


def middle(where, tokens, cotangent, mixp, vec, bexp, wq, we, wr, n_img, rows):
    slots, seq, width = tokens.shape
    ff = we.shape[2]
    mix = mixp.shape[1]
    total = n_img * rows
    col = width // 4
    row_block = lambda n: pl.BlockSpec((rows, n), lambda i, s: (i, 0))
    whole = lambda a: pl.BlockSpec(
        a.shape, lambda i, s, nd=len(a.shape): (0,) * nd, pipeline_mode=pl.Buffered(1)
    )
    image = pl.BlockSpec((1, seq, width), lambda i, s: (s[0] + i, 0, 0))
    return pl.pallas_call(
        functools.partial(middle_body, seq),
        out_shape=[
            jax.ShapeDtypeStruct((total, width), bf16),
            jax.ShapeDtypeStruct((total, 4 * ff), bf16),
            jax.ShapeDtypeStruct((total, 4 * ff), bf16),
            jax.ShapeDtypeStruct((total, width), bf16),
            jax.ShapeDtypeStruct((total, width), f32),
            jax.ShapeDtypeStruct((total, width), bf16),
            jax.ShapeDtypeStruct((total, mix), bf16),
            jax.ShapeDtypeStruct((4, n_img, seq, col), bf16),
            jax.ShapeDtypeStruct((8, width), f32),
            jax.ShapeDtypeStruct((4, 8, ff), f32),
        ],
        grid_spec=pltpu.PrefetchScalarGridSpec(
            num_scalar_prefetch=1,
            grid=(n_img,),
            in_specs=[image, image, row_block(mix)] + [whole(a) for a in (vec, bexp, wq, we, wr)],
            out_specs=[
                row_block(width),
                row_block(4 * ff),
                row_block(4 * ff),
                row_block(width),
                row_block(width),
                row_block(width),
                row_block(mix),
                pl.BlockSpec((4, 1, seq, col), lambda i, s: (0, i, 0, 0)),
                pl.BlockSpec((8, width), lambda i, s: (0, 0)),
                pl.BlockSpec((4, 8, ff), lambda i, s: (0, 0, 0)),
            ],
            scratch_shapes=[pltpu.VMEM((rows, width), f32), pltpu.VMEM((rows, width), f32)],
        ),
        compiler_params=pltpu.CompilerParams(vmem_limit_bytes=VMEM_MAX),
        name="middle",
    )(where, tokens, cotangent, mixp, vec, bexp, wq, we, wr)


def back_body(
    seq,
    n_heads,
    where,
    x_ref,
    qkv_ref,
    lse_ref,
    dmix_ref,
    dres_ref,
    vec_ref,
    wq_ref,
    dqkv_ref,
    gt_ref,
    dvec_ref,
    dbias_ref,
    xs,
):
    i = pl.program_id(0)

    @pl.when(i == 0)
    def _():
        xs[...] = jnp.zeros_like(xs)
        dvec_ref[...] = jnp.zeros_like(dvec_ref)
        dbias_ref[...] = jnp.zeros_like(dbias_ref)

    load_rows(x_ref, xs, seq)
    rows, width = xs.shape
    mask = key_mask(rows, seq)
    q_width = n_heads * HEAD_DIM
    wide = qkv_ref.shape[1] // 4
    mix = dmix_ref.shape[1] // 4
    scale_qk = HEAD_DIM**-0.5
    d_a1 = jnp.zeros((rows, width), f32)
    for t in range(4):
        dq, dk, dv = [], [], []
        for h in range(n_heads):
            at = t * wide + h * HEAD_DIM
            q = qkv_ref[:, at : at + HEAD_DIM]
            k = qkv_ref[:, at + q_width : at + q_width + HEAD_DIM]
            v = qkv_ref[:, at + 2 * q_width : at + 2 * q_width + HEAD_DIM]
            m_at = (t + 1) * mix - q_width + h * HEAD_DIM
            dm = dmix_ref[:, m_at : m_at + HEAD_DIM]
            lse = lse_ref[:, t * n_heads + h : t * n_heads + h + 1]
            p = jnp.where(mask, jnp.exp(dot_nt(q, k) * scale_qk - lse), 0.0)
            dv.append(dot_tn(p.astype(bf16), dm))
            d_p = dot_nt(dm, v)
            delta = jnp.sum(p * d_p, axis=-1, keepdims=True)
            ds = (p * (d_p - delta) * scale_qk).astype(bf16)
            dq.append(dot_nn(ds, k))
            dk.append(dot_tn(ds, q))
        d_all = jnp.concatenate(dq + dk + dv + [jnp.zeros((rows, wide - 3 * q_width), f32)], axis=1)
        dbias_ref[t, 0:1, :] += jnp.sum(d_all, axis=0, keepdims=True)
        d_half = d_all.astype(bf16)
        dqkv_ref[:, t * wide : (t + 1) * wide] = d_half
        d_a1 += half_round(dot_nt(d_half, wq_ref[t, :, :wide]))
    normed, scale = norm_stats(xs[...])
    grad = dres_ref[...] + norm_back(d_a1, normed, scale, vec_ref[0:1, :])
    col = width // 4
    for t in range(4):
        gt_ref[t, 0] = grad[:seq, t * col : (t + 1) * col].astype(bf16)
    dvec_ref[0:1, :] += jnp.sum(d_a1 * normed, axis=0, keepdims=True)
    dvec_ref[1:2, :] += jnp.sum(d_a1, axis=0, keepdims=True)


def back(where, tokens, qkv, lse, dmix, dres, vec, wq, n_img, rows, n_heads):
    slots, seq, width = tokens.shape
    total = n_img * rows
    wide = qkv.shape[1] // 4
    col = width // 4
    row_block = lambda n: pl.BlockSpec((rows, n), lambda i, s: (i, 0))
    whole = lambda a: pl.BlockSpec(
        a.shape, lambda i, s, nd=len(a.shape): (0,) * nd, pipeline_mode=pl.Buffered(1)
    )
    return pl.pallas_call(
        functools.partial(back_body, seq, n_heads),
        out_shape=[
            jax.ShapeDtypeStruct((total, 4 * wide), bf16),
            jax.ShapeDtypeStruct((4, n_img, seq, col), bf16),
            jax.ShapeDtypeStruct((8, width), f32),
            jax.ShapeDtypeStruct((4, 8, wide), f32),
        ],
        grid_spec=pltpu.PrefetchScalarGridSpec(
            num_scalar_prefetch=1,
            grid=(n_img,),
            in_specs=[
                pl.BlockSpec((1, seq, width), lambda i, s: (s[0] + i, 0, 0)),
                row_block(4 * wide),
                row_block(128),
                row_block(dmix.shape[1]),
                row_block(width),
                whole(vec),
                whole(wq),
            ],
            out_specs=[
                row_block(4 * wide),
                pl.BlockSpec((4, 1, seq, col), lambda i, s: (0, i, 0, 0)),
                pl.BlockSpec((8, width), lambda i, s: (0, 0)),
                pl.BlockSpec((4, 8, wide), lambda i, s: (0, 0, 0)),
            ],
            scratch_shapes=[pltpu.VMEM((rows, width), f32)],
        ),
        compiler_params=pltpu.CompilerParams(vmem_limit_bytes=VMEM_MAX),
        name="back",
    )(where, tokens, qkv, lse, dmix, dres, vec, wq)


def adamw(master, grad, first, second, rate, decay_rate):
    first_new = beta_one * first + (1.0 - beta_one) * grad
    second_new = beta_two * second + (1.0 - beta_two) * grad * grad
    first_hat = first_new / (1.0 - beta_one**adam_step)
    second_hat = second_new / (1.0 - beta_two**adam_step)
    new = master - rate * (first_hat / (jnp.sqrt(second_hat) + adam_eps) + decay_rate * master)
    return (new, first_new, second_new)


def on_device(
    tokens,
    cotangent,
    counts,
    qkv_weight,
    proj_weight,
    expand_weight,
    reduce_weight,
    qv_bias,
    expand_bias,
    vectors,
    first_qkv_weight,
    second_qkv_weight,
    first_proj_weight,
    second_proj_weight,
    first_expand_weight,
    second_expand_weight,
    first_reduce_weight,
    second_reduce_weight,
    first_qv_bias,
    second_qv_bias,
    first_expand_bias,
    second_expand_bias,
    first_vectors,
    second_vectors,
):
    n_dp = lax.axis_size("dp")
    n_t = lax.axis_size("tensor")
    slots, seq, width = tokens.shape
    n_img = slots // n_t
    rows = -(-seq // 16) * 16
    own_d = qkv_weight.shape[0]
    q_width = qkv_weight.shape[2]
    n_heads = q_width // HEAD_DIM
    ff = expand_weight.shape[1]
    qb, eb, vb = qv_bias.shape[1], expand_bias.shape[0], vectors.shape[1]
    wide = -(-3 * q_width // 128) * 128
    pad = wide - 3 * q_width

    shard_q = jnp.concatenate(
        [qkv_weight.reshape(own_d, 3 * q_width), proj_weight.T], axis=1
    ).astype(bf16)
    shard_e = expand_weight.astype(bf16)
    shard_r = reduce_weight.T.astype(bf16)
    n_small = 2 * qb + eb + 6 * vb
    small = jnp.concatenate(
        [qv_bias.reshape(-1), expand_bias, vectors.reshape(-1), jnp.zeros((width - n_small,), f32)]
    )
    shard_s = jnp.zeros((SMALL_ROWS, width), bf16).at[0].set(small.astype(bf16))
    g_s, g_q, g_e, g_r = gather_all([shard_s, shard_q, shard_e, shard_r], n_dp)
    w_q = g_q.reshape(n_t, width, width)
    w_e = g_e.reshape(n_t, width, ff)
    w_r = g_r.reshape(n_t, width, ff)
    got_s = g_s.reshape(n_t, n_dp, SMALL_ROWS, width)[:, :, 0].astype(f32)
    b_qv = got_s[:, :, : 2 * qb].reshape(n_t, n_dp, 2, qb).transpose(0, 2, 1, 3).reshape(n_t, 2, q_width)
    b_exp = got_s[:, :, 2 * qb : 2 * qb + eb].reshape(n_t, 1, ff)
    vec = got_s[0, :, 2 * qb + eb : n_small].reshape(n_dp, 6, vb).transpose(1, 0, 2).reshape(6, width)
    vec = jnp.pad(vec, ((0, 2), (0, 0)))
    bias = jnp.concatenate(
        [b_qv[:, 0], jnp.zeros((n_t, q_width), f32), b_qv[:, 1], jnp.zeros((n_t, pad), f32)], axis=1
    )
    bias = jnp.pad(bias[:, None], ((0, 0), (0, 7), (0, 0)))
    b_exp = jnp.pad(b_exp, ((0, 0), (0, 7), (0, 0)))

    start = lax.axis_index("tensor") * n_img
    where = jnp.stack([start, counts[0]]).astype(jnp.int32)
    a1, qkv, mixp, lse = front(where, tokens, vec, bias, w_q, n_img, rows, n_heads)
    a2, hid, dpre, gh, dres, drh, dmix, out_t, dvec_a, dbexp = middle(
        where, tokens, cotangent, mixp, vec, b_exp, w_q, w_e, w_r, n_img, rows
    )
    dqkv, gt_t, dvec_b, dbias = back(where, tokens, qkv, lse, dmix, dres, vec, w_q, n_img, rows, n_heads)

    output = lax.all_to_all(out_t, "tensor", 0, 0, tiled=True).astype(f32).reshape(slots, seq, -1)
    grad_tokens = lax.all_to_all(gt_t, "tensor", 0, 0, tiled=True).astype(f32).reshape(slots, seq, -1)

    d_r = dot_tn(gh, hid).astype(bf16)
    d_e = dot_tn(a2, dpre).astype(bf16)
    mix = mixp.shape[1] // n_t
    d_q = dot_tn(a1, dqkv).reshape(width, n_t, wide)
    d_p = dot_tn(drh, mixp).reshape(width, n_t, mix)
    d_q = (
        (
            jnp.pad(d_q, ((0, 0), (0, 0), (0, width - wide)))
            + jnp.pad(d_p, ((0, 0), (0, 0), (width - mix, 0)))
        )
        .astype(bf16)
        .reshape(width, n_t * width)
    )
    dvec = jnp.concatenate([dvec_b[0:2], dvec_a[2:6]], axis=0)
    db = dbias[:, 0]
    s_qv = jnp.stack([db[:, :q_width], db[:, 2 * q_width : 3 * q_width]], axis=1)
    s_qv = s_qv.reshape(n_t, 2, n_dp, qb).transpose(2, 0, 1, 3).reshape(n_dp, n_t, 2 * qb)
    s_exp = dbexp[:, 0].reshape(n_t, n_dp, eb).transpose(1, 0, 2)
    s_vec = dvec.reshape(6, n_dp, vb).transpose(1, 0, 2).reshape(n_dp, 1, 6 * vb)
    s_vec = jnp.broadcast_to(s_vec, (n_dp, n_t, 6 * vb))
    d_s = jnp.concatenate([s_qv, s_exp, s_vec, jnp.zeros((n_dp, n_t, width - n_small), f32)], axis=2)
    d_s = jnp.pad(d_s.reshape(n_dp, 1, n_t * width), ((0, 0), (0, SMALL_ROWS - 1), (0, 0)))
    d_s = d_s.reshape(n_dp * SMALL_ROWS, n_t * width).astype(bf16)
    g_s, g_r, g_e, g_q = reduce_all([d_s, d_r, d_e, d_q], [width, ff, ff, width], n_dp)

    g_qkv = g_q[:, : 3 * q_width].reshape(own_d, 3, q_width)
    g_proj = g_q[:, 3 * q_width :].T
    g_expand = g_e
    g_reduce = g_r.T
    g_row = g_s[0]
    g_qvb = g_row[: 2 * qb].reshape(2, qb)
    g_expb = g_row[2 * qb : 2 * qb + eb]
    g_vec = g_row[2 * qb + eb : n_small].reshape(6, vb)

    results = [output, grad_tokens]
    for master, grad, first, second, rate, wd in (
        (qkv_weight, g_qkv, first_qkv_weight, second_qkv_weight, lr_matrix, decay),
        (proj_weight, g_proj, first_proj_weight, second_proj_weight, lr_matrix, decay),
        (expand_weight, g_expand, first_expand_weight, second_expand_weight, lr_matrix, decay),
        (reduce_weight, g_reduce, first_reduce_weight, second_reduce_weight, lr_matrix, decay),
        (qv_bias, g_qvb, first_qv_bias, second_qv_bias, lr_vector, 0.0),
        (expand_bias, g_expb, first_expand_bias, second_expand_bias, lr_vector, 0.0),
        (vectors, g_vec, first_vectors, second_vectors, lr_vector, 0.0),
    ):
        results.append(grad)
        results.extend(adamw(master, grad, first, second, rate, wd))
    return tuple(results)


def solution(mesh):
    matrix = {
        "qkv": P("dp", None, "tensor"),
        "proj": P("tensor", "dp"),
        "expand": P("dp", "tensor"),
        "reduce": P("tensor", "dp"),
        "qvb": P(None, ("tensor", "dp")),
        "expb": P(("tensor", "dp")),
        "vec": P(None, "dp"),
    }
    specs = list(matrix.values())
    in_specs = [P("dp", None, None), P("dp", None, None), P("dp")] + specs
    out_specs = [P("dp", None, "tensor"), P("dp", None, "tensor")]
    for s in specs:
        in_specs += [s, s]
        out_specs += [s, s, s, s]
    return jax.shard_map(
        on_device,
        mesh=mesh,
        in_specs=tuple(in_specs),
        out_specs=tuple(out_specs),
        check_vma=False,
    )
```

time: 1080 us -> 435 us (0.40)
  waiting for transfers between devices: 465 us -> 15.6 us
  Pallas kernels: 0 us -> 286 us
  matrix products: 195 us -> 33.1 us
  blocking collectives: 156 us -> 0 us
  other arithmetic: 124 us -> 32.2 us
  local copies, waits for them, and re-layouts: 116 us -> 55.7 us
  between operations: 18.9 us -> 1.71 us
    pallas_call x0 -> x5, Pallas kernels: none -> 286 us  [the longest x1 94 us: reduce_all(): pl.pallas_call(functools.partial(reduce_body, n_w, n_z, tuple(widths)), o...]
    psum x3 -> x0, waiting for transfers between devices: 274 us -> none  [the longest x1 111 us: on_device(): lax.psum(mlp_part.astype(jnp.bfloat16), 'tensor').astype(jnp.float32)]
    dot_general x18 -> x4, matrix products: 195 us -> 33.1 us  [dot_tn(): lax.dot_general(a, b, (((0,), (0,)), ((), ())), preferred_element_type=f32)]
    reduce_scatter x3 -> x0, waiting for transfers between devices: 126 us -> none  [the longest x1 65 us: on_device(): lax.psum_scatter(d_reduce.astype(jnp.bfloat16), 'dp', scatter_dimension=1...]
    all_gather x4 -> x0, blocking collectives: 117 us -> none  [the longest x1 37 us: on_device(): lax.all_gather(qkv_weight.astype(bf16), 'dp', axis=0, tiled=True)]
    reduce_sum x11 -> x0, other arithmetic: 86.4 us -> none  [the longest x2 17.5 us: layer_norm(): mean = jnp.mean(rows, axis=-1, keepdims=True)]
    reshape x7 -> x13, local copies, waits for them, and re-layouts: 59.7 us -> 13.7 us  [the longest x1 9.95 us: on_device(): d_q = dot_tn(a1, dqkv).reshape(width, n_t, wide)]
    all_gather x2 -> x0, waiting for transfers between devices: 41 us -> none  [the longest x1 41 us: on_device(): lax.all_gather(reduce_weight.astype(bf16), 'dp', axis=1, tiled=True)]
  transfers between devices with their start and end apart: 10 -> 2, of which waited for: 7 -> 1; matrix products, arithmetic and copies ran while one was open for 24% -> 23% of each run, Pallas kernels for 0% -> 22%
where the time goes in v1:
time: 435 us; the launch traced here: 433 us
  Pallas kernels  286 us (66%)
  local copies, waits for them, and re-layouts  55.7 us (13%)
  matrix products  33.1 us (8%)
  other arithmetic  32.2 us (7%)
  waiting for transfers between devices  15.6 us (4%)
  starting transfers between devices  8.21 us (2%)
    pallas_call x1, Pallas kernels, reduce_all(): pl.pallas_call(functools.partial(reduce_body, n_w, n_z, tuple(widths)), o...  94 us
    pallas_call x1, Pallas kernels, gather_all(): pl.pallas_call(functools.partial(gather_body, n_w, n_z), out_shape=[jax.S...  86.5 us
    pallas_call x1, Pallas kernels, back(): pl.pallas_call(functools.partial(back_body, seq, n_heads), out_shape=[jax...  43.1 us
    pallas_call x1, Pallas kernels, middle(): pl.pallas_call(functools.partial(middle_body, seq), out_shape=[jax.ShapeD...  40.5 us
    dot_general x4, matrix products, dot_tn(): lax.dot_general(a, b, (((0,), (0,)), ((), ())), preferred_element_type=f32)  33.1 us
    pallas_call x1, Pallas kernels, front(): pl.pallas_call(functools.partial(front_body, seq, n_heads), out_shape=[ja...  22.3 us
    all_to_all x1, waiting for transfers between devices, on_device(): lax.all_to_all(out_t, 'tensor', 0, 0, tiled=True).astype(f32)  15.6 us
    unnamed x61, local copies, waits for them, and re-layouts  13 us
  transfers between devices with their start and end apart: 2, of which 1 were waited for; matrix products, arithmetic and copies ran while one was open for 23% of the time, Pallas kernels for 22%

profile of v1, /device:TPU:0, one launch (start us, length us, event | category | flops | bytes accessed | tf_op | source)
XLA Modules:
  0.0 432.9 jit_solution(4294620840348347313)
XLA Ops:
  6.0 1.6 convert_bitcast_fusion.refs_3_
  7.6 1.6 convert_element_type.49.refs_2_
  10.0 86.5 %gather_weights.1 = (bf16[2,2,4,2,16,768]{5,4,3,2,1,0:T(8,128)(2,1)}, bf16[2,2,4,2,96,768]{5,4,3,2,1,0:T(8,128)(2,1)}, bf16[2,2,4,2,96,768]{5,4,3,2,1,0:T(8,128)(2,1)}, bf16[2,2,4,2,96,768]{5,4,3,2,1,0:T(8,128)(2,1)}) custom-call(bf16[16,768]{1,0:T(8,128)(2,1)} %scatter.4.refs_0_, bf16[96,768]{1,0:T(8,128)(2,1)} %pad_maximum_fusion.refs_1_, ...), custom_call_target="tpu_custom_call" | custom-call | tf_op jit(solution)/shard_map/gather_weights/pallas_call | solution.py:168
  96.5 1.1 slice.95
  101.5 22.3 %front.1 = (bf16[1040,768]{1,0:T(8,128)(2,1)}, bf16[1040,2560]{1,0:T(8,128)(2,1)}, bf16[1040,1024]{1,0:T(8,128)(2,1)}, f32[1040,128]{1,0:T(8,128)}) custom-call(s32[2]{0:T(128)} %pad_add_fusion.where, f32[20,197,768]{2,1,0:T(8,128)} %x_ref.5, f32[8,768]{1,0:T(8,128)} %pad.28.vec_ref, f32[4,8,640]{2,1,0:T(8,128)} %pad.29.bias_ref, bf16[4,768,768]{2,1,0:T(8,128)(2,1)} %bitcast.71), custom_call_target="tpu_custom_call" | custom-call | tf_op jit(solution)/shard_map/front/pallas_call | solution.py:343
  123.8 40.5 %middle.1 = (bf16[1040,768]{1,0:T(8,128)(2,1)}, bf16[1040,3072]{1,0:T(8,128)(2,1)}, bf16[1040,3072]{1,0:T(8,128)(2,1)}, bf16[1040,768]{1,0:T(8,128)(2,1)}, f32[1...) custom-call(s32[2]{0:T(128)} %pad_add_fusion.where, ...), custom_call_target="tpu_custom_call" | custom-call | tf_op jit(solution)/shard_map/middle/pallas_call | solution.py:460
  164.3 43.1 %back.1 = (bf16[1040,2560]{1,0:T(8,128)(2,1)}, bf16[4,5,197,192]{3,2,1,0:T(8,128)(2,1)}, f32[8,768]{1,0:T(8,128)}, f32[4,8,640]{2,1,0:T(8,128)}) custom-call(s32[2]{0:T(128)} %pad_add_fusion.where, f32[20,197,768]{2,1,0:T(8,128)} %x_ref.5, bf16[1040,2560]{1,0:T(8,128)(2,1)} %get-tuple-element.74.qkv_ref, f32[1040,128]{1,0:T(8,128)} %get-tuple-element.75.lse_ref, ...), custom_call_target="tpu_custom_call" | custom-call | tf_op jit(solution)/shard_map/back/pallas_call | solution.py:570
  207.5 4.4 %copy.111 = bf16[4,5,197,192]{2,3,1,0:T(8,128)(2,1)} copy(bf16[4,5,197,192]{3,2,1,0:T(8,128)(2,1)} %get-tuple-element.78) | data formatting | bytes 3025920 | tf_op jit(solution)/shard_map/back/pallas_call | solution.py:570
  211.8 4.4 %all-to-all-start.1 = ((bf16[4,5,197,192]{2,3,1,0:T(8,128)(2,1)}), bf16[4,5,197,192]{2,3,1,0:T(8,128)(2,1)}, u32[]{:S(2)}, u32[]{:S(2)}) async-start(bf16[4,5,197,192]{2,3,1,0:T(8,128)(2,1)} %copy.111), calls=%async_computation.1 | async-start | bytes 3932160 | tf_op jit(solution)/shard_map/all_to_all | solution.py:685
  216.5 9.9 %fusion.17 = f32[768,2560]{1,0:T(8,128)} fusion(bf16[1040,768]{1,0:T(8,128)(2,1)S(1)} %copy-done.19, bf16[1040,2560]{1,0:T(8,128)(2,1)} %get-tuple-element.88), kind=kOutput, calls=%fused_computation.58 | convolution fusion | flops 4089446400 | bytes 14786560 | tf_op jit(solution)/shard_map/dot_general | solution.py:35
  226.4 10.0 %reshape.237 = f32[768,4,640]{2,1,0:T(4,128)} reshape(f32[768,2560]{1,0:T(8,128)} %fusion.17) | data formatting | bytes 15728640 | tf_op jit(solution)/shard_map/reshape | solution.py:690
  236.3 4.3 fusion.18
  240.7 2.9 reshape.238
  243.6 8.1 %add_convert_fusion = bf16[768,4,768]{2,1,0:T(4,128)(2,1)} fusion(f32[768,4,256]{2,1,0:T(4,128)} %reshape.238, f32[768,4,640]{2,1,0:T(4,128)} %reshape.237), kind=kLoop, calls=%fused_computation | loop fusion | flops 4718592 | bytes 15728640 | tf_op jit(solution)/shard_map/convert_element_type | solution.py:697
  251.7 9.3 %reshape_reshape.3.refs_3_ = bf16[4,2,96,3072]{3,2,1,0:T(8,128)(2,1)} reshape(bf16[768,4,768]{2,1,0:T(4,128)(2,1)} %add_convert_fusion) | data formatting | bytes 9437184 | tf_op jit(solution)/shard_map/reshape;reshape | solution.py:271
  264.0 1.1 fusion.5
  266.3 10.5 %convolution_convert_fusion = bf16[768,3072]{1,0:T(8,128)(2,1)} fusion(bf16[1040,768]{1,0:T(8,128)(2,1)} %get-tuple-element.85, bf16[1040,3072]{1,0:T(8,128)(2,1)} %get-tuple-element.86), kind=kOutput, calls=%fused_computation.1 | convolution fusion | flops 4909694976 | bytes 12705792 | tf_op jit(solution)/shard_map/dot_general | solution.py:35
  276.8 8.3 %convolution_convert_fusion.1 = bf16[768,3072]{1,0:T(8,128)(2,1)} fusion(bf16[1040,768]{1,0:T(8,128)(2,1)S(1)} %copy-done.18, bf16[1040,3072]{1,0:T(8,128)(2,1)S(1)} %bitcast.90), kind=kOutput, calls=%fused_computation.2 | convolution fusion | flops 4909694976 | bytes 12705792 | tf_op jit(solution)/shard_map/dot_general | solution.py:35
  285.1 94.0 %reduce_grads.1 = (f32[16,768]{1,0:T(8,128)}, f32[96,768]{1,0:T(8,128)}, f32[96,768]{1,0:T(8,128)}, f32[96,768]{1,0:T(8,128)}) custom-call(bf16[4,2,16,3072]{3,2,1,0:T(8,128)(2,1)} %bitcast.78, bf16[4,2,96,3072]{3,2,1,0:T(8,128)(2,1)} %bitcast.75, bf16[4,2,96,3072]{3,2,1,0:T(8,128)(2,1)} %bitcast.74, bf16[4,2,96,3072]{3,2,1,0:T(8,128)(2,1)} %reshape_reshape.3.refs_3_), custom_call_target="tpu_custom_call" | custom-call | tf_op jit(solution)/shard_map/reduce_grads/pallas_call | solution.py:281
  379.2 1.0 slice.89
  381.2 1.8 copy.120
  383.9 2.0 multiply_subtract_fusion.2
  385.9 1.9 copy.128
  389.7 1.0 multiply_subtract_fusion.3
  396.5 2.4 copy.110
  398.9 1.4 multiply_subtract_fusion.6
  400.9 3.8 all-to-all-start
  405.3 2.0 multiply_subtract_fusion.1
  407.3 2.1 multiply_subtract_fusion
  409.4 3.9 bitcast_convert_fusion
  413.3 15.6 %all-to-all-done = bf16[4,5,197,192]{2,3,1,0:T(8,128)(2,1)S(1)} async-done(((bf16[4,5,197,192]{2,3,1,0:T(8,128)(2,1)}), bf16[4,5,197,192]{2,3,1,0:T(8,128)(2,1)S(1)}, u32[]{:S(2)}, u32[]{:S(2)}) %all-to-all-start) | async-done | bytes 1512992 | tf_op jit(solution)/shard_map/all_to_all | solution.py:684
  429.0 2.5 bitcast_convert_fusion.1
  (124 shorter events, 25.7 us)
Async XLA Ops:
  207.4 8.9 %copy-start.1 = (f32[96,3,192]{2,0,1:T(8,128)S(1)}, f32[96,3,192]{2,0,1:T(8,128)}, u32[]{:S(2)}) copy-start(f32[96,3,192]{2,0,1:T(8,128)} %param.29) | copy-start | bytes 663556
  207.4 9.0 %copy-start.19 = (bf16[1040,768]{1,0:T(8,128)(2,1)S(1)}, bf16[1040,768]{1,0:T(8,128)(2,1)}, u32[]{:S(2)}) copy-start(bf16[1040,768]{1,0:T(8,128)(2,1)} %get-tuple-element.87) | copy-start | bytes 4792324
  211.8 189.1 %all-to-all-start.1 = ((bf16[4,5,197,192]{2,3,1,0:T(8,128)(2,1)}), bf16[4,5,197,192]{2,3,1,0:T(8,128)(2,1)}, u32[]{:S(2)}, u32[]{:S(2)}) async-start(bf16[4,5,197,192]{2,3,1,0:T(8,128)(2,1)} %copy.111), calls=%async_computation.1 | async-start | bytes 3932160 | tf_op jit(solution)/shard_map/all_to_all | solution.py:685
  263.9 12.9 %slice-start = ((s8[6389760]{0:T(1024)(128)(4,1)}), s8[2195456]{0:T(1024)(128)(4,1)S(1)}, s32[]{:S(2)}) async-start(s8[6389760]{0:T(1024)(128)(4,1)} %bitcast.89), calls=%async_computation.2 | async-start | bytes 4390912
  266.3 10.5 %slice-start.1 = ((s8[6389760]{0:T(1024)(128)(4,1)}), s8[4194304]{0:T(1024)(128)(4,1)S(1)}, s32[]{:S(2)}) async-start(s8[6389760]{0:T(1024)(128)(4,1)} %bitcast.89), calls=%async_computation.3 | async-start | bytes 8388608
  266.3 10.5 %copy-start.18 = (bf16[1040,768]{1,0:T(8,128)(2,1)S(1)}, bf16[1040,768]{1,0:T(8,128)(2,1)}, u32[]{:S(2)}) copy-start(bf16[1040,768]{1,0:T(8,128)(2,1)} %get-tuple-element.83) | copy-start | bytes 4792324
  285.1 95.2 %copy-start.6 = (f32[96,3,192]{2,0,1:T(8,128)S(1)}, f32[96,3,192]{2,0,1:T(8,128)}, u32[]{:S(2)}) copy-start(f32[96,3,192]{2,0,1:T(8,128)} %param.36) | copy-start | bytes 663556
  379.1 10.4 %copy-start.8 = (f32[192,96]{1,0:T(8,128)S(1)}, f32[192,96]{1,0:T(8,128)}, u32[]{:S(2)}) copy-start(f32[192,96]{1,0:T(8,128)} %param.38) | copy-start | bytes 221188
  379.1 10.5 %copy-start.9 = (f32[192,96]{1,0:T(8,128)S(1)}, f32[192,96]{1,0:T(8,128)}, u32[]{:S(2)}) copy-start(f32[192,96]{1,0:T(8,128)} %param.39) | copy-start | bytes 221188
  380.3 16.1 %copy-start = (bf16[4,5,197,192]{3,2,1,0:T(8,128)(2,1)S(1)}, bf16[4,5,197,192]{3,2,1,0:T(8,128)(2,1)}, u32[]{:S(2)}) copy-start(bf16[4,5,197,192]{3,2,1,0:T(8,128)(2,1)} %get-tuple-element.73) | copy-start | bytes 4538884
  385.9 14.4 %copy-start.10 = (f32[6,96]{1,0:T(8,128)S(1)}, f32[6,96]{1,0:T(8,128)}, u32[]{:S(2)}) copy-start(f32[6,96]{1,0:T(8,128)} %param.35) | copy-start | bytes 6916
  385.9 14.4 %copy-start.12 = (f32[6,96]{1,0:T(8,128)S(1)}, f32[6,96]{1,0:T(8,128)}, u32[]{:S(2)}) copy-start(f32[6,96]{1,0:T(8,128)} %param.48) | copy-start | bytes 6916
  385.9 14.4 %copy-start.13 = (f32[6,96]{1,0:T(8,128)S(1)}, f32[6,96]{1,0:T(8,128)}, u32[]{:S(2)}) copy-start(f32[6,96]{1,0:T(8,128)} %param.49) | copy-start | bytes 6916
  395.6 5.3 %copy-start.11 = (f32[6,96]{1,0:T(8,128)}, f32[6,96]{1,0:T(8,128)S(1)}, u32[]{:S(2)}) copy-start(f32[6,96]{1,0:T(8,128)S(1)} %reshape.241) | copy-start | bytes 6916
  396.4 8.3 %copy-start.17 = (f32[2,24]{1,0:T(2,128)}, f32[2,24]{1,0:T(2,128)S(1)}, u32[]{:S(2)}) copy-start(f32[2,24]{1,0:T(2,128)S(1)} %reshape.240) | copy-start | bytes 580
  396.4 8.3 %copy-start.14 = (f32[2,24]{1,0:T(2,128)S(1)}, f32[2,24]{1,0:T(2,128)}, u32[]{:S(2)}) copy-start(f32[2,24]{1,0:T(2,128)} %param.33) | copy-start | bytes 580
  396.4 8.3 %copy-start.15 = (f32[2,24]{1,0:T(2,128)S(1)}, f32[2,24]{1,0:T(2,128)}, u32[]{:S(2)}) copy-start(f32[2,24]{1,0:T(2,128)} %param.44) | copy-start | bytes 580
  396.4 8.3 %copy-start.16 = (f32[2,24]{1,0:T(2,128)S(1)}, f32[2,24]{1,0:T(2,128)}, u32[]{:S(2)}) copy-start(f32[2,24]{1,0:T(2,128)} %param.45) | copy-start | bytes 580
  396.4 8.9 %copy-start.2 = (f32[96,768]{1,0:T(8,128)S(1)}, f32[96,768]{1,0:T(8,128)}, u32[]{:S(2)}) copy-start(f32[96,768]{1,0:T(8,128)} %param.31) | copy-start | bytes 884740
  396.4 8.9 %copy-start.5 = (f32[96,768]{1,0:T(8,128)S(1)}, f32[96,768]{1,0:T(8,128)}, u32[]{:S(2)}) copy-start(f32[96,768]{1,0:T(8,128)} %get-tuple-element.250) | copy-start | bytes 884740
  396.5 8.9 %copy-start.7 = (f32[96,768]{1,0:T(8,128)S(1)}, f32[96,768]{1,0:T(8,128)}, u32[]{:S(2)}) copy-start(f32[96,768]{1,0:T(8,128)} %param.40) | copy-start | bytes 884740
  398.9 8.4 %copy-start.3 = (f32[768,96]{0,1:T(8,128)S(1)}, f32[768,96]{0,1:T(8,128)}, u32[]{:S(2)}) copy-start(f32[768,96]{0,1:T(8,128)} %param.32) | copy-start | bytes 884740
  398.9 8.4 %copy-start.4 = (f32[96,768]{1,0:T(8,128)S(1)}, f32[96,768]{1,0:T(8,128)}, u32[]{:S(2)}) copy-start(f32[96,768]{1,0:T(8,128)} %get-tuple-element.92) | copy-start | bytes 884740
  400.9 28.0 %all-to-all-start = ((bf16[4,5,197,192]{2,3,1,0:T(8,128)(2,1)}), bf16[4,5,197,192]{2,3,1,0:T(8,128)(2,1)S(1)}, u32[]{:S(2)}, u32[]{:S(2)}) async-start(bf16[4,5,197,192]{2,3,1,0:T(8,128)(2,1)} %copy.110), calls=%async_computation | async-start | bytes 3932160 | tf_op jit(solution)/shard_map/all_to_all | solution.py:684

commit v2 on v1

--- a/solution.py
+++ b/solution.py
@@ -182,115 +182,6 @@
     )(*shards)
 
 
-def reduce_body(n_w, n_z, widths, *refs):
-    grads, outs = refs[:n_w], refs[n_w : 2 * n_w]
-    acc, got = refs[2 * n_w : 3 * n_w], refs[3 * n_w : 4 * n_w]
-    got2, got1, gotz = refs[4 * n_w : 5 * n_w], refs[5 * n_w : 6 * n_w], refs[6 * n_w : 7 * n_w]
-    local_sem, c_send, c_recv, s_send, s_recv, z_send, z_recv = refs[7 * n_w :]
-    z, x, y, c, first, second, sibling, sets, along_z = places(n_z)
-    greet([first, second, sibling] + along_z)
-    swap = (0, 2, 1, 3)
-
-    def part(w, which, core):
-        sy, sx = sets[which]
-        lanes = pl.ds(pl.multiple_of((sy * 2 + core) * widths[w], 128), widths[w])
-        return grads[w].at[:, sx, :, lanes]
-
-    def mine(w, k):
-        return pltpu.make_async_copy(part(w, k, c), acc[w].at[k], local_sem.at[w, k])
-
-    def to_sibling(w, k):
-        s = swap[k]
-        return push(part(w, k, 1 - c), got[w].at[s], c_send.at[w, s], c_recv.at[w, s], sibling)
-
-    def to_second(w, k):
-        return push(acc[w].at[k], got2[w].at[k - 2], s_send.at[w, k - 2], s_recv.at[w, k - 2], second)
-
-    def to_first(w):
-        return push(acc[w].at[1], got1[w], s_send.at[w, 2], s_recv.at[w, 2], first)
-
-    def to_z(w, k):
-        return push(
-            acc[w].at[0, along_z[k][0] // 2], gotz[w].at[k], z_send.at[w, k], z_recv.at[w, k], along_z[k]
-        )
-
-    def add(w, k, other):
-        def one(i, carry):
-            acc[w][k, i] = (acc[w][k, i].astype(f32) + other(i).astype(f32)).astype(bf16)
-            return carry
-
-        lax.fori_loop(0, n_z, one, 0)
-
-    for w in range(n_w):
-        for k in (3, 1, 2, 0):
-            to_sibling(w, k).start()
-        for k in (3, 2, 1, 0):
-            mine(w, k).start()
-    for step in range(n_w + 3):
-        w = step
-        if 0 <= w < n_w:
-            for k in (3, 2, 1, 0):
-                mine(w, k).wait()
-                to_sibling(w, swap[k]).wait_recv()
-                add(w, k, lambda i, k=k: got[w][k, i])
-                if k >= 2:
-                    to_second(w, k).start()
-        w = step - 1
-        if 0 <= w < n_w:
-            to_second(w, 3).wait_recv()
-            add(w, 1, lambda i: got2[w][1, i])
-            to_first(w).start()
-            to_second(w, 2).wait_recv()
-            add(w, 0, lambda i: got2[w][0, i])
-        w = step - 2
-        if 0 <= w < n_w:
-            to_first(w).wait_recv()
-            add(w, 0, lambda i: got1[w][i])
-            for k in range(n_z - 1):
-                to_z(w, k).start()
-        w = step - 3
-        if 0 <= w < n_w:
-            total = acc[w][0, z].astype(f32)
-            for k in range(n_z - 1):
-                to_z(w, k).wait_recv()
-                total = total + gotz[w][k].astype(f32)
-            outs[w][...] = total
-    for w in range(n_w):
-        for k in range(4):
-            to_sibling(w, k).wait_send()
-        to_second(w, 2).wait_send()
-        to_second(w, 3).wait_send()
-        to_first(w).wait_send()
-        for k in range(n_z - 1):
-            to_z(w, k).wait_send()
-
-
-def reduce_all(grads, widths, n_dp):
-    n_w, n_z = len(grads), n_dp // 2
-    rows = [g.shape[0] // n_dp for g in grads]
-    shaped = [g.reshape(n_z, 2, r, g.shape[1]) for g, r in zip(grads, rows)]
-    blocks = list(zip(rows, widths))
-    scratch = [pltpu.VMEM((4, n_z) + b, bf16) for b in blocks]
-    scratch += [pltpu.VMEM((4, n_z) + b, bf16) for b in blocks]
-    scratch += [pltpu.VMEM((2, n_z) + b, bf16) for b in blocks]
-    scratch += [pltpu.VMEM((n_z,) + b, bf16) for b in blocks]
-    scratch += [pltpu.VMEM((n_z - 1,) + b, bf16) for b in blocks]
-    scratch += [pltpu.SemaphoreType.DMA((n_w, 4))] * 3
-    scratch += [pltpu.SemaphoreType.DMA((n_w, 3))] * 2
-    scratch += [pltpu.SemaphoreType.DMA((n_w, n_z - 1))] * 2
-    return pl.pallas_call(
-        functools.partial(reduce_body, n_w, n_z, tuple(widths)),
-        out_shape=[jax.ShapeDtypeStruct(b, f32) for b in blocks],
-        in_specs=[pl.BlockSpec(memory_space=pl.ANY)] * n_w,
-        out_specs=[pl.BlockSpec(memory_space=pltpu.VMEM)] * n_w,
-        scratch_shapes=scratch,
-        compiler_params=pltpu.CompilerParams(
-            collective_id=1, has_side_effects=True, vmem_limit_bytes=VMEM_MAX
-        ),
-        name="reduce_grads",
-    )(*shaped)
-
-
 def key_mask(rows, seq):
     return lax.broadcasted_iota(jnp.int32, (rows, rows), 1) < seq
 
@@ -299,7 +190,7 @@
     dst[pl.ds(0, seq), :] = src[0]
 
 
-def front_body(seq, n_heads, where, x_ref, vec_ref, bias_ref, wq_ref, a1_ref, qkv_ref, mix_ref, lse_ref, xs):
+def front_body(seq, n_heads, where, x_ref, vec_ref, bias_ref, wq_ref, a1_ref, n1_ref, qkv_ref, mix_ref, lse_ref, xs):
     rows = xs.shape[0]
 
     @pl.when(pl.program_id(0) == 0)
@@ -307,12 +198,13 @@
         xs[...] = jnp.zeros_like(xs)
 
     load_rows(x_ref, xs, seq)
-    normed, unused = norm_stats(xs[...])
+    normed, scale = norm_stats(xs[...])
+    n1_ref[...] = normed
     a1 = (normed * vec_ref[0:1, :] + vec_ref[1:2, :]).astype(bf16)
     a1_ref[...] = a1
     mask = key_mask(rows, seq)
     lane = lax.broadcasted_iota(jnp.int32, (rows, 128), 1)
-    lse_ref[...] = jnp.zeros_like(lse_ref)
+    lse_ref[...] = jnp.where(lane == 127, scale, 0.0)
     q_width = n_heads * HEAD_DIM
     wide = bias_ref.shape[2]
     pad = mix_ref.shape[1] // 4 - q_width
@@ -344,6 +236,7 @@
         functools.partial(front_body, seq, n_heads),
         out_shape=[
             jax.ShapeDtypeStruct((total, width), bf16),
+            jax.ShapeDtypeStruct((total, width), f32),
             jax.ShapeDtypeStruct((total, 4 * wide), bf16),
             jax.ShapeDtypeStruct((total, 4 * mix), bf16),
             jax.ShapeDtypeStruct((total, 128), f32),
@@ -359,6 +252,7 @@
             ],
             out_specs=[
                 pl.BlockSpec((rows, width), lambda i, s: (i, 0)),
+                pl.BlockSpec((rows, width), lambda i, s: (i, 0)),
                 pl.BlockSpec((rows, 4 * wide), lambda i, s: (i, 0)),
                 pl.BlockSpec((rows, 4 * mix), lambda i, s: (i, 0)),
                 pl.BlockSpec((rows, 128), lambda i, s: (i, 0)),
@@ -382,8 +276,7 @@
     we_ref,
     wr_ref,
     a2_ref,
-    hid_ref,
-    dpre_ref,
+    hd_ref,
     gh_ref,
     dres_ref,
     drh_ref,
@@ -423,16 +316,16 @@
         cdf = 0.5 + 0.5 * lax.erf(pre * (0.5**0.5))
         hid = (pre * cdf).astype(bf16)
         slope = cdf + pre * jnp.exp(-0.5 * pre * pre) * ((2.0 * jnp.pi) ** -0.5)
-        hid_ref[:, t * ff : (t + 1) * ff] = hid
+        hd_ref[:, t * ff : (t + 1) * ff] = hid
         d_pre = dot_nn(gh_ref[...], wr_ref[t]) * slope
         dbexp_ref[t, 0:1, :] += jnp.sum(d_pre, axis=0, keepdims=True)
         dph = d_pre.astype(bf16)
-        dpre_ref[:, t * ff : (t + 1) * ff] = dph
+        hd_ref[:, (4 + t) * ff : (5 + t) * ff] = dph
         feed += half_round(dot_nt(hid, wr_ref[t]))
         d_a2 += half_round(dot_nt(dph, we_ref[t]))
     out = (resid + feed + vec_ref[5:6, :]) * live
-    col = width // 4
-    for t in range(4):
+    col = width // 2
+    for t in range(2):
         out_ref[t, 0] = out[:seq, t * col : (t + 1) * col].astype(bf16)
     d_resid = gs[...] + norm_back(d_a2, normed2, scale2, vec_ref[3:4, :])
     dres_ref[...] = d_resid
@@ -451,7 +344,7 @@
     ff = we.shape[2]
     mix = mixp.shape[1]
     total = n_img * rows
-    col = width // 4
+    col = width // 2
     row_block = lambda n: pl.BlockSpec((rows, n), lambda i, s: (i, 0))
     whole = lambda a: pl.BlockSpec(
         a.shape, lambda i, s, nd=len(a.shape): (0,) * nd, pipeline_mode=pl.Buffered(1)
@@ -461,13 +354,12 @@
         functools.partial(middle_body, seq),
         out_shape=[
             jax.ShapeDtypeStruct((total, width), bf16),
-            jax.ShapeDtypeStruct((total, 4 * ff), bf16),
-            jax.ShapeDtypeStruct((total, 4 * ff), bf16),
+            jax.ShapeDtypeStruct((total, 8 * ff), bf16),
             jax.ShapeDtypeStruct((total, width), bf16),
             jax.ShapeDtypeStruct((total, width), f32),
             jax.ShapeDtypeStruct((total, width), bf16),
             jax.ShapeDtypeStruct((total, mix), bf16),
-            jax.ShapeDtypeStruct((4, n_img, seq, col), bf16),
+            jax.ShapeDtypeStruct((2, n_img, seq, col), bf16),
             jax.ShapeDtypeStruct((8, width), f32),
             jax.ShapeDtypeStruct((4, 8, ff), f32),
         ],
@@ -477,13 +369,12 @@
             in_specs=[image, image, row_block(mix)] + [whole(a) for a in (vec, bexp, wq, we, wr)],
             out_specs=[
                 row_block(width),
-                row_block(4 * ff),
-                row_block(4 * ff),
+                row_block(8 * ff),
                 row_block(width),
                 row_block(width),
                 row_block(width),
                 row_block(mix),
-                pl.BlockSpec((4, 1, seq, col), lambda i, s: (0, i, 0, 0)),
+                pl.BlockSpec((2, 1, seq, col), lambda i, s: (0, i, 0, 0)),
                 pl.BlockSpec((8, width), lambda i, s: (0, 0)),
                 pl.BlockSpec((4, 8, ff), lambda i, s: (0, 0, 0)),
             ],
@@ -494,110 +385,440 @@
     )(where, tokens, cotangent, mixp, vec, bexp, wq, we, wr)
 
 
-def back_body(
-    seq,
-    n_heads,
-    where,
-    x_ref,
-    qkv_ref,
-    lse_ref,
-    dmix_ref,
-    dres_ref,
-    vec_ref,
-    wq_ref,
-    dqkv_ref,
-    gt_ref,
-    dvec_ref,
-    dbias_ref,
-    xs,
-):
-    i = pl.program_id(0)
-
-    @pl.when(i == 0)
-    def _():
-        xs[...] = jnp.zeros_like(xs)
-        dvec_ref[...] = jnp.zeros_like(dvec_ref)
-        dbias_ref[...] = jnp.zeros_like(dbias_ref)
-
-    load_rows(x_ref, xs, seq)
-    rows, width = xs.shape
+S_ROWS = 24
+
+
+def attention_back(seq, n_heads, qkv_ref, lse_ref, dmix_ref, t, wide, mix):
+    rows = qkv_ref.shape[0]
+    q_width = n_heads * HEAD_DIM
+    scale_qk = HEAD_DIM**-0.5
     mask = key_mask(rows, seq)
-    q_width = n_heads * HEAD_DIM
-    wide = qkv_ref.shape[1] // 4
-    mix = dmix_ref.shape[1] // 4
-    scale_qk = HEAD_DIM**-0.5
-    d_a1 = jnp.zeros((rows, width), f32)
-    for t in range(4):
-        dq, dk, dv = [], [], []
-        for h in range(n_heads):
-            at = t * wide + h * HEAD_DIM
-            q = qkv_ref[:, at : at + HEAD_DIM]
-            k = qkv_ref[:, at + q_width : at + q_width + HEAD_DIM]
-            v = qkv_ref[:, at + 2 * q_width : at + 2 * q_width + HEAD_DIM]
-            m_at = (t + 1) * mix - q_width + h * HEAD_DIM
-            dm = dmix_ref[:, m_at : m_at + HEAD_DIM]
-            lse = lse_ref[:, t * n_heads + h : t * n_heads + h + 1]
-            p = jnp.where(mask, jnp.exp(dot_nt(q, k) * scale_qk - lse), 0.0)
-            dv.append(dot_tn(p.astype(bf16), dm))
-            d_p = dot_nt(dm, v)
-            delta = jnp.sum(p * d_p, axis=-1, keepdims=True)
-            ds = (p * (d_p - delta) * scale_qk).astype(bf16)
-            dq.append(dot_nn(ds, k))
-            dk.append(dot_tn(ds, q))
-        d_all = jnp.concatenate(dq + dk + dv + [jnp.zeros((rows, wide - 3 * q_width), f32)], axis=1)
-        dbias_ref[t, 0:1, :] += jnp.sum(d_all, axis=0, keepdims=True)
-        d_half = d_all.astype(bf16)
-        dqkv_ref[:, t * wide : (t + 1) * wide] = d_half
-        d_a1 += half_round(dot_nt(d_half, wq_ref[t, :, :wide]))
-    normed, scale = norm_stats(xs[...])
-    grad = dres_ref[...] + norm_back(d_a1, normed, scale, vec_ref[0:1, :])
-    col = width // 4
-    for t in range(4):
-        gt_ref[t, 0] = grad[:seq, t * col : (t + 1) * col].astype(bf16)
-    dvec_ref[0:1, :] += jnp.sum(d_a1 * normed, axis=0, keepdims=True)
-    dvec_ref[1:2, :] += jnp.sum(d_a1, axis=0, keepdims=True)
-
-
-def back(where, tokens, qkv, lse, dmix, dres, vec, wq, n_img, rows, n_heads):
-    slots, seq, width = tokens.shape
-    total = n_img * rows
-    wide = qkv.shape[1] // 4
-    col = width // 4
-    row_block = lambda n: pl.BlockSpec((rows, n), lambda i, s: (i, 0))
+    dq, dk, dv = [], [], []
+    for h in range(n_heads):
+        at = t * wide + h * HEAD_DIM
+        q = qkv_ref[:, at : at + HEAD_DIM]
+        k = qkv_ref[:, at + q_width : at + q_width + HEAD_DIM]
+        v = qkv_ref[:, at + 2 * q_width : at + 2 * q_width + HEAD_DIM]
+        m_at = (t + 1) * mix - q_width + h * HEAD_DIM
+        dm = dmix_ref[:, m_at : m_at + HEAD_DIM]
+        lse = lse_ref[:, t * n_heads + h : t * n_heads + h + 1]
+        p = jnp.where(mask, jnp.exp(dot_nt(q, k) * scale_qk - lse), 0.0)
+        dv.append(dot_tn(p.astype(bf16), dm))
+        d_p = dot_nt(dm, v)
+        delta = jnp.sum(p * d_p, axis=-1, keepdims=True)
+        ds = (p * (d_p - delta) * scale_qk).astype(bf16)
+        dq.append(dot_nn(ds, k))
+        dk.append(dot_tn(ds, q))
+    return jnp.concatenate(dq + dk + dv + [jnp.zeros((rows, wide - 3 * q_width), f32)], axis=1)
+
+
+def rear_body(cfg, *refs):
+    n_z, n_img, seq, rows, n_heads, shard_rows, wide, mix, ff = cfg
+    (hd_ref, mix_ref, qkv_ref, lse_ref, dmix_ref, dres_ref, n1_ref, vec_ref, wq_ref, dvec_in, dbexp_in) = refs[:11]
+    gh_any, a2_any, a1_any, drh_any, out2_any = refs[11:16]
+    gr_out, ge_out, gq_out, gs_out, ro_out, rg_out = refs[16:22]
+    (lhs_a, lhs_b, dqs, gts) = refs[22:26]
+    part, got, got2, got1, gotz = (refs[26 + 3 * k : 29 + 3 * k] for k in range(5))
+    sv, sgot, sz = refs[41:44]
+    (
+        lhs_sem,
+        load_sem,
+        keep_sem,
+        o_send,
+        o_recv,
+        g_send,
+        g_recv,
+        f_send,
+        f_recv,
+        h_send,
+        h_recv,
+        s_send,
+        s_recv,
+        z_send,
+        z_recv,
+        v_send,
+        v_recv,
+        vz_send,
+        vz_recv,
+    ) = refs[44:]
+    outs = (gr_out, ge_out, gq_out)
+    s = pl.program_id(0)
+    n_t = 4
+    base_e, base_b = n_t, 2 * n_t
+    base_q = base_b + n_img
+    base_t = base_q + n_t
+    width = n1_ref.shape[1]
+    n_dp = 2 * n_z
+
+    dp = lax.axis_index("dp")
+    t_me = lax.axis_index("tensor")
+    z, x = dp // 2, dp % 2
+    y, c = t_me // 2, t_me % 2
+    fy, fx = 1 - 2 * y, 1 - 2 * x
+    sibling = (dp, t_me + 1 - 2 * c)
+    over_y = (dp, t_me + 2 * fy)
+    over_x = (dp + fx, t_me)
+    along_z = [(lax.rem(z + k, n_z) * 2 + x, t_me) for k in range(1, n_z)]
+
+    def route(w):
+        m = c if w == 2 else 0 * c
+        first = (dp + m * fx, t_me + (1 - m) * 2 * fy)
+        second = (dp + (1 - m) * fx, t_me + m * 2 * fy)
+        sets = (
+            (y, x),
+            (y + (1 - m) * fy, x + m * fx),
+            (y + m * fy, x + (1 - m) * fx),
+            (1 - y, 1 - x),
+        )
+        return first, second, sets
+
+    def half(w, yy):
+        return push(part[w].at[1 - c, yy], got[w].at[yy], h_send.at[w, yy], h_recv.at[w, yy], sibling)
+
+    def to_second(w, k):
+        first, second, sets = route(w)
+        sy, sx = sets[k]
+        return push(
+            part[w].at[c, sy, sx], got2[w].at[k - 2], s_send.at[w, k - 2], s_recv.at[w, k - 2], second
+        )
+
+    def to_first(w):
+        first, second, sets = route(w)
+        sy, sx = sets[1]
+        return push(part[w].at[c, sy, sx], got1[w], s_send.at[w, 2], s_recv.at[w, 2], first)
+
+    def to_z(w, k):
+        return push(
+            part[w].at[c, y, x, along_z[k][0] // 2],
+            gotz[w].at[k],
+            z_send.at[w, k],
+            z_recv.at[w, k],
+            along_z[k],
+        )
+
+    def add(w, k, other):
+        sy, sx = route(w)[2][k]
+
+        def one(i, carry):
+            mine = part[w][c, sy, sx, i].astype(f32)
+            part[w][c, sy, sx, i] = (mine + other(sy, sx, i).astype(f32)).astype(bf16)
+            return carry
+
+        lax.fori_loop(0, n_z, one, 0)
+
+    def stage_b(w):
+        half(w, 0).wait_recv()
+        half(w, 1).wait_recv()
+        for k in (3, 2, 1, 0):
+            add(w, k, lambda sy, sx, i: got[w][sy, sx, i])
+            if k >= 2:
+                to_second(w, k).start()
+
+    def stage_c(w):
+        to_second(w, 3).wait_recv()
+        add(w, 1, lambda sy, sx, i: got2[w][1, i])
+        to_first(w).start()
+        to_second(w, 2).wait_recv()
+        add(w, 0, lambda sy, sx, i: got2[w][0, i])
+
+    def stage_d(w):
+        to_first(w).wait_recv()
+        add(w, 0, lambda sy, sx, i: got1[w][i])
+        for k in range(n_z - 1):
+            to_z(w, k).start()
+
+    def stage_f(w):
+        total = part[w][c, y, x, z].astype(f32)
+        for k in range(n_z - 1):
+            to_z(w, k).wait_recv()
+            total = total + gotz[w][k].astype(f32)
+        outs[w][...] = total
+
+    def small(k):
+        peer = (sibling, over_x, over_y)[k]
+        return push(sv.at[k], sgot.at[k], v_send.at[k], v_recv.at[k], peer)
+
+    def small_step(k):
+        small(k).wait_recv()
+        sv[k + 1] = sv[k] + sgot[k]
+        if k < 2:
+            small(k + 1).start()
+        else:
+            sz[z] = sv[3]
+            for j in range(n_z - 1):
+                small_z(j).start()
+
+    def small_z(j):
+        return push(sv.at[3], sz.at[z], vz_send.at[j], vz_recv.at[j], along_z[j])
+
+    def small_end():
+        for j in range(n_z - 1):
+            small_z(j).wait_recv()
+        total = sz[0]
+        for j in range(1, n_z):
+            total = total + sz[j]
+        gs_out[...] = total
+
+    def load(k, src):
+        return pltpu.make_async_copy(src, (lhs_a, lhs_b)[k], lhs_sem.at[k])
+
+    def out_load():
+        return pltpu.make_async_copy(out2_any, gts, load_sem.at[0])
+
+    def out_keep():
+        return pltpu.make_async_copy(gts.at[y], ro_out.at[t_me], keep_sem.at[0])
+
+    def out_sibling():
+        return push(out2_any.at[y], ro_out.at[t_me], o_send.at[0], o_recv.at[0], sibling)
+
+    def out_y():
+        return push(out2_any.at[1 - y], ro_out.at[t_me], o_send.at[1], o_recv.at[1], over_y)
+
+    def forward(ref, slot):
+        row = ref.at[t_me + 2 * fy]
+        return push(row, row, f_send.at[slot], f_recv.at[slot], sibling)
+
+    def gt_keep(i):
+        return pltpu.make_async_copy(gts.at[y, i], rg_out.at[t_me, i], keep_sem.at[1 + i])
+
+    def gt_sibling(i):
+        return push(gts.at[y, i], rg_out.at[t_me, i], g_send.at[i, 0], g_recv.at[i, 0], sibling)
+
+    def gt_y(i):
+        return push(gts.at[1 - y, i], rg_out.at[t_me, i], g_send.at[i, 1], g_recv.at[i, 1], over_y)
+
+    def at(step):
+        return pl.when(s == step)
+
+    @at(0)
+    def _():
+        load(0, gh_any).start()
+        load(1, a2_any).start()
+        out_load().start()
+        greet([sibling, over_x, over_y] + along_z)
+        out_y().start()
+        out_sibling().start()
+        sv[...] = jnp.zeros_like(sv)
+        load(0, gh_any).wait()
+        load(1, a2_any).wait()
+        out_load().wait()
+        out_keep().start()
+
+    @at(base_e + 1)
+    def _():
+        stage_b(0)
+
+    @at(base_b)
+    def _():
+        load(0, a1_any).start()
+        load(1, drh_any).start()
+        out_keep().wait()
+        out_y().wait_recv()
+        forward(ro_out, 0).start()
+
+    early = [
+        (base_b + 1, lambda: stage_b(1)),
+        (base_b + 2, lambda: stage_c(0)),
+        (base_b + 3, lambda: stage_d(0)),
+        (base_b + 4, lambda: stage_c(1)),
+        (base_b + 4, lambda: stage_f(0)),
+    ]
+    for step, event in early:
+        at(min(step, base_q))(event)
+
+    @at(base_q)
+    def _():
+        stage_d(1)
+        load(0, a1_any).wait()
+        load(1, drh_any).wait()
+        small(0).start()
+
+    at(base_q + 1)(lambda: small_step(0))
+    at(base_q + 2)(lambda: small_step(1))
+
+    @at(base_q + 3)
+    def _():
+        stage_f(1)
+        small_step(2)
+
+    @at(base_t)
+    def _():
+        stage_b(2)
+        small_end()
+        for i in range(n_img):
+            gt_y(i).wait_recv()
+        forward(rg_out, 1).start()
+
+    at(base_t + 1)(lambda: stage_c(2))
+    at(base_t + 2)(lambda: stage_d(2))
+
+    def put(w, t, g):
+        g = g.astype(bf16)
+        for d in range(n_dp):
+            part[w][t % 2, t // 2, d % 2, d // 2] = g[d * shard_rows : (d + 1) * shard_rows]
+
+    @pl.when(s < base_e)
+    def _():
+        put(0, s, dot_tn(lhs_a[...], hd_ref[...]))
+
+    @pl.when((s >= base_e) & (s < base_b))
+    def _():
+        put(1, s - base_e, dot_tn(lhs_b[...], hd_ref[...]))
+
+    @pl.when((s >= base_b) & (s < base_q))
+    def _():
+        i = s - base_b
+        d_a1 = jnp.zeros((rows, width), f32)
+        for t in range(4):
+            d_all = attention_back(seq, n_heads, qkv_ref, lse_ref, dmix_ref, t, wide, mix)
+            sv[0, 4 + t : 5 + t, :wide] += jnp.sum(d_all, axis=0, keepdims=True)
+            d_half = d_all.astype(bf16)
+            dqs[t, pl.ds(i * rows, rows), :] = d_half
+            d_a1 += half_round(dot_nt(d_half, wq_ref[t, :, :wide]))
+        normed, scale = n1_ref[...], lse_ref[:, 127:128]
+        grad = dres_ref[...] + norm_back(d_a1, normed, scale, vec_ref[0:1, :])
+        col = width // 2
+        for h in range(2):
+            gts[h, i] = grad[:seq, h * col : (h + 1) * col].astype(bf16)
+        sv[0, 8:9, :] += jnp.sum(d_a1 * normed, axis=0, keepdims=True)
+        sv[0, 9:10, :] += jnp.sum(d_a1, axis=0, keepdims=True)
+
+    @pl.when((s >= base_q) & (s < base_t))
+    def _():
+        t = s - base_q
+        dq = dot_tn(lhs_a[...], dqs[t])
+        dp_ = dot_tn(lhs_b[...], mix_ref[...])
+        cut = width - mix
+        put(
+            2,
+            t,
+            jnp.concatenate(
+                [dq[:, :cut], dq[:, cut:] + dp_[:, : wide - cut], dp_[:, wide - cut :]], axis=1
+            ),
+        )
+
+    at(1)(lambda: half(0, 0).start())
+    at(3)(lambda: half(0, 1).start())
+    at(base_e + 1)(lambda: half(1, 0).start())
+    at(base_e + 3)(lambda: half(1, 1).start())
+    for i in range(n_img):
+
+        @at(base_b + i)
+        def _(i=i):
+            gt_keep(i).start()
+            gt_y(i).start()
+            gt_sibling(i).start()
+
+    @at(base_q - 1)
+    def _():
+        sv[0, 10:14, :] = dvec_in[2:6, :]
+        for t in range(4):
+            sv[0, t : t + 1, :] = dbexp_in[t, 0:1, :]
+
+    at(base_q + 1)(lambda: half(2, 0).start())
+    at(base_q + 3)(lambda: half(2, 1).start())
+
+    @at(base_t + 3)
+    def _():
+        stage_f(2)
+        out_sibling().wait_recv()
+        forward(ro_out, 0).wait_recv()
+        for i in range(n_img):
+            gt_keep(i).wait()
+            gt_sibling(i).wait_recv()
+        forward(rg_out, 1).wait_recv()
+        out_sibling().wait_send()
+        out_y().wait_send()
+        for i in range(n_img):
+            gt_sibling(i).wait_send()
+            gt_y(i).wait_send()
+        forward(ro_out, 0).wait_send()
+        forward(rg_out, 1).wait_send()
+        for w in range(3):
+            half(w, 0).wait_send()
+            half(w, 1).wait_send()
+            to_second(w, 2).wait_send()
+            to_second(w, 3).wait_send()
+            to_first(w).wait_send()
+            for k in range(n_z - 1):
+                to_z(w, k).wait_send()
+        for k in range(3):
+            small(k).wait_send()
+        for j in range(n_z - 1):
+            small_z(j).wait_send()
+
+
+def rear(hd, mixp, qkv, lse, dmix, dres, n1, vec, wq, dvec, dbexp, gh, a2, a1, drh, out2, n_dp, n_img, n_heads):
+    total, width = n1.shape
+    rows = total // n_img
+    ff = hd.shape[1] // 8
+    wide, mix = qkv.shape[1] // 4, mixp.shape[1] // 4
+    seq, col = out2.shape[2], out2.shape[3]
+    n_z = n_dp // 2
+    shard_rows = width // n_dp
+    n_t = 4
+    base_b = 2 * n_t
+    base_q = base_b + n_img
+    n_steps = base_q + n_t + 4
+    cfg = (n_z, n_img, seq, rows, n_heads, shard_rows, wide, mix, ff)
+    image = lambda s: (jnp.clip(s - base_b, 0, n_img - 1), 0)
+    by_image = lambda n: pl.BlockSpec((rows, n), image)
     whole = lambda a: pl.BlockSpec(
-        a.shape, lambda i, s, nd=len(a.shape): (0,) * nd, pipeline_mode=pl.Buffered(1)
-    )
+        a.shape, lambda s, nd=len(a.shape): (0,) * nd, pipeline_mode=pl.Buffered(1)
+    )
+    anywhere = pl.BlockSpec(memory_space=pl.ANY)
+    resident = lambda shape: pl.BlockSpec(
+        shape, lambda s, nd=len(shape): (0,) * nd, pipeline_mode=pl.Buffered(1)
+    )
+    block = (shard_rows, width)
+    dma = pltpu.SemaphoreType.DMA
+    scratch = [
+        pltpu.VMEM((total, width), bf16),
+        pltpu.VMEM((total, width), bf16),
+        pltpu.VMEM((4, total, wide), bf16),
+        pltpu.VMEM((2, n_img, seq, col), bf16),
+    ]
+    scratch += [pltpu.VMEM((2, 2, 2, n_z) + block, bf16)] * 3
+    scratch += [pltpu.VMEM((2, 2, n_z) + block, bf16)] * 3
+    scratch += [pltpu.VMEM((2, n_z) + block, bf16)] * 3
+    scratch += [pltpu.VMEM((n_z,) + block, bf16)] * 3
+    scratch += [pltpu.VMEM((n_z - 1,) + block, bf16)] * 3
+    scratch += [
+        pltpu.VMEM((4, S_ROWS, width), f32),
+        pltpu.VMEM((3, S_ROWS, width), f32),
+        pltpu.VMEM((n_z, S_ROWS, width), f32),
+    ]
+    scratch += [dma((2,)), dma((1,)), dma((1 + n_img,))]
+    scratch += [dma((2,))] * 2 + [dma((n_img, 2))] * 2 + [dma((2,))] * 2
+    scratch += [dma((3, 2))] * 2 + [dma((3, 3))] * 2 + [dma((3, n_z - 1))] * 2
+    scratch += [dma((3,))] * 2 + [dma((n_z - 1,))] * 2
     return pl.pallas_call(
-        functools.partial(back_body, seq, n_heads),
-        out_shape=[
-            jax.ShapeDtypeStruct((total, 4 * wide), bf16),
-            jax.ShapeDtypeStruct((4, n_img, seq, col), bf16),
-            jax.ShapeDtypeStruct((8, width), f32),
-            jax.ShapeDtypeStruct((4, 8, wide), f32),
-        ],
-        grid_spec=pltpu.PrefetchScalarGridSpec(
-            num_scalar_prefetch=1,
-            grid=(n_img,),
-            in_specs=[
-                pl.BlockSpec((1, seq, width), lambda i, s: (s[0] + i, 0, 0)),
-                row_block(4 * wide),
-                row_block(128),
-                row_block(dmix.shape[1]),
-                row_block(width),
-                whole(vec),
-                whole(wq),
-            ],
-            out_specs=[
-                row_block(4 * wide),
-                pl.BlockSpec((4, 1, seq, col), lambda i, s: (0, i, 0, 0)),
-                pl.BlockSpec((8, width), lambda i, s: (0, 0)),
-                pl.BlockSpec((4, 8, wide), lambda i, s: (0, 0, 0)),
-            ],
-            scratch_shapes=[pltpu.VMEM((rows, width), f32)],
+        functools.partial(rear_body, cfg),
+        out_shape=[jax.ShapeDtypeStruct(block, f32)] * 3
+        + [jax.ShapeDtypeStruct((S_ROWS, width), f32)]
+        + [jax.ShapeDtypeStruct((n_t, n_img, seq, col), bf16)] * 2,
+        grid=(n_steps,),
+        in_specs=[
+            pl.BlockSpec((total, ff), lambda s: (0, jnp.clip(s, 0, 2 * n_t - 1))),
+            pl.BlockSpec((total, mix), lambda s: (0, jnp.clip(s - base_q, 0, n_t - 1))),
+            by_image(4 * wide),
+            by_image(128),
+            by_image(4 * mix),
+            by_image(width),
+            by_image(width),
+            whole(vec),
+            whole(wq),
+            whole(dvec),
+            whole(dbexp),
+        ]
+        + [anywhere] * 5,
+        out_specs=[resident(block)] * 3 + [resident((S_ROWS, width))] + [anywhere] * 2,
+        scratch_shapes=scratch,
+        compiler_params=pltpu.CompilerParams(
+            collective_id=1, has_side_effects=True, vmem_limit_bytes=VMEM_MAX
         ),
-        compiler_params=pltpu.CompilerParams(vmem_limit_bytes=VMEM_MAX),
-        name="back",
-    )(where, tokens, qkv, lse, dmix, dres, vec, wq)
+        name="rear",
+    )(hd, mixp, qkv, lse, dmix, dres, n1, vec, wq, dvec, dbexp, gh, a2, a1, drh, out2)
 
 
 def adamw(master, grad, first, second, rate, decay_rate):
@@ -675,48 +896,30 @@
 
     start = lax.axis_index("tensor") * n_img
     where = jnp.stack([start, counts[0]]).astype(jnp.int32)
-    a1, qkv, mixp, lse = front(where, tokens, vec, bias, w_q, n_img, rows, n_heads)
-    a2, hid, dpre, gh, dres, drh, dmix, out_t, dvec_a, dbexp = middle(
+    a1, n1, qkv, mixp, lse = front(where, tokens, vec, bias, w_q, n_img, rows, n_heads)
+    a2, hd, gh, dres, drh, dmix, out2, dvec, dbexp = middle(
         where, tokens, cotangent, mixp, vec, b_exp, w_q, w_e, w_r, n_img, rows
     )
-    dqkv, gt_t, dvec_b, dbias = back(where, tokens, qkv, lse, dmix, dres, vec, w_q, n_img, rows, n_heads)
-
-    output = lax.all_to_all(out_t, "tensor", 0, 0, tiled=True).astype(f32).reshape(slots, seq, -1)
-    grad_tokens = lax.all_to_all(gt_t, "tensor", 0, 0, tiled=True).astype(f32).reshape(slots, seq, -1)
-
-    d_r = dot_tn(gh, hid).astype(bf16)
-    d_e = dot_tn(a2, dpre).astype(bf16)
-    mix = mixp.shape[1] // n_t
-    d_q = dot_tn(a1, dqkv).reshape(width, n_t, wide)
-    d_p = dot_tn(drh, mixp).reshape(width, n_t, mix)
-    d_q = (
-        (
-            jnp.pad(d_q, ((0, 0), (0, 0), (0, width - wide)))
-            + jnp.pad(d_p, ((0, 0), (0, 0), (width - mix, 0)))
-        )
-        .astype(bf16)
-        .reshape(width, n_t * width)
-    )
-    dvec = jnp.concatenate([dvec_b[0:2], dvec_a[2:6]], axis=0)
-    db = dbias[:, 0]
-    s_qv = jnp.stack([db[:, :q_width], db[:, 2 * q_width : 3 * q_width]], axis=1)
-    s_qv = s_qv.reshape(n_t, 2, n_dp, qb).transpose(2, 0, 1, 3).reshape(n_dp, n_t, 2 * qb)
-    s_exp = dbexp[:, 0].reshape(n_t, n_dp, eb).transpose(1, 0, 2)
-    s_vec = dvec.reshape(6, n_dp, vb).transpose(1, 0, 2).reshape(n_dp, 1, 6 * vb)
-    s_vec = jnp.broadcast_to(s_vec, (n_dp, n_t, 6 * vb))
-    d_s = jnp.concatenate([s_qv, s_exp, s_vec, jnp.zeros((n_dp, n_t, width - n_small), f32)], axis=2)
-    d_s = jnp.pad(d_s.reshape(n_dp, 1, n_t * width), ((0, 0), (0, SMALL_ROWS - 1), (0, 0)))
-    d_s = d_s.reshape(n_dp * SMALL_ROWS, n_t * width).astype(bf16)
-    g_s, g_r, g_e, g_q = reduce_all([d_s, d_r, d_e, d_q], [width, ff, ff, width], n_dp)
-
-    g_qkv = g_q[:, : 3 * q_width].reshape(own_d, 3, q_width)
+    g_r, g_e, g_q, g_s, got_out, got_gt = rear(
+        hd, mixp, qkv, lse, dmix, dres, n1, vec, w_q, dvec, dbexp, gh, a2, a1, drh, out2, n_dp, n_img, n_heads
+    )
+    t_me, dp_me = lax.axis_index("tensor"), lax.axis_index("dp")
+
+    def own_columns(both):
+        picked = jnp.where(t_me % 2 == 0, both[..., :q_width], both[..., q_width:])
+        return picked.astype(f32).reshape(slots, seq, q_width)
+
+    output = own_columns(got_out)
+    grad_tokens = own_columns(got_gt)
+
+    g_qkv = jnp.stack([g_q[:, j * q_width : (j + 1) * q_width] for j in range(3)], axis=1)
     g_proj = g_q[:, 3 * q_width :].T
     g_expand = g_e
     g_reduce = g_r.T
-    g_row = g_s[0]
-    g_qvb = g_row[: 2 * qb].reshape(2, qb)
-    g_expb = g_row[2 * qb : 2 * qb + eb]
-    g_vec = g_row[2 * qb + eb : n_small].reshape(6, vb)
+    take = lambda row, at, n: lax.dynamic_slice(g_s, (row, at), (1, n))[0]
+    g_expb = take(t_me, dp_me * eb, eb)
+    g_qvb = jnp.stack([take(4 + t_me, dp_me * qb, qb), take(4 + t_me, 2 * q_width + dp_me * qb, qb)])
+    g_vec = lax.dynamic_slice(g_s, (8, dp_me * vb), (6, vb))
 
     results = [output, grad_tokens]
     for master, grad, first, second, rate, wd in (

time: 435 us -> 346 us (0.80)
  matrix products: 33.1 us -> 0 us
  local copies, waits for them, and re-layouts: 55.7 us -> 23.9 us
  waiting for transfers between devices: 15.6 us -> 0 us
  starting transfers between devices: 8.21 us -> 0 us
  other arithmetic: 32.2 us -> 25.4 us
  Pallas kernels: 286 us -> 291 us
    dot_general x4 -> x0, matrix products: 33.1 us -> none  [dot_tn(): lax.dot_general(a, b, (((0,), (0,)), ((), ())), preferred_element_type=f32)]
    all_to_all x2 -> x0, waiting for transfers between devices: 15.6 us -> none  [the longest x1 15.6 us: on_device(): lax.all_to_all(out_t, 'tensor', 0, 0, tiled=True).astype(f32)]
    reshape x7 -> x0, local copies, waits for them, and re-layouts: 13.2 us -> none  [the longest x1 9.95 us: on_device(): d_q = dot_tn(a1, dqkv).reshape(width, n_t, wide)]
    another operation x8 -> x1, local copies, waits for them, and re-layouts: 9.91 us -> 0.16 us  [the longest x1 9.31 us: reduce_all(): shaped = [g.reshape(n_z, 2, r, g.shape[1]) for g, r in zip(grads, rows)]]
    all_to_all x2 -> x0, starting transfers between devices: 8.21 us -> none  [the longest x1 4.44 us: on_device(): lax.all_to_all(gt_t, 'tensor', 0, 0, tiled=True).astype(f32)]
    convert_element_type x1 -> x0, other arithmetic: 8.1 us -> none  [on_device(): d_q = (jnp.pad(d_q, ((0, 0), (0, 0), (0, width - wide))) + jnp.pad(d_p, (...]
    pallas_call x2 -> x0, local copies, waits for them, and re-layouts: 6.8 us -> none  [the longest x1 4.38 us: back(): pl.pallas_call(functools.partial(back_body, seq, n_heads), out_shape=[jax...]
    slice x9 -> x0, local copies, waits for them, and re-layouts: 6.12 us -> none  [the longest x2 1.48 us: on_device(): dvec = jnp.concatenate([dvec_b[0:2], dvec_a[2:6]], axis=0)]
  transfers between devices with their start and end apart: 2 -> 0, of which waited for: 1 -> 0; matrix products, arithmetic and copies ran while one was open for 23% -> 0% of each run, Pallas kernels for 22% -> 0%
where the time goes in v2:
time: 346 us; the launch traced here: 342 us
  Pallas kernels  291 us (84%)
  other arithmetic  25.4 us (7%)
  local copies, waits for them, and re-layouts  23.9 us (7%)
    pallas_call x1, Pallas kernels, rear(): pl.pallas_call(functools.partial(rear_body, cfg), out_shape=[jax.ShapeDty...  142 us
    pallas_call x1, Pallas kernels, gather_all(): pl.pallas_call(functools.partial(gather_body, n_w, n_z), out_shape=[jax.S...  86.5 us
    pallas_call x1, Pallas kernels, middle(): pl.pallas_call(functools.partial(middle_body, seq), out_shape=[jax.ShapeD...  40.3 us
    pallas_call x1, Pallas kernels, front(): pl.pallas_call(functools.partial(front_body, seq, n_heads), out_shape=[ja...  22.4 us
    unnamed x49, local copies, waits for them, and re-layouts  17 us
    sub x7, other arithmetic, adamw(): master - rate * (first_hat / (jnp.sqrt(second_hat) + adam_eps) + decay_ra...  8.24 us

profile of v2, /device:TPU:0, one launch (start us, length us, event | category | flops | bytes accessed | tf_op | source)
XLA Modules:
  0.0 342.3 jit_solution(7949149624397322974)
XLA Ops:
  0.7 1.0 copy.69
  1.7 1.0 convert.28
  3.0 0.8 pad_maximum_fusion.1.refs_1_
  3.7 1.6 convert_bitcast_fusion.refs_3_
  5.4 1.6 convert_element_type.29.refs_2_
  7.0 0.7 convert.27
  7.9 0.7 convert.25
  10.0 86.5 %gather_weights.1 = (bf16[2,2,4,2,16,768]{5,4,3,2,1,0:T(8,128)(2,1)}, bf16[2,2,4,2,96,768]{5,4,3,2,1,0:T(8,128)(2,1)}, bf16[2,2,4,2,96,768]{5,4,3,2,1,0:T(8,128)(2,1)}, bf16[2,2,4,2,96,768]{5,4,3,2,1,0:T(8,128)(2,1)}) custom-call(bf16[16,768]{1,0:T(8,128)(2,1)} %scatter.4.refs_0_, bf16[96,768]{1,0:T(8,128)(2,1)} %pad_maximum_fusion.1.refs_1_, ...), custom_call_target="tpu_custom_call" | custom-call | tf_op jit(solution)/shard_map/gather_weights/pallas_call | solution.py:168
  96.5 1.1 slice.70
  100.7 22.4 %front.1 = (bf16[1040,768]{1,0:T(8,128)(2,1)}, f32[1040,768]{1,0:T(8,128)}, bf16[1040,2560]{1,0:T(8,128)(2,1)}, bf16[1040,1024]{1,0:T(8,128)(2,1)}, f32[1040,128]{1,0:T(8,128)}) custom-call(s32[2]{0:T(128)} %pad_add_fusion.where, f32[20,197,768]{2,1,0:T(8,128)} %x_ref.3, f32[8,768]{1,0:T(8,128)} %pad.15.vec_ref.refs_7_, f32[4,8,640]{2,1,0:T(8,128)} %pad.16.bias_ref, ...), custom_call_target="tpu_custom_call" | custom-call | tf_op jit(solution)/shard_map/front/pallas_call | solution.py:235
  123.9 40.3 %middle.1 = (bf16[1040,768]{1,0:T(8,128)(2,1)}, bf16[1040,6144]{1,0:T(8,128)(2,1)}, bf16[1040,768]{1,0:T(8,128)(2,1)}, f32[1040,768]{1,0:T(8,128)}, bf16[1040,76...) custom-call(s32[2]{0:T(128)} %pad_add_fusion.where, ...), custom_call_target="tpu_custom_call" | custom-call | tf_op jit(solution)/shard_map/middle/pallas_call | solution.py:353
  164.2 142.3 %rear.1 = (f32[96,768]{1,0:T(8,128)}, f32[96,768]{1,0:T(8,128)}, f32[96,768]{1,0:T(8,128)}, f32[24,768]{1,0:T(8,128)}, bf16[4,5,197,384]{3,2,1,0:T(8,128)(2,1)}, /*index=5*/bf16[4,5,197,384]{3,2,1,0:T(8,128)(2,1)}) custom-call(bf16[1040,6144]{1,0:T(8,128)(2,1)} %get-tuple-element.71.refs_0_, bf16[1040,1024]{1,0:T(8,128)(2,1)} %get-tuple-element.68.mix_ref.refs_1_, ...), custom_call_target="tpu_custom_call" | custom-call | tf_op jit(solution)/shard_map/rear/pallas_call | solution.py:795
  306.5 0.8 fusion.15
  307.3 1.3 multiply_subtract_fusion.5
  308.6 1.2 slice_bitcast_fusion
  309.8 1.1 multiply_subtract_fusion.2
  310.9 4.6 %slice_select_fusion = (bf16[4,5,197,192]{3,2,1,0:T(8,128)(2,1)S(1)}, bf16[4,5,197,192]{3,2,1,0:T(8,128)(2,1)S(1)}) fusion(bf16[4,5,197,384]{3,2,1,0:T(8,128)(2,1)} %get-tuple-element.85, pred[]{:T(512)S(6)} %eq.7, bf16[4,5,197,384]{3,2,1,0:T(8,128)(2,1)} %get-tuple-element.84), kind=kLoop, calls=%fused_computation.2 | loop fusion | flops 1512960 | bytes 9077761 | tf_op jit(solution)/shard_map/jit(_where)/select_n | solution.py:909
  315.6 2.4 bitcast_convert_fusion.1
  317.9 5.6 %copy.78 = f32[20,197,192]{1,2,0:T(8,128)} copy(f32[20,197,192]{2,1,0:T(8,128)} %bitcast_convert_fusion.1) | data formatting | bytes 6051840
  323.5 2.4 bitcast_convert_fusion
  326.0 5.8 %copy.79 = f32[20,197,192]{1,2,0:T(8,128)} copy(f32[20,197,192]{2,1,0:T(8,128)} %bitcast_convert_fusion) | data formatting | bytes 6051840
  331.9 1.0 multiply_subtract_fusion.1
  332.9 1.0 multiply_subtract_fusion
  334.2 1.0 multiply_subtract_fusion.3
  335.2 0.7 copy.81
  336.0 0.7 copy.82
  336.7 0.7 copy.83
  337.4 0.7 copy.80
  338.2 1.4 multiply_subtract_fusion.4
  339.6 1.3 multiply_subtract_fusion.6
  340.9 0.7 copy.93
  341.6 0.7 copy.94
  (72 shorter events, 5.5 us)
Async XLA Ops:
  164.2 145.6 %copy-start = (f32[96,3,192]{2,0,1:T(8,128)S(1)}, f32[96,3,192]{2,0,1:T(8,128)}, u32[]{:S(2)}) copy-start(f32[96,3,192]{2,0,1:T(8,128)} %param.29) | copy-start | bytes 663556
  164.2 145.6 %copy-start.5 = (f32[96,3,192]{2,0,1:T(8,128)S(1)}, f32[96,3,192]{2,0,1:T(8,128)}, u32[]{:S(2)}) copy-start(f32[96,3,192]{2,0,1:T(8,128)} %param.36) | copy-start | bytes 663556
  164.2 145.6 %copy-start.6 = (f32[96,3,192]{2,0,1:T(8,128)S(1)}, f32[96,3,192]{2,0,1:T(8,128)}, u32[]{:S(2)}) copy-start(f32[96,3,192]{2,0,1:T(8,128)} %param.37) | copy-start | bytes 663556
  325.9 5.9 %copy-start.1 = (f32[96,768]{1,0:T(8,128)S(1)}, f32[96,768]{1,0:T(8,128)}, u32[]{:S(2)}) copy-start(f32[96,768]{1,0:T(8,128)} %param.31) | copy-start | bytes 884740
  325.9 5.9 %copy-start.4 = (f32[96,768]{1,0:T(8,128)S(1)}, f32[96,768]{1,0:T(8,128)}, u32[]{:S(2)}) copy-start(f32[96,768]{1,0:T(8,128)} %get-tuple-element.225) | copy-start | bytes 884740
  325.9 5.9 %copy-start.7 = (f32[96,768]{1,0:T(8,128)S(1)}, f32[96,768]{1,0:T(8,128)}, u32[]{:S(2)}) copy-start(f32[96,768]{1,0:T(8,128)} %param.40) | copy-start | bytes 884740
  325.9 5.9 %copy-start.8 = (f32[96,768]{1,0:T(8,128)S(1)}, f32[96,768]{1,0:T(8,128)}, u32[]{:S(2)}) copy-start(f32[96,768]{1,0:T(8,128)} %param.41) | copy-start | bytes 884740
  325.9 7.0 %copy-start.2 = (f32[768,96]{0,1:T(8,128)S(1)}, f32[768,96]{0,1:T(8,128)}, u32[]{:S(2)}) copy-start(f32[768,96]{0,1:T(8,128)} %param.32) | copy-start | bytes 884740
  325.9 7.0 %copy-start.3 = (f32[96,768]{1,0:T(8,128)S(1)}, f32[96,768]{1,0:T(8,128)}, u32[]{:S(2)}) copy-start(f32[96,768]{1,0:T(8,128)} %get-tuple-element.88) | copy-start | bytes 884740
  326.0 7.0 %copy-start.9 = (f32[768,96]{0,1:T(8,128)S(1)}, f32[768,96]{0,1:T(8,128)}, u32[]{:S(2)}) copy-start(f32[768,96]{0,1:T(8,128)} %param.42) | copy-start | bytes 884740
  326.0 6.9 %copy-start.10 = (f32[768,96]{0,1:T(8,128)S(1)}, f32[768,96]{0,1:T(8,128)}, u32[]{:S(2)}) copy-start(f32[768,96]{0,1:T(8,128)} %param.43) | copy-start | bytes 884740
  331.7 2.2 copy-start.11
  331.8 2.3 copy-start.12
  331.8 6.4 %copy-start.13 = (f32[6,96]{1,0:T(8,128)S(1)}, f32[6,96]{1,0:T(8,128)}, u32[]{:S(2)}) copy-start(f32[6,96]{1,0:T(8,128)} %param.35) | copy-start | bytes 6916
  331.8 6.4 %copy-start.14 = (f32[6,96]{1,0:T(8,128)S(1)}, f32[6,96]{1,0:T(8,128)}, u32[]{:S(2)}) copy-start(f32[6,96]{1,0:T(8,128)} %param.48) | copy-start | bytes 6916
  331.8 6.4 %copy-start.15 = (f32[6,96]{1,0:T(8,128)S(1)}, f32[6,96]{1,0:T(8,128)}, u32[]{:S(2)}) copy-start(f32[6,96]{1,0:T(8,128)} %param.49) | copy-start | bytes 6916
  331.8 7.8 %copy-start.16 = (f32[96]{0:T(128)S(1)}, f32[96]{0:T(128)}, u32[]{:S(2)}) copy-start(f32[96]{0:T(128)} %param.34) | copy-start | bytes 1156
  331.8 7.8 %copy-start.17 = (f32[96]{0:T(128)S(1)}, f32[96]{0:T(128)}, u32[]{:S(2)}) copy-start(f32[96]{0:T(128)} %param.46) | copy-start | bytes 1156
  331.8 7.8 %copy-start.18 = (f32[96]{0:T(128)S(1)}, f32[96]{0:T(128)}, u32[]{:S(2)}) copy-start(f32[96]{0:T(128)} %param.47) | copy-start | bytes 1156

commit v3 on v2

--- a/solution.py
+++ b/solution.py
@@ -19,7 +19,6 @@
 adam_eps = 1e-08
 adam_step = 2.0
 norm_eps = 1e-06
-SMALL_ROWS = 16
 VMEM_MAX = 63 * 1024 * 1024
 
 
@@ -93,22 +92,52 @@
     )
 
 
-def gather_body(n_w, n_z, *refs):
-    shards, outs = refs[:n_w], refs[n_w : 2 * n_w]
-    local_sem, z_send, z_recv, s_send, s_recv = refs[2 * n_w :]
+def key_mask(rows, seq):
+    return lax.broadcasted_iota(jnp.int32, (rows, rows), 1) < seq
+
+
+def load_rows(src, dst, seq):
+    dst[pl.ds(0, seq), :] = src[0]
+
+
+S_ROWS = 24
+NAT_ROWS = 32
+NAT_VEC = 8
+
+
+def fore_body(cfg, *refs):
+    n_z, n_img, seq, rows, n_heads, wide, mix = cfg
+    (qkv_w, proj_w, exp_w, red_w, nat_own, tokens) = refs[:6]
+    (gq, ge, gr, nat_ref, a1_ref, n1_ref, qkv_ref, mix_ref, lse_ref) = refs[6:15]
+    (xs, xall, sh_q, sh_e, sh_r, gs, wq) = refs[15:22]
+    x_sem, w_sem, local_sem, z_send, z_recv, s_send, s_recv = refs[22:]
+    s = pl.program_id(0)
     z, x, y, c, first, second, sibling, sets, along_z = places(n_z)
-    greet([first, second, sibling] + along_z)
-
-    def own(w):
-        return pltpu.make_async_copy(shards[w], outs[w].at[y, c, z, x], local_sem.at[w])
-
-    def to_z(w, k):
-        return push(shards[w], outs[w].at[y, c, z, x], z_send.at[w, k], z_recv.at[w, k], along_z[k])
-
-    def move(w, which, peer, slot):
-        sy, sx = sets[which]
-        part = outs[w].at[sy, c, :, sx]
-        return push(part, part, s_send.at[w, slot], s_recv.at[w, slot], peer)
+    t_me = lax.axis_index("tensor")
+    width = xs.shape[1]
+    half = width // 2
+    q_width = n_heads * HEAD_DIM
+    whole = slice(None)
+    pieces = [(nat_own, gs, whole)]
+    for shard, out in ((sh_q, gq), (sh_e, ge), (sh_r, gr)):
+        pieces += [(shard, out, pl.ds(0, half)), (shard, out, pl.ds(half, half))]
+    n_p = len(pieces)
+
+    def place(p, at):
+        shard, out, cols = pieces[p]
+        if cols is whole:
+            return out.at[at]
+        return out.at[at + (whole, cols)]
+
+    def source(p):
+        shard, out, cols = pieces[p]
+        return shard if cols is whole else shard.at[:, cols]
+
+    def own(p):
+        return pltpu.make_async_copy(source(p), place(p, (y, c, z, x)), local_sem.at[p])
+
+    def to_z(p, k):
+        return push(source(p), place(p, (y, c, z, x)), z_send.at[p, k], z_recv.at[p, k], along_z[k])
 
     plan = {
         0: (0, first),
@@ -120,148 +149,176 @@
         6: (3, sibling),
     }
 
-    def go(w, slot):
+    def move(p, slot):
         which, peer = plan[slot]
-        move(w, which, peer, slot).start()
-
-    def arrived(w, slot):
-        which, peer = plan[slot]
-        move(w, which, peer, slot).wait_recv()
-
-    for w in range(n_w):
-        own(w).start()
+        sy, sx = sets[which]
+        shard, out, cols = pieces[p]
+        part = out.at[sy, c, :, sx] if cols is whole else out.at[sy, c, :, sx, :, cols]
+        return push(part, part, s_send.at[p, slot], s_recv.at[p, slot], peer)
+
+    ahead = 3
+
+    def send_z(p):
         for k in range(n_z - 1):
-            to_z(w, k).start()
-    for step in range(n_w + 3):
-        w = step
-        if 0 <= w < n_w:
-            own(w).wait()
+            to_z(p, k).start()
+
+    def advance(step):
+        p = step
+        if 0 <= p < n_p:
+            own(p).wait()
             for k in range(n_z - 1):
-                to_z(w, k).wait_recv()
+                to_z(p, k).wait_recv()
             for slot in (0, 1, 3):
-                go(w, slot)
-        w = step - 1
-        if 0 <= w < n_w:
-            arrived(w, 0)
-            go(w, 2)
-            go(w, 4)
-        w = step - 2
-        if 0 <= w < n_w:
-            arrived(w, 1)
-            go(w, 5)
-            arrived(w, 2)
-            go(w, 6)
-        w = step - 3
-        if 0 <= w < n_w:
+                move(p, slot).start()
+            if p + ahead < n_p:
+                send_z(p + ahead)
+        p = step - 1
+        if 0 <= p < n_p:
+            move(p, 0).wait_recv()
+            move(p, 2).start()
+            move(p, 4).start()
+        p = step - 2
+        if 0 <= p < n_p:
+            move(p, 1).wait_recv()
+            move(p, 5).start()
+            move(p, 2).wait_recv()
+            move(p, 6).start()
+        p = step - 3
+        if 0 <= p < n_p:
             for slot in (3, 4, 5, 6):
-                arrived(w, slot)
-    for w in range(n_w):
-        for k in range(n_z - 1):
-            to_z(w, k).wait_send()
-        for slot, (which, peer) in plan.items():
-            move(w, which, peer, slot).wait_send()
-
-
-def gather_all(shards, n_dp):
-    n_w, n_z = len(shards), n_dp // 2
-    shapes = [(2, 2, n_z, 2) + s.shape for s in shards]
+                move(p, slot).wait_recv()
+
+    def image(i):
+        return pltpu.make_async_copy(tokens.at[t_me * n_img + i], xall.at[i], x_sem.at[i])
+
+    def fetch_wq():
+        return pltpu.make_async_copy(gq, wq, w_sem.at[0])
+
+    @pl.when(s == 0)
+    def _():
+        for i in range(n_img):
+            image(i).start()
+        for j in range(3):
+            sh_q[:, j * q_width : (j + 1) * q_width] = qkv_w[j].astype(bf16)
+        sh_q[:, 3 * q_width :] = proj_w[...].T.astype(bf16)
+        sh_e[...] = exp_w[...].astype(bf16)
+        sh_r[...] = red_w[...].astype(bf16)
+        xs[...] = jnp.zeros_like(xs)
+        greet([first, second, sibling] + along_z)
+        for p in range(n_p):
+            own(p).start()
+        for p in range(ahead):
+            send_z(p)
+        for step in range(6):
+            advance(step)
+        fetch_wq().start()
+        total = jnp.zeros((NAT_ROWS, width), f32)
+        for yy in range(2):
+            for cc in range(2):
+                for xx in range(2):
+                    for zz in range(n_z):
+                        total = total + gs[yy, cc, zz, xx].astype(f32)
+        nat_ref[...] = total
+        for i in range(n_img):
+            image(i).wait()
+        fetch_wq().wait()
+
+    for grid_step, step in ((2, 6), (3, 7), (4, 8)):
+        pl.when(s == grid_step)(lambda step=step: advance(step))
+
+    @pl.when((s >= 1) & (s <= n_img))
+    def _():
+        xs[pl.ds(0, seq), :] = xall[s - 1]
+        normed, scale = norm_stats(xs[...])
+        n1_ref[...] = normed
+        a1_ref[...] = (normed * nat_ref[NAT_VEC : NAT_VEC + 1, :] + nat_ref[NAT_VEC + 1 : NAT_VEC + 2, :]).astype(bf16)
+        mask = key_mask(rows, seq)
+        lane = lax.broadcasted_iota(jnp.int32, (rows, 128), 1)
+        lse_all = jnp.where(lane == 127, scale, 0.0)
+        pad = mix - q_width
+        for t in range(4):
+            w_t = wq[t // 2, t % 2, :, :, :, :wide].reshape(width, wide)
+            qkv = (dot_nn(a1_ref[...], w_t) + nat_ref[4 + t : 5 + t, :wide]).astype(bf16)
+            qkv_ref[:, t * wide : (t + 1) * wide] = qkv
+            outs = [jnp.zeros((rows, pad), bf16)]
+            for h in range(n_heads):
+                q = qkv[:, h * HEAD_DIM : (h + 1) * HEAD_DIM]
+                k = qkv[:, q_width + h * HEAD_DIM : q_width + (h + 1) * HEAD_DIM]
+                v = qkv[:, 2 * q_width + h * HEAD_DIM : 2 * q_width + (h + 1) * HEAD_DIM]
+                scores = jnp.where(mask, dot_nt(q, k) * (HEAD_DIM**-0.5), -1e30)
+                top = jnp.max(scores, axis=-1, keepdims=True)
+                e = jnp.exp(scores - top)
+                total = jnp.sum(e, axis=-1, keepdims=True)
+                p = (e * (1.0 / total)).astype(bf16)
+                outs.append(dot_nn(p, v).astype(bf16))
+                lse_all = jnp.where(lane == t * n_heads + h, top + jnp.log(total), lse_all)
+            mix_ref[:, t * mix : (t + 1) * mix] = jnp.concatenate(outs, axis=1)
+        lse_ref[...] = lse_all
+
+    @pl.when(s == n_img + 1)
+    def _():
+        advance(9)
+        for p in range(n_p):
+            for k in range(n_z - 1):
+                to_z(p, k).wait_send()
+            for slot in plan:
+                move(p, slot).wait_send()
+
+
+def fore(qkv_w, proj_w, exp_w, red_w, nat_own, tokens, n_dp, n_img, rows, n_heads):
+    slots, seq, width = tokens.shape
+    n_z = n_dp // 2
+    own_d = exp_w.shape[0]
+    q3 = 3 * n_heads * HEAD_DIM
+    wide, mix = -(-q3 // 128) * 128, width - (q3 // 128) * 128
+    total = n_img * rows
+    cfg = (n_z, n_img, seq, rows, n_heads, wide, mix)
+    block = (own_d, width)
+    full = (2, 2, n_z, 2)
+    whole = lambda shape: pl.BlockSpec(
+        shape, lambda s, nd=len(shape): (0,) * nd, pipeline_mode=pl.Buffered(1)
+    )
+    by_image = lambda n: pl.BlockSpec((rows, n), lambda s: (jnp.clip(s - 1, 0, n_img - 1), 0))
+    anywhere = pl.BlockSpec(memory_space=pl.ANY)
+    dma = pltpu.SemaphoreType.DMA
+    n_p = 7
     return pl.pallas_call(
-        functools.partial(gather_body, n_w, n_z),
-        out_shape=[jax.ShapeDtypeStruct(s, bf16) for s in shapes],
-        in_specs=[pl.BlockSpec(memory_space=pltpu.VMEM)] * n_w,
-        out_specs=[pl.BlockSpec(memory_space=pl.ANY)] * n_w,
-        scratch_shapes=[
-            pltpu.SemaphoreType.DMA((n_w,)),
-            pltpu.SemaphoreType.DMA((n_w, n_z - 1)),
-            pltpu.SemaphoreType.DMA((n_w, n_z - 1)),
-            pltpu.SemaphoreType.DMA((n_w, 7)),
-            pltpu.SemaphoreType.DMA((n_w, 7)),
-        ],
-        compiler_params=pltpu.CompilerParams(collective_id=0, has_side_effects=True),
-        name="gather_weights",
-    )(*shards)
-
-
-def key_mask(rows, seq):
-    return lax.broadcasted_iota(jnp.int32, (rows, rows), 1) < seq
-
-
-def load_rows(src, dst, seq):
-    dst[pl.ds(0, seq), :] = src[0]
-
-
-def front_body(seq, n_heads, where, x_ref, vec_ref, bias_ref, wq_ref, a1_ref, n1_ref, qkv_ref, mix_ref, lse_ref, xs):
-    rows = xs.shape[0]
-
-    @pl.when(pl.program_id(0) == 0)
-    def _():
-        xs[...] = jnp.zeros_like(xs)
-
-    load_rows(x_ref, xs, seq)
-    normed, scale = norm_stats(xs[...])
-    n1_ref[...] = normed
-    a1 = (normed * vec_ref[0:1, :] + vec_ref[1:2, :]).astype(bf16)
-    a1_ref[...] = a1
-    mask = key_mask(rows, seq)
-    lane = lax.broadcasted_iota(jnp.int32, (rows, 128), 1)
-    lse_ref[...] = jnp.where(lane == 127, scale, 0.0)
-    q_width = n_heads * HEAD_DIM
-    wide = bias_ref.shape[2]
-    pad = mix_ref.shape[1] // 4 - q_width
-    for t in range(4):
-        qkv = (dot_nn(a1_ref[...], wq_ref[t, :, :wide]) + bias_ref[t, 0:1, :]).astype(bf16)
-        qkv_ref[:, t * wide : (t + 1) * wide] = qkv
-        outs = [jnp.zeros((rows, pad), bf16)]
-        for h in range(n_heads):
-            q = qkv[:, h * HEAD_DIM : (h + 1) * HEAD_DIM]
-            k = qkv[:, q_width + h * HEAD_DIM : q_width + (h + 1) * HEAD_DIM]
-            v = qkv[:, 2 * q_width + h * HEAD_DIM : 2 * q_width + (h + 1) * HEAD_DIM]
-            s = jnp.where(mask, dot_nt(q, k) * (HEAD_DIM**-0.5), -1e30)
-            top = jnp.max(s, axis=-1, keepdims=True)
-            e = jnp.exp(s - top)
-            total = jnp.sum(e, axis=-1, keepdims=True)
-            p = (e * (1.0 / total)).astype(bf16)
-            outs.append(dot_nn(p, v).astype(bf16))
-            lse = top + jnp.log(total)
-            lse_ref[...] = jnp.where(lane == t * n_heads + h, lse, lse_ref[...])
-        mix_ref[:, t * (pad + q_width) : (t + 1) * (pad + q_width)] = jnp.concatenate(outs, axis=1)
-
-
-def front(where, tokens, vec, bias, wq, n_img, rows, n_heads):
-    slots, seq, width = tokens.shape
-    wide = bias.shape[2]
-    mix = width - (3 * n_heads * HEAD_DIM // 128) * 128
-    total = n_img * rows
-    return pl.pallas_call(
-        functools.partial(front_body, seq, n_heads),
-        out_shape=[
+        functools.partial(fore_body, cfg),
+        out_shape=[jax.ShapeDtypeStruct(full + block, bf16)] * 3
+        + [
+            jax.ShapeDtypeStruct((NAT_ROWS, width), f32),
             jax.ShapeDtypeStruct((total, width), bf16),
             jax.ShapeDtypeStruct((total, width), f32),
             jax.ShapeDtypeStruct((total, 4 * wide), bf16),
             jax.ShapeDtypeStruct((total, 4 * mix), bf16),
             jax.ShapeDtypeStruct((total, 128), f32),
         ],
-        grid_spec=pltpu.PrefetchScalarGridSpec(
-            num_scalar_prefetch=1,
-            grid=(n_img,),
-            in_specs=[
-                pl.BlockSpec((1, seq, width), lambda i, s: (s[0] + i, 0, 0)),
-                pl.BlockSpec(vec.shape, lambda i, s: (0, 0)),
-                pl.BlockSpec(bias.shape, lambda i, s: (0, 0, 0)),
-                pl.BlockSpec(wq.shape, lambda i, s: (0, 0, 0), pipeline_mode=pl.Buffered(1)),
-            ],
-            out_specs=[
-                pl.BlockSpec((rows, width), lambda i, s: (i, 0)),
-                pl.BlockSpec((rows, width), lambda i, s: (i, 0)),
-                pl.BlockSpec((rows, 4 * wide), lambda i, s: (i, 0)),
-                pl.BlockSpec((rows, 4 * mix), lambda i, s: (i, 0)),
-                pl.BlockSpec((rows, 128), lambda i, s: (i, 0)),
-            ],
-            scratch_shapes=[pltpu.VMEM((rows, width), f32)],
+        grid=(n_img + 2,),
+        in_specs=[whole(a.shape) for a in (qkv_w, proj_w, exp_w, red_w, nat_own)] + [anywhere],
+        out_specs=[anywhere] * 3
+        + [whole((NAT_ROWS, width))]
+        + [by_image(n) for n in (width, width, 4 * wide, 4 * mix, 128)],
+        scratch_shapes=[
+            pltpu.VMEM((rows, width), f32),
+            pltpu.VMEM((n_img, seq, width), f32),
+            pltpu.VMEM(block, bf16),
+            pltpu.VMEM(block, bf16),
+            pltpu.VMEM(block, bf16),
+            pltpu.VMEM(full + (NAT_ROWS, width), bf16),
+            pltpu.VMEM(full + block, bf16),
+            dma((n_img,)),
+            dma((1,)),
+            dma((n_p,)),
+            dma((n_p, n_z - 1)),
+            dma((n_p, n_z - 1)),
+            dma((n_p, 7)),
+            dma((n_p, 7)),
+        ],
+        compiler_params=pltpu.CompilerParams(
+            collective_id=0, has_side_effects=True, vmem_limit_bytes=VMEM_MAX
         ),
-        compiler_params=pltpu.CompilerParams(vmem_limit_bytes=VMEM_MAX),
-        name="front",
-    )(where, tokens, vec, bias, wq)
+        name="fore",
+    )(qkv_w, proj_w, exp_w, red_w, nat_own, tokens)
 
 
 def middle_body(
@@ -270,8 +327,7 @@
     x_ref,
     cot_ref,
     mix_ref,
-    vec_ref,
-    bexp_ref,
+    nat_ref,
     wq_ref,
     we_ref,
     wr_ref,
@@ -305,14 +361,14 @@
     att = jnp.zeros((rows, width), f32)
     for t in range(4):
         att += half_round(dot_nt(mix_ref[:, t * mix : (t + 1) * mix], wq_ref[t, :, width - mix :]))
-    resid = xs[...] + att + vec_ref[2:3, :]
+    resid = xs[...] + att + nat_ref[NAT_VEC + 2 : NAT_VEC + 3, :]
     normed2, scale2 = norm_stats(resid)
-    a2_ref[...] = (normed2 * vec_ref[3:4, :] + vec_ref[4:5, :]).astype(bf16)
+    a2_ref[...] = (normed2 * nat_ref[NAT_VEC + 3 : NAT_VEC + 4, :] + nat_ref[NAT_VEC + 4 : NAT_VEC + 5, :]).astype(bf16)
     gh_ref[...] = gs[...].astype(bf16)
     feed = jnp.zeros((rows, width), f32)
     d_a2 = jnp.zeros((rows, width), f32)
     for t in range(4):
-        pre = dot_nn(a2_ref[...], we_ref[t]) + bexp_ref[t, 0:1, :]
+        pre = dot_nn(a2_ref[...], we_ref[t]) + nat_ref[t : t + 1, :ff]
         cdf = 0.5 + 0.5 * lax.erf(pre * (0.5**0.5))
         hid = (pre * cdf).astype(bf16)
         slope = cdf + pre * jnp.exp(-0.5 * pre * pre) * ((2.0 * jnp.pi) ** -0.5)
@@ -323,11 +379,11 @@
         hd_ref[:, (4 + t) * ff : (5 + t) * ff] = dph
         feed += half_round(dot_nt(hid, wr_ref[t]))
         d_a2 += half_round(dot_nt(dph, we_ref[t]))
-    out = (resid + feed + vec_ref[5:6, :]) * live
+    out = (resid + feed + nat_ref[NAT_VEC + 5 : NAT_VEC + 6, :]) * live
     col = width // 2
     for t in range(2):
         out_ref[t, 0] = out[:seq, t * col : (t + 1) * col].astype(bf16)
-    d_resid = gs[...] + norm_back(d_a2, normed2, scale2, vec_ref[3:4, :])
+    d_resid = gs[...] + norm_back(d_a2, normed2, scale2, nat_ref[NAT_VEC + 3 : NAT_VEC + 4, :])
     dres_ref[...] = d_resid
     drh = d_resid.astype(bf16)
     drh_ref[...] = drh
@@ -339,7 +395,7 @@
     dvec_ref[5:6, :] += jnp.sum(gs[...], axis=0, keepdims=True)
 
 
-def middle(where, tokens, cotangent, mixp, vec, bexp, wq, we, wr, n_img, rows):
+def middle(where, tokens, cotangent, mixp, nat, wq, we, wr, n_img, rows):
     slots, seq, width = tokens.shape
     ff = we.shape[2]
     mix = mixp.shape[1]
@@ -366,7 +422,7 @@
         grid_spec=pltpu.PrefetchScalarGridSpec(
             num_scalar_prefetch=1,
             grid=(n_img,),
-            in_specs=[image, image, row_block(mix)] + [whole(a) for a in (vec, bexp, wq, we, wr)],
+            in_specs=[image, image, row_block(mix)] + [whole(a) for a in (nat, wq, we, wr)],
             out_specs=[
                 row_block(width),
                 row_block(8 * ff),
@@ -382,18 +438,15 @@
         ),
         compiler_params=pltpu.CompilerParams(vmem_limit_bytes=VMEM_MAX),
         name="middle",
-    )(where, tokens, cotangent, mixp, vec, bexp, wq, we, wr)
-
-
-S_ROWS = 24
-
-
-def attention_back(seq, n_heads, qkv_ref, lse_ref, dmix_ref, t, wide, mix):
+    )(where, tokens, cotangent, mixp, nat, wq, we, wr)
+
+
+def attention_back(seq, n_heads, qkv_ref, lse_rows, dmix_ref, t, wide, mix):
     rows = qkv_ref.shape[0]
     q_width = n_heads * HEAD_DIM
     scale_qk = HEAD_DIM**-0.5
-    mask = key_mask(rows, seq)
-    dq, dk, dv = [], [], []
+    mask = lax.broadcasted_iota(jnp.int32, (rows, rows), 0) < seq
+    dq_t, dk, dv = [], [], []
     for h in range(n_heads):
         at = t * wide + h * HEAD_DIM
         q = qkv_ref[:, at : at + HEAD_DIM]
@@ -401,25 +454,26 @@
         v = qkv_ref[:, at + 2 * q_width : at + 2 * q_width + HEAD_DIM]
         m_at = (t + 1) * mix - q_width + h * HEAD_DIM
         dm = dmix_ref[:, m_at : m_at + HEAD_DIM]
-        lse = lse_ref[:, t * n_heads + h : t * n_heads + h + 1]
-        p = jnp.where(mask, jnp.exp(dot_nt(q, k) * scale_qk - lse), 0.0)
-        dv.append(dot_tn(p.astype(bf16), dm))
-        d_p = dot_nt(dm, v)
-        delta = jnp.sum(p * d_p, axis=-1, keepdims=True)
+        lse = lse_rows[t * n_heads + h : t * n_heads + h + 1, :]
+        p = jnp.where(mask, jnp.exp(dot_nt(k, q) * scale_qk - lse), 0.0)
+        dv.append(dot_nn(p.astype(bf16), dm))
+        d_p = dot_nt(v, dm)
+        delta = jnp.sum(p * d_p, axis=0, keepdims=True)
         ds = (p * (d_p - delta) * scale_qk).astype(bf16)
-        dq.append(dot_nn(ds, k))
-        dk.append(dot_tn(ds, q))
-    return jnp.concatenate(dq + dk + dv + [jnp.zeros((rows, wide - 3 * q_width), f32)], axis=1)
+        dq_t.append(dot_tn(k, ds))
+        dk.append(dot_nn(ds, q))
+    dq = jnp.concatenate(dq_t, axis=0).T
+    return jnp.concatenate([dq] + dk + dv + [jnp.zeros((rows, wide - 3 * q_width), f32)], axis=1)
 
 
 def rear_body(cfg, *refs):
     n_z, n_img, seq, rows, n_heads, shard_rows, wide, mix, ff = cfg
-    (hd_ref, mix_ref, qkv_ref, lse_ref, dmix_ref, dres_ref, n1_ref, vec_ref, wq_ref, dvec_in, dbexp_in) = refs[:11]
+    (hd_ref, mix_ref, qkv_ref, lse_ref, dmix_ref, dres_ref, n1_ref, nat_ref, wq_ref, dvec_in, dbexp_in) = refs[:11]
     gh_any, a2_any, a1_any, drh_any, out2_any = refs[11:16]
     gr_out, ge_out, gq_out, gs_out, ro_out, rg_out = refs[16:22]
     (lhs_a, lhs_b, dqs, gts) = refs[22:26]
-    part, got, got2, got1, gotz = (refs[26 + 3 * k : 29 + 3 * k] for k in range(5))
-    sv, sgot, sz = refs[41:44]
+    part, got, got2, got1, gotz = (refs[26 + 4 * k : 30 + 4 * k] for k in range(5))
+    sv, sgot, sz = refs[46:49]
     (
         lhs_sem,
         load_sem,
@@ -440,8 +494,9 @@
         v_recv,
         vz_send,
         vz_recv,
-    ) = refs[44:]
-    outs = (gr_out, ge_out, gq_out)
+    ) = refs[49:]
+    half_q = gq_out.shape[1] // 2
+    outs = (gr_out, ge_out, gq_out.at[:, :half_q], gq_out.at[:, half_q:])
     s = pl.program_id(0)
     n_t = 4
     base_e, base_b = n_t, 2 * n_t
@@ -461,7 +516,7 @@
     along_z = [(lax.rem(z + k, n_z) * 2 + x, t_me) for k in range(1, n_z)]
 
     def route(w):
-        m = c if w == 2 else 0 * c
+        m = c
         first = (dp + m * fx, t_me + (1 - m) * 2 * fy)
         second = (dp + (1 - m) * fx, t_me + m * 2 * fy)
         sets = (
@@ -612,16 +667,15 @@
     def _():
         load(0, a1_any).start()
         load(1, drh_any).start()
+        stage_b(1)
         out_keep().wait()
         out_y().wait_recv()
         forward(ro_out, 0).start()
 
     early = [
-        (base_b + 1, lambda: stage_b(1)),
-        (base_b + 2, lambda: stage_c(0)),
+        (base_b + 1, lambda: stage_c(0)),
         (base_b + 3, lambda: stage_d(0)),
         (base_b + 4, lambda: stage_c(1)),
-        (base_b + 4, lambda: stage_f(0)),
     ]
     for step, event in early:
         at(min(step, base_q))(event)
@@ -638,25 +692,36 @@
 
     @at(base_q + 3)
     def _():
+        small_step(2)
+
+    @at(base_t)
+    def _():
+        stage_b(2)
+        stage_b(3)
+        small_end()
+        stage_f(0)
         stage_f(1)
-        small_step(2)
-
-    @at(base_t)
-    def _():
-        stage_b(2)
-        small_end()
         for i in range(n_img):
             gt_y(i).wait_recv()
         forward(rg_out, 1).start()
 
-    at(base_t + 1)(lambda: stage_c(2))
-    at(base_t + 2)(lambda: stage_d(2))
+    for step, stage in ((base_t + 1, stage_c), (base_t + 2, stage_d)):
+
+        @at(step)
+        def _(stage=stage):
+            stage(2)
+            stage(3)
+
 
     def put(w, t, g):
         g = g.astype(bf16)
         for d in range(n_dp):
             part[w][t % 2, t // 2, d % 2, d // 2] = g[d * shard_rows : (d + 1) * shard_rows]
 
+    def put_q(t, g):
+        put(2, t, g[:, :half_q])
+        put(3, t, g[:, half_q:])
+
     @pl.when(s < base_e)
     def _():
         put(0, s, dot_tn(lhs_a[...], hd_ref[...]))
@@ -669,14 +734,15 @@
     def _():
         i = s - base_b
         d_a1 = jnp.zeros((rows, width), f32)
+        lse_rows = lse_ref[...].T
         for t in range(4):
-            d_all = attention_back(seq, n_heads, qkv_ref, lse_ref, dmix_ref, t, wide, mix)
+            d_all = attention_back(seq, n_heads, qkv_ref, lse_rows, dmix_ref, t, wide, mix)
             sv[0, 4 + t : 5 + t, :wide] += jnp.sum(d_all, axis=0, keepdims=True)
             d_half = d_all.astype(bf16)
             dqs[t, pl.ds(i * rows, rows), :] = d_half
             d_a1 += half_round(dot_nt(d_half, wq_ref[t, :, :wide]))
         normed, scale = n1_ref[...], lse_ref[:, 127:128]
-        grad = dres_ref[...] + norm_back(d_a1, normed, scale, vec_ref[0:1, :])
+        grad = dres_ref[...] + norm_back(d_a1, normed, scale, nat_ref[NAT_VEC : NAT_VEC + 1, :])
         col = width // 2
         for h in range(2):
             gts[h, i] = grad[:seq, h * col : (h + 1) * col].astype(bf16)
@@ -689,8 +755,7 @@
         dq = dot_tn(lhs_a[...], dqs[t])
         dp_ = dot_tn(lhs_b[...], mix_ref[...])
         cut = width - mix
-        put(
-            2,
+        put_q(
             t,
             jnp.concatenate(
                 [dq[:, :cut], dq[:, cut:] + dp_[:, : wide - cut], dp_[:, wide - cut :]], axis=1
@@ -715,12 +780,18 @@
         for t in range(4):
             sv[0, t : t + 1, :] = dbexp_in[t, 0:1, :]
 
-    at(base_q + 1)(lambda: half(2, 0).start())
-    at(base_q + 3)(lambda: half(2, 1).start())
+    for step, yy in ((base_q + 1, 0), (base_q + 3, 1)):
+
+        @at(step)
+        def _(yy=yy):
+            half(2, yy).start()
+            half(3, yy).start()
+
 
     @at(base_t + 3)
     def _():
         stage_f(2)
+        stage_f(3)
         out_sibling().wait_recv()
         forward(ro_out, 0).wait_recv()
         for i in range(n_img):
@@ -734,7 +805,7 @@
             gt_y(i).wait_send()
         forward(ro_out, 0).wait_send()
         forward(rg_out, 1).wait_send()
-        for w in range(3):
+        for w in range(4):
             half(w, 0).wait_send()
             half(w, 1).wait_send()
             to_second(w, 2).wait_send()
@@ -778,11 +849,9 @@
         pltpu.VMEM((4, total, wide), bf16),
         pltpu.VMEM((2, n_img, seq, col), bf16),
     ]
-    scratch += [pltpu.VMEM((2, 2, 2, n_z) + block, bf16)] * 3
-    scratch += [pltpu.VMEM((2, 2, n_z) + block, bf16)] * 3
-    scratch += [pltpu.VMEM((2, n_z) + block, bf16)] * 3
-    scratch += [pltpu.VMEM((n_z,) + block, bf16)] * 3
-    scratch += [pltpu.VMEM((n_z - 1,) + block, bf16)] * 3
+    pieces = [block, block, (shard_rows, width // 2), (shard_rows, width // 2)]
+    for lead in ((2, 2, 2, n_z), (2, 2, n_z), (2, n_z), (n_z,), (n_z - 1,)):
+        scratch += [pltpu.VMEM(lead + piece, bf16) for piece in pieces]
     scratch += [
         pltpu.VMEM((4, S_ROWS, width), f32),
         pltpu.VMEM((3, S_ROWS, width), f32),
@@ -790,7 +859,7 @@
     ]
     scratch += [dma((2,)), dma((1,)), dma((1 + n_img,))]
     scratch += [dma((2,))] * 2 + [dma((n_img, 2))] * 2 + [dma((2,))] * 2
-    scratch += [dma((3, 2))] * 2 + [dma((3, 3))] * 2 + [dma((3, n_z - 1))] * 2
+    scratch += [dma((4, 2))] * 2 + [dma((4, 3))] * 2 + [dma((4, n_z - 1))] * 2
     scratch += [dma((3,))] * 2 + [dma((n_z - 1,))] * 2
     return pl.pallas_call(
         functools.partial(rear_body, cfg),
@@ -819,6 +888,82 @@
         ),
         name="rear",
     )(hd, mixp, qkv, lse, dmix, dres, n1, vec, wq, dvec, dbexp, gh, a2, a1, drh, out2)
+
+
+def finish_body(n_heads, where, out_ref, gt_ref, o_ref, g_ref):
+    q_width = n_heads * HEAD_DIM
+    for src, dst in ((out_ref, o_ref), (gt_ref, g_ref)):
+        for i in range(src.shape[0]):
+            both = src[i]
+            picked = jnp.where(where[2] == 0, both[:, :q_width], both[:, q_width:])
+            dst[i] = picked.astype(f32).T
+
+
+def finish(where, got_out, got_gt, n_heads):
+    n_t, n_img, seq, col = got_out.shape
+    q_width = n_heads * HEAD_DIM
+    slots = n_t * n_img
+    src = pl.BlockSpec((n_img, seq, col), lambda i, s: (i, 0, 0))
+    dst = pl.BlockSpec((n_img, q_width, seq), lambda i, s: (i, 0, 0))
+    outs = pl.pallas_call(
+        functools.partial(finish_body, n_heads),
+        out_shape=[jax.ShapeDtypeStruct((slots, q_width, seq), f32)] * 2,
+        grid_spec=pltpu.PrefetchScalarGridSpec(
+            num_scalar_prefetch=1, grid=(n_t,), in_specs=[src, src], out_specs=[dst, dst]
+        ),
+        name="finish",
+    )(where, got_out.reshape(slots, seq, col), got_gt.reshape(slots, seq, col))
+    return [o.transpose(0, 2, 1) for o in outs]
+
+
+def update_body(sizes, where, *refs):
+    q_width, qb, eb, vb = sizes
+    g_q, g_e, g_r, g_s = refs[:4]
+    state, outs = refs[4:25], refs[25:]
+    dp, t = where[3], where[4]
+    width = g_s.shape[1]
+
+    def columns(rows, at, n):
+        return pltpu.roll(rows, lax.rem(width - at, width), 1)[:, :n]
+
+    exp_row = g_s[pl.ds(t, 1), :]
+    qv_row = g_s[pl.ds(4 + t, 1), :]
+    grads = [
+        None,
+        g_q[:, 3 * q_width :].T,
+        g_e[...],
+        g_r[...],
+        jnp.concatenate(
+            [columns(qv_row, dp * qb, qb), columns(qv_row, 2 * q_width + dp * qb, qb)], axis=0
+        ),
+        columns(exp_row, dp * eb, eb),
+        columns(g_s[8:24, :], dp * vb, vb)[:6],
+    ]
+    for k in range(7):
+        master, first, second = state[3 * k : 3 * k + 3]
+        dst = outs[4 * k : 4 * k + 4]
+        rate, wd = (lr_matrix, decay) if k < 4 else (lr_vector, 0.0)
+        if k == 0:
+            for j in range(3):
+                g = g_q[:, j * q_width : (j + 1) * q_width]
+                dst[0][j] = g
+                dst[1][j], dst[2][j], dst[3][j] = adamw(master[j], g, first[j], second[j], rate, wd)
+        else:
+            g = grads[k]
+            dst[0][...] = g
+            dst[1][...], dst[2][...], dst[3][...] = adamw(master[...], g, first[...], second[...], rate, wd)
+
+
+def update(where, grads, state, q_width, qb, eb, vb):
+    spec = pl.BlockSpec(memory_space=pltpu.VMEM)
+    shapes = [jax.ShapeDtypeStruct(state[3 * k].shape, f32) for k in range(7) for j in range(4)]
+    return pl.pallas_call(
+        functools.partial(update_body, (q_width, qb, eb, vb)),
+        out_shape=shapes,
+        in_specs=[pl.BlockSpec(memory_space=pltpu.SMEM)] + [spec] * (len(grads) + len(state)),
+        out_specs=[spec] * len(shapes),
+        name="update",
+    )(where, *grads, *state)
 
 
 def adamw(master, grad, first, second, rate, decay_rate):
@@ -861,78 +1006,53 @@
     slots, seq, width = tokens.shape
     n_img = slots // n_t
     rows = -(-seq // 16) * 16
-    own_d = qkv_weight.shape[0]
     q_width = qkv_weight.shape[2]
     n_heads = q_width // HEAD_DIM
-    ff = expand_weight.shape[1]
     qb, eb, vb = qv_bias.shape[1], expand_bias.shape[0], vectors.shape[1]
-    wide = -(-3 * q_width // 128) * 128
-    pad = wide - 3 * q_width
-
-    shard_q = jnp.concatenate(
-        [qkv_weight.reshape(own_d, 3 * q_width), proj_weight.T], axis=1
-    ).astype(bf16)
-    shard_e = expand_weight.astype(bf16)
-    shard_r = reduce_weight.T.astype(bf16)
-    n_small = 2 * qb + eb + 6 * vb
-    small = jnp.concatenate(
-        [qv_bias.reshape(-1), expand_bias, vectors.reshape(-1), jnp.zeros((width - n_small,), f32)]
+    dp_me, t_me = lax.axis_index("dp"), lax.axis_index("tensor")
+
+    nat = jnp.zeros((NAT_ROWS, width), f32)
+    nat = lax.dynamic_update_slice(nat, expand_bias[None], (t_me, dp_me * eb))
+    nat = lax.dynamic_update_slice(nat, qv_bias[:1], (4 + t_me, dp_me * qb))
+    nat = lax.dynamic_update_slice(nat, qv_bias[1:], (4 + t_me, 2 * q_width + dp_me * qb))
+    nat = lax.dynamic_update_slice(nat, jnp.where(t_me == 0, vectors, 0.0), (NAT_VEC, dp_me * vb))
+    flip = lambda a: a.transpose(1, 0, 2)
+    g_q, g_e, g_r, nat, a1, n1, qkv, mixp, lse = fore(
+        flip(qkv_weight),
+        proj_weight,
+        expand_weight,
+        reduce_weight.T,
+        nat.astype(bf16),
+        tokens,
+        n_dp,
+        n_img,
+        rows,
+        n_heads,
     )
-    shard_s = jnp.zeros((SMALL_ROWS, width), bf16).at[0].set(small.astype(bf16))
-    g_s, g_q, g_e, g_r = gather_all([shard_s, shard_q, shard_e, shard_r], n_dp)
-    w_q = g_q.reshape(n_t, width, width)
-    w_e = g_e.reshape(n_t, width, ff)
-    w_r = g_r.reshape(n_t, width, ff)
-    got_s = g_s.reshape(n_t, n_dp, SMALL_ROWS, width)[:, :, 0].astype(f32)
-    b_qv = got_s[:, :, : 2 * qb].reshape(n_t, n_dp, 2, qb).transpose(0, 2, 1, 3).reshape(n_t, 2, q_width)
-    b_exp = got_s[:, :, 2 * qb : 2 * qb + eb].reshape(n_t, 1, ff)
-    vec = got_s[0, :, 2 * qb + eb : n_small].reshape(n_dp, 6, vb).transpose(1, 0, 2).reshape(6, width)
-    vec = jnp.pad(vec, ((0, 2), (0, 0)))
-    bias = jnp.concatenate(
-        [b_qv[:, 0], jnp.zeros((n_t, q_width), f32), b_qv[:, 1], jnp.zeros((n_t, pad), f32)], axis=1
-    )
-    bias = jnp.pad(bias[:, None], ((0, 0), (0, 7), (0, 0)))
-    b_exp = jnp.pad(b_exp, ((0, 0), (0, 7), (0, 0)))
-
-    start = lax.axis_index("tensor") * n_img
-    where = jnp.stack([start, counts[0]]).astype(jnp.int32)
-    a1, n1, qkv, mixp, lse = front(where, tokens, vec, bias, w_q, n_img, rows, n_heads)
+    w_q, w_e, w_r = (g.reshape(n_t, width, width) for g in (g_q, g_e, g_r))
+    start = t_me * n_img
+    where = jnp.stack([start, counts[0], t_me % 2, dp_me, t_me]).astype(jnp.int32)
     a2, hd, gh, dres, drh, dmix, out2, dvec, dbexp = middle(
-        where, tokens, cotangent, mixp, vec, b_exp, w_q, w_e, w_r, n_img, rows
+        where, tokens, cotangent, mixp, nat, w_q, w_e, w_r, n_img, rows
     )
     g_r, g_e, g_q, g_s, got_out, got_gt = rear(
-        hd, mixp, qkv, lse, dmix, dres, n1, vec, w_q, dvec, dbexp, gh, a2, a1, drh, out2, n_dp, n_img, n_heads
+        hd, mixp, qkv, lse, dmix, dres, n1, nat, w_q, dvec, dbexp, gh, a2, a1, drh, out2, n_dp, n_img, n_heads
     )
-    t_me, dp_me = lax.axis_index("tensor"), lax.axis_index("dp")
-
-    def own_columns(both):
-        picked = jnp.where(t_me % 2 == 0, both[..., :q_width], both[..., q_width:])
-        return picked.astype(f32).reshape(slots, seq, q_width)
-
-    output = own_columns(got_out)
-    grad_tokens = own_columns(got_gt)
-
-    g_qkv = jnp.stack([g_q[:, j * q_width : (j + 1) * q_width] for j in range(3)], axis=1)
-    g_proj = g_q[:, 3 * q_width :].T
-    g_expand = g_e
-    g_reduce = g_r.T
-    take = lambda row, at, n: lax.dynamic_slice(g_s, (row, at), (1, n))[0]
-    g_expb = take(t_me, dp_me * eb, eb)
-    g_qvb = jnp.stack([take(4 + t_me, dp_me * qb, qb), take(4 + t_me, 2 * q_width + dp_me * qb, qb)])
-    g_vec = lax.dynamic_slice(g_s, (8, dp_me * vb), (6, vb))
-
+    output, grad_tokens = finish(where, got_out, got_gt, n_heads)
+    row = lambda a: a[None]
+    state = [flip(a) for a in (qkv_weight, first_qkv_weight, second_qkv_weight)]
+    state += [proj_weight, first_proj_weight, second_proj_weight]
+    state += [expand_weight, first_expand_weight, second_expand_weight]
+    state += [a.T for a in (reduce_weight, first_reduce_weight, second_reduce_weight)]
+    state += [qv_bias, first_qv_bias, second_qv_bias]
+    state += [row(a) for a in (expand_bias, first_expand_bias, second_expand_bias)]
+    state += [vectors, first_vectors, second_vectors]
+    new = update(where, [g_q, g_e, g_r, g_s], state, q_width, qb, eb, vb)
+    restore = [flip, None, None, lambda a: a.T, None, lambda a: a[0], None]
     results = [output, grad_tokens]
-    for master, grad, first, second, rate, wd in (
-        (qkv_weight, g_qkv, first_qkv_weight, second_qkv_weight, lr_matrix, decay),
-        (proj_weight, g_proj, first_proj_weight, second_proj_weight, lr_matrix, decay),
-        (expand_weight, g_expand, first_expand_weight, second_expand_weight, lr_matrix, decay),
-        (reduce_weight, g_reduce, first_reduce_weight, second_reduce_weight, lr_matrix, decay),
-        (qv_bias, g_qvb, first_qv_bias, second_qv_bias, lr_vector, 0.0),
-        (expand_bias, g_expb, first_expand_bias, second_expand_bias, lr_vector, 0.0),
-        (vectors, g_vec, first_vectors, second_vectors, lr_vector, 0.0),
-    ):
-        results.append(grad)
-        results.extend(adamw(master, grad, first, second, rate, wd))
+    for k in range(28):
+        back_to = restore[k // 4]
+        results.append(new[k] if back_to is None else back_to(new[k]))
     return tuple(results)
 
 

time: 346 us -> 280 us (0.81)
  other arithmetic: 25.4 us -> 0.69 us
  local copies, waits for them, and re-layouts: 23.9 us -> 3.5 us
  Pallas kernels: 291 us -> 272 us
    pallas_call x1, Pallas kernels: 142 us -> 124 us  [rear(): pl.pallas_call(functools.partial(rear_body, cfg), out_shape=[jax.ShapeDty...]
    unnamed x49 -> x2, local copies, waits for them, and re-layouts: 17 us -> 0.61 us
    sub x7 -> x0, other arithmetic: 8.24 us -> none  [adamw(): master - rate * (first_hat / (jnp.sqrt(second_hat) + adam_eps) + decay_ra...]
    reshape x2 -> x0, other arithmetic: 4.75 us -> none  [own_columns(): return picked.astype(f32).reshape(slots, seq, q_width)]
    select_n x1, other arithmetic: 4.64 us -> 0.69 us  [on_device(): jnp.where(t_me == 0, vectors, 0.0)]
    pallas_call x2 -> x3, Pallas kernels: 109 us -> 108 us  [the longest x1 94.8 us: fore(): pl.pallas_call(functools.partial(fore_body, cfg), out_shape=[jax.ShapeDty...]
where the time goes in v3:
time: 280 us; the launch traced here: 278 us
  Pallas kernels  272 us (97%)
  local copies, waits for them, and re-layouts  3.5 us (1%)
    pallas_call x1, Pallas kernels, rear(): pl.pallas_call(functools.partial(rear_body, cfg), out_shape=[jax.ShapeDty...  124 us
    pallas_call x1, Pallas kernels, fore(): pl.pallas_call(functools.partial(fore_body, cfg), out_shape=[jax.ShapeDty...  94.8 us
    pallas_call x1, Pallas kernels, middle(): pl.pallas_call(functools.partial(middle_body, seq), out_shape=[jax.ShapeD...  40.4 us
    pallas_call x1, Pallas kernels, finish(): pl.pallas_call(functools.partial(finish_body, n_heads), out_shape=[jax.Sh...  8.96 us

profile of v3, /device:TPU:0, one launch (start us, length us, event | category | flops | bytes accessed | tf_op | source)
XLA Modules:
  0.0 277.9 jit_solution(14867089722393887595)
XLA Ops:
  1.3 0.7 stack.19.where
  2.0 0.8 fusion
  2.8 0.7 broadcast_select_fusion
  3.5 0.8 dynamic_update_slice.12
  4.2 0.2 dynamic_update_slice.13
  4.4 0.2 dynamic_update_slice.14
  4.6 0.3 dynamic_update_slice.15.refs_4_
  4.9 0.0 copy-start
  5.0 0.6 copy-done
  5.6 94.8 %fore.1 = (bf16[2,2,4,2,96,768]{5,4,3,2,1,0:T(8,128)(2,1)}, bf16[2,2,4,2,96,768]{5,4,3,2,1,0:T(8,128)(2,1)}, bf16[2,2,4,2,96,768]{5,4,3,2,1,0:T(8,128)(2,1)}, f3...) custom-call(f32[3,96,192]{2,1,0:T(8,128)} %bitcast.38, ...), custom_call_target="tpu_custom_call" | custom-call | tf_op jit(solution)/shard_map/fore/pallas_call | solution.py:285
  100.3 40.4 %middle.1 = (bf16[1040,768]{1,0:T(8,128)(2,1)}, bf16[1040,6144]{1,0:T(8,128)(2,1)}, bf16[1040,768]{1,0:T(8,128)(2,1)}, f32[1040,768]{1,0:T(8,128)}, bf16[1040,76...) custom-call(s32[5]{0:T(128)} %stack.19.where, ...), custom_call_target="tpu_custom_call" | custom-call | tf_op jit(solution)/shard_map/middle/pallas_call | solution.py:409
  140.7 123.7 %rear.1 = (f32[96,768]{1,0:T(8,128)}, f32[96,768]{1,0:T(8,128)}, f32[96,768]{1,0:T(8,128)}, f32[24,768]{1,0:T(8,128)}, bf16[4,5,197,384]{3,2,1,0:T(8,128)(2,1)}, /*index=5*/bf16[4,5,197,384]{3,2,1,0:T(8,128)(2,1)}) custom-call(bf16[1040,6144]{1,0:T(8,128)(2,1)} %get-tuple-element.89.refs_0_, bf16[1040,1024]{1,0:T(8,128)(2,1)} %get-tuple-element.84.mix_ref.refs_1_, ...), custom_call_target="tpu_custom_call" | custom-call | tf_op jit(solution)/shard_map/rear/pallas_call | solution.py:864
  264.4 9.0 %finish.1 = (f32[20,192,197]{2,1,0:T(8,128)}, f32[20,192,197]{2,1,0:T(8,128)}) custom-call(s32[5]{0:T(128)} %stack.19.where, bf16[20,197,384]{2,1,0:T(8,128)(2,1)} %bitcast.36, bf16[20,197,384]{2,1,0:T(8,128)(2,1)} %bitcast.37), custom_call_target="tpu_custom_call" | custom-call | tf_op jit(solution)/shard_map/finish/pallas_call | solution.py:908
  273.4 4.4 %update.1 = (f32[3,96,192]{2,1,0:T(8,128)}, f32[3,96,192]{2,1,0:T(8,128)}, f32[3,96,192]{2,1,0:T(8,128)}, f32[3,96,192]{2,1,0:T(8,128)}, f32[192,96]{1,0:T(8,128...) custom-call(s32[5]{0:T(128)} %stack.19.where, ...), custom_call_target="tpu_custom_call" | custom-call | tf_op jit(solution)/shard_map/update/pallas_call | solution.py:960
  (1 shorter events, 0.0 us)
Async XLA Ops:
  4.9 0.6 copy-start

commit v4 on v3

--- a/solution.py
+++ b/solution.py
@@ -101,7 +101,7 @@
 
 
 S_ROWS = 24
-NAT_ROWS = 32
+NAT_ROWS = 16
 NAT_VEC = 8
 
 
@@ -162,31 +162,34 @@
         for k in range(n_z - 1):
             to_z(p, k).start()
 
+    def stage_a(p):
+        own(p).wait()
+        for k in range(n_z - 1):
+            to_z(p, k).wait_recv()
+        for slot in (0, 1, 3):
+            move(p, slot).start()
+        if p + ahead < n_p:
+            send_z(p + ahead)
+
+    def stage_b(p):
+        move(p, 0).wait_recv()
+        move(p, 2).start()
+        move(p, 4).start()
+
+    def stage_c(p):
+        move(p, 1).wait_recv()
+        move(p, 5).start()
+        move(p, 2).wait_recv()
+        move(p, 6).start()
+
+    def stage_d(p):
+        for slot in (3, 4, 5, 6):
+            move(p, slot).wait_recv()
+
     def advance(step):
-        p = step
-        if 0 <= p < n_p:
-            own(p).wait()
-            for k in range(n_z - 1):
-                to_z(p, k).wait_recv()
-            for slot in (0, 1, 3):
-                move(p, slot).start()
-            if p + ahead < n_p:
-                send_z(p + ahead)
-        p = step - 1
-        if 0 <= p < n_p:
-            move(p, 0).wait_recv()
-            move(p, 2).start()
-            move(p, 4).start()
-        p = step - 2
-        if 0 <= p < n_p:
-            move(p, 1).wait_recv()
-            move(p, 5).start()
-            move(p, 2).wait_recv()
-            move(p, 6).start()
-        p = step - 3
-        if 0 <= p < n_p:
-            for slot in (3, 4, 5, 6):
-                move(p, slot).wait_recv()
+        for stage, p in ((stage_c, step - 2), (stage_b, step - 1), (stage_a, step), (stage_d, step - 3)):
+            if 0 <= p < n_p:
+                stage(p)
 
     def image(i):
         return pltpu.make_async_copy(tokens.at[t_me * n_img + i], xall.at[i], x_sem.at[i])

time: 280 us -> 275 us (0.982)
  Pallas kernels: 272 us -> 268 us
    pallas_call x1, Pallas kernels: 94.8 us -> 90.1 us  [fore(): pl.pallas_call(functools.partial(fore_body, cfg), out_shape=[jax.ShapeDty...]
where the time goes in v4:
time: 275 us; the launch traced here: 274 us
  Pallas kernels  268 us (97%)
  local copies, waits for them, and re-layouts  3.4 us (1%)
    pallas_call x1, Pallas kernels, rear(): pl.pallas_call(functools.partial(rear_body, cfg), out_shape=[jax.ShapeDty...  124 us
    pallas_call x1, Pallas kernels, fore(): pl.pallas_call(functools.partial(fore_body, cfg), out_shape=[jax.ShapeDty...  90.1 us
    pallas_call x1, Pallas kernels, middle(): pl.pallas_call(functools.partial(middle_body, seq), out_shape=[jax.ShapeD...  40.2 us
    pallas_call x1, Pallas kernels, finish(): pl.pallas_call(functools.partial(finish_body, n_heads), out_shape=[jax.Sh...  8.96 us

profile of v4, /device:TPU:0, one launch (start us, length us, event | category | flops | bytes accessed | tf_op | source)
XLA Modules:
  0.0 273.6 jit_solution(6161124805186422174)
XLA Ops:
  1.3 0.6 stack.19.where
  1.9 0.8 fusion
  2.7 0.7 broadcast_select_fusion
  3.4 0.8 dynamic_update_slice.12
  4.2 0.2 dynamic_update_slice.13
  4.4 0.2 dynamic_update_slice.14
  4.5 0.3 dynamic_update_slice.15.refs_4_
  4.8 0.0 copy-start
  4.9 0.6 copy-done
  5.5 90.1 %fore.1 = (bf16[2,2,4,2,96,768]{5,4,3,2,1,0:T(8,128)(2,1)}, bf16[2,2,4,2,96,768]{5,4,3,2,1,0:T(8,128)(2,1)}, bf16[2,2,4,2,96,768]{5,4,3,2,1,0:T(8,128)(2,1)}, f3...) custom-call(f32[3,96,192]{2,1,0:T(8,128)} %bitcast.38, ...), custom_call_target="tpu_custom_call" | custom-call | tf_op jit(solution)/shard_map/fore/pallas_call | solution.py:288
  95.6 40.2 %middle.1 = (bf16[1040,768]{1,0:T(8,128)(2,1)}, bf16[1040,6144]{1,0:T(8,128)(2,1)}, bf16[1040,768]{1,0:T(8,128)(2,1)}, f32[1040,768]{1,0:T(8,128)}, bf16[1040,76...) custom-call(s32[5]{0:T(128)} %stack.19.where, ...), custom_call_target="tpu_custom_call" | custom-call | tf_op jit(solution)/shard_map/middle/pallas_call | solution.py:412
  135.8 124.3 %rear.1 = (f32[96,768]{1,0:T(8,128)}, f32[96,768]{1,0:T(8,128)}, f32[96,768]{1,0:T(8,128)}, f32[24,768]{1,0:T(8,128)}, bf16[4,5,197,384]{3,2,1,0:T(8,128)(2,1)}, /*index=5*/bf16[4,5,197,384]{3,2,1,0:T(8,128)(2,1)}) custom-call(bf16[1040,6144]{1,0:T(8,128)(2,1)} %get-tuple-element.89.refs_0_, bf16[1040,1024]{1,0:T(8,128)(2,1)} %get-tuple-element.84.mix_ref.refs_1_, ...), custom_call_target="tpu_custom_call" | custom-call | tf_op jit(solution)/shard_map/rear/pallas_call | solution.py:867
  260.1 9.0 %finish.1 = (f32[20,192,197]{2,1,0:T(8,128)}, f32[20,192,197]{2,1,0:T(8,128)}) custom-call(s32[5]{0:T(128)} %stack.19.where, bf16[20,197,384]{2,1,0:T(8,128)(2,1)} %bitcast.36, bf16[20,197,384]{2,1,0:T(8,128)(2,1)} %bitcast.37), custom_call_target="tpu_custom_call" | custom-call | tf_op jit(solution)/shard_map/finish/pallas_call | solution.py:911
  269.1 4.4 %update.1 = (f32[3,96,192]{2,1,0:T(8,128)}, f32[3,96,192]{2,1,0:T(8,128)}, f32[3,96,192]{2,1,0:T(8,128)}, f32[3,96,192]{2,1,0:T(8,128)}, f32[192,96]{1,0:T(8,128...) custom-call(s32[5]{0:T(128)} %stack.19.where, ...), custom_call_target="tpu_custom_call" | custom-call | tf_op jit(solution)/shard_map/update/pallas_call | solution.py:963
  (1 shorter events, 0.0 us)
Async XLA Ops:
  4.8 0.6 copy-start
